TPU v7x, 256 devices: a 4x2x16 block of a 4x16x16 slice. The times are simulated.
256 devices in a mesh: member: 2 (over y), lat: 128 (over z, x, core).
Axes of the slice: x: 4, y: 2, z: 16, core: 2. Of those that a mesh axis runs over, the one named last changes fastest.
The devices are a block of a 4x16x16 slice.
Arguments:
- increment: float32 [274, 2048, 128], P('member', 'lat'), parts along dimension 0, may hold values from -6 to 6
- filter_taps: int32 [4, 2, 2, 5], replicated, may hold values from 1 to 8
- band_roots: float32 [5, 137, 137], replicated, may hold values from -1 to 1
Outputs:
- adjoint: float32 [274, 2048, 128], P('member', 'lat'), parts along dimension 0
There are 2 independent parts, one for each index of `member`. A program takes and returns all parts, laid end to end along the dimension named above; an argument that names none is the same for every part. Nothing has to cross between parts.
All inputs are finite; a program needn't handle non-finite values.
Results may differ from a plain program's by a relative error of at most 0.0001.
Values sent between devices are 32-bit elements; how exact they have to be, the bound alone decides.
No kernel may reach another device: no remote copies, remote signals or barrier semaphores. Data moves between devices by JAX's collectives and lax.ppermute only.
A program may use at most 64 MiB of HBM per device.

v0:
```python
import functools
import math

import jax
import jax.numpy as jnp
from jax import lax
from jax.experimental import pallas as pl
from jax.experimental.pallas import tpu as pltpu
from jax.sharding import PartitionSpec as P

LEVELS = 4
TAPS = 5
ROOT_TWO = math.sqrt(2.0)
F32 = jnp.float32
BF16 = jnp.bfloat16
MIB = 1024 * 1024

ROWS = 16
OWN = (8, 4, 2, 1)
FIRST = -1
LAST = (8, 5, 3, 2)
COUNT = (10, 7, 5, 4)
BASE = (0, 10, 17, 22)
SLOTS = 26
LANES = 128
PAD = 144
KPAD = 256


def dot(a, b):
    return lax.dot_general(a, b, (((1,), (0,)), ((), ())), preferred_element_type=F32)


def dot_t(a, b):
    return lax.dot_general(a, b, (((1,), (1,)), ((), ())), preferred_element_type=F32)


def split(values):
    high = values.astype(BF16)
    return high, (values - high.astype(F32)).astype(BF16)


def slot(level, index):
    return BASE[level] + index - FIRST


def lane_ids(rows):
    return lax.broadcasted_iota(jnp.int32, (rows, LANES), 1)


def write_filters(taps_ref, filt_ref):
    signs = (1.0, -1.0, 1.0, -1.0, 1.0)
    ones = jnp.full((1, LANES), 1.0, F32)
    for level in range(LEVELS):
        for way in range(2):
            low = [taps_ref[level, way, 0, k].astype(F32) * ones for k in range(TAPS)]
            high = [taps_ref[level, way, 1, k].astype(F32) * ones for k in range(TAPS)]
            low_scale = ROOT_TWO / functools.reduce(jnp.add, low)
            high_scale = 1.0 / jnp.sqrt(functools.reduce(jnp.add, [h * h for h in high]))
            row = (level * 2 + way) * 2 * TAPS
            for k in range(TAPS):
                filt_ref[row + k : row + k + 1, :] = low[k] * low_scale
                filt_ref[row + TAPS + k : row + TAPS + k + 1, :] = (signs[k] * high[k]) * high_scale


def coeffs(filt_ref, level, way, kind):
    row = ((level * 2 + way) * 2 + kind) * TAPS
    return [filt_ref[row + k : row + k + 1, :] for k in range(TAPS)]


def write_weights(filt_ref, w0_ref, w_ref, ww_ref):
    row = lax.broadcasted_iota(jnp.int32, (LANES, LANES), 0)
    lane = lax.broadcasted_iota(jnp.int32, (LANES, LANES), 1)
    composed = None
    for level in range(LEVELS):
        half = (LANES // 2) >> level
        low = coeffs(filt_ref, level, 1, 0)
        high = coeffs(filt_ref, level, 1, 1)
        is_low = lane < half
        tap = row - 2 * jnp.where(is_low, lane, lane - half) + 2
        inside = (lane < 2 * half) & (row < 2 * half)
        step = jnp.zeros((LANES, LANES), F32)
        for k in range(TAPS):
            chosen = jnp.where(is_low, low[k], high[k])
            step = jnp.where(inside & (tap == k), chosen, step)
        if composed is None:
            composed = step
        else:
            composed = lax.dot_general(
                composed, step, (((1,), (0,)), ((), ())),
                precision=lax.Precision.HIGHEST, preferred_element_type=F32,
            )
        zeros = jnp.zeros((LANES, LANES), BF16)
        if level == 0:
            d_high, d_low = split(composed)
            moved = jnp.where(lane < half, pltpu.roll(composed, LANES - half, 1), 0.0)
            a_high, a_low = split(moved)
            w0_ref[0:LANES, 0:128] = zeros
            w0_ref[0:LANES, 128:256] = a_high
            w0_ref[0:LANES, 256:384] = zeros
            w0_ref[0:LANES, 384:512] = a_low
            w0_ref[LANES:256, 0:128] = d_high
            w0_ref[LANES:256, 128:256] = zeros
            w0_ref[LANES:256, 256:384] = d_low
            w0_ref[LANES:256, 384:512] = zeros
        else:
            moved = jnp.where((lane >= 2 * half) & (lane < 3 * half), pltpu.roll(composed, half, 1), 0.0)
            if level == LEVELS - 1:
                moved = moved + jnp.where(
                    (lane >= 3 * half) & (lane < 4 * half), pltpu.roll(composed, 3 * half, 1), 0.0
                )
            for part, values in ((0, moved), (1, composed)):
                rows = slice(part * LANES, part * LANES + LANES)
                v_high, v_low = split(values)
                w_ref[level - 1, rows, 0:128] = v_high
                w_ref[level - 1, rows, 128:256] = v_low
                ww_ref[level - 1, rows, 0:128] = v_high
                ww_ref[level - 1, rows, 128:256] = v_high


def edge_flags():
    place = lax.axis_index("lat")
    count = lax.axis_size("lat")
    lower = jnp.where(place == 0, 0.0, 1.0).astype(F32)
    upper = jnp.where(place == count - 1, 0.0, 1.0).astype(F32)
    return lower, upper


def masked(values, index, own, flags):
    if index < 0:
        return values * flags[0]
    if index >= own:
        return values * flags[1]
    return values


def latitude_analysis(rows, filt_ref, flags):
    out = {}
    for level in range(LEVELS):
        low = coeffs(filt_ref, level, 0, 0)
        high = coeffs(filt_ref, level, 0, 1)
        smooth = {}
        for index in range(FIRST, LAST[level] + 1):
            a = d = None
            for k in range(TAPS):
                source = rows.get(2 * index - 2 + k)
                if source is None:
                    continue
                a = low[k] * source if a is None else a + low[k] * source
                d = high[k] * source if d is None else d + high[k] * source
            if level < LEVELS - 1:
                a = masked(a, index, OWN[level], flags)
            smooth[index] = a
            out[slot(level, index)] = (a, d)
        rows = smooth
    return out


def latitude_synthesis(pick, filt_ref, flags):
    rows = None
    for level in reversed(range(LEVELS)):
        low = coeffs(filt_ref, level, 0, 0)
        high = coeffs(filt_ref, level, 0, 1)
        first, last = (FIRST, LAST[level - 1]) if level else (0, ROWS - 1)
        smooth, sharp = {}, {}
        for index in range(FIRST, LAST[level] + 1):
            a, d = pick(slot(level, index))
            smooth[index] = a if rows is None else a + rows[index]
            sharp[index] = d
        out = {}
        for r in range(first, last + 1):
            total = None
            for index in range(FIRST, LAST[level] + 1):
                k = r - 2 * index + 2
                if 0 <= k < TAPS:
                    term = low[k] * smooth[index] + high[k] * sharp[index]
                    total = term if total is None else total + term
            out[r] = masked(total, r, OWN[level - 1], flags) if level else total
        rows = out
    return rows


def pack(c0, c1, c2, c3, c1b=None, c2b=None):
    lane = lane_ids(PAD)
    extra = jnp.zeros((PAD, LANES), F32) if c2b is None else pltpu.roll(c2b, 80, 1)
    tiles = [
        c0[:, 0:128],
        jnp.where(lane < 64, c0[:, 128:256], jnp.where(lane < 112, pltpu.roll(c2, 64, 1), extra)),
        jnp.where(lane < 96, c1, pltpu.roll(c3, 96, 1)),
    ]
    if c1b is not None:
        tiles.append(jnp.where(lane < 96, c1b, pltpu.roll(c2b, 96, 1)))
    return tiles


def unpack(ref):
    tile1 = ref[:, 128:256]
    tile2 = ref[:, 256:384]
    parts = [ref[:, 0:256], tile2, pltpu.roll(tile1, 64, 1), pltpu.roll(tile2, 32, 1)]
    if ref.shape[1] > 384:
        tile3 = ref[:, 384:512]
        lane = lane_ids(PAD)
        parts += [tile3, jnp.where(lane < 32, pltpu.roll(tile3, 32, 1), pltpu.roll(tile1, 48, 1))]
    return parts


def pack_coarse(c3):
    lane = lane_ids(40)
    last = jnp.concatenate([c3[120:144], jnp.zeros((16, LANES), F32)], axis=0)
    return jnp.where(
        lane < 32,
        c3[0:40],
        jnp.where(
            lane < 64,
            pltpu.roll(c3[40:80], 32, 1),
            jnp.where(lane < 96, pltpu.roll(c3[80:120], 64, 1), pltpu.roll(last, 96, 1)),
        ),
    )


def unpack_coarse(ref):
    values = ref[...]
    parts = [values] + [pltpu.roll(values, LANES - 32 * q, 1) for q in (1, 2, 3)]
    return jnp.concatenate(parts[:3] + [parts[3][0:24]], axis=0)


def store_split(hi_ref, lo_ref, out, at):
    for place, (a, d) in out.items():
        for part, values in ((0, a), (1, d)):
            lanes = slice(part * LANES, part * LANES + LANES)
            high, low = split(values)
            hi_ref[place, at, lanes] = high
            lo_ref[place, at, lanes] = low


def longitude_analysis(hi_ref, lo_ref, w0_ref, w_ref, c0_ref, c1_ref, c2_ref, c3_ref, up_ref, down_ref, far_ref):
    def level0(index):
        s = slot(0, index)
        w_high, w_low = w0_ref[:, 0:256], w0_ref[:, 256:512]
        high = hi_ref[s]
        return dot(high, w_high) + dot(high, w_low) + dot(lo_ref[s], w_high)

    def others(level, index):
        s = slot(level, index)
        both = dot(hi_ref[s], w_ref[level - 1])
        return both[:, 0:128] + both[:, 128:256] + dot(lo_ref[s], w_ref[level - 1, :, 0:128])

    c3 = {i: others(3, i) for i in range(-1, 3)}
    far_ref[...] = pack_coarse(c3[2])
    up = pack(level0(8), others(1, 4), others(2, 2), c3[1], others(1, 5), others(2, 3))
    for t, tile in enumerate(up):
        up_ref[:, t * LANES : t * LANES + LANES] = tile
    down = pack(level0(-1), others(1, -1), others(2, -1), c3[-1])
    for t, tile in enumerate(down):
        down_ref[:, t * LANES : t * LANES + LANES] = tile
    c3_ref[...] = c3[0]
    for i in range(8):
        c0_ref[i] = level0(i)
    for i in range(4):
        c1_ref[i // 2, :, (i % 2) * 128 : (i % 2) * 128 + 128] = others(1, i)
    for i in range(2):
        c2_ref[:, i * 128 : i * 128 + 128] = others(2, i)


def longitude_synthesis(
    y0_ref, y1_ref, y2_ref, y3_ref, below_ref, above_ref, far_ref, w0_ref, w_ref, ww_ref, u_ref
):
    below = unpack(below_ref)
    above = unpack(above_ref)
    far = unpack_coarse(far_ref)
    c0 = {-1: below[0], 8: above[0]}
    c1 = {-1: below[1], 4: above[1], 5: above[4]}
    c2 = {-1: below[2], 2: above[2], 3: above[5]}
    c3 = {-1: below[3], 1: above[3], 2: far, 0: y3_ref[...]}
    for i in range(8):
        c0[i] = y0_ref[i]
    for i in range(4):
        c1[i] = y1_ref[i // 2, :, (i % 2) * 128 : (i % 2) * 128 + 128]
    for i in range(2):
        c2[i] = y2_ref[:, i * 128 : i * 128 + 128]
    for i, values in c0.items():
        high, low = split(values)
        w_high, w_low = w0_ref[:, 0:256], w0_ref[:, 256:512]
        u_ref[slot(0, i)] = dot_t(high, w_high) + dot_t(low, w_high) + dot_t(high, w_low)
    for level, group in ((1, c1), (2, c2), (3, c3)):
        for i, values in group.items():
            high, low = split(values)
            pair = jnp.concatenate([high, low], axis=1)
            u_ref[slot(level, i)] = dot_t(pair, ww_ref[level - 1]) + dot_t(high, w_ref[level - 1, :, 128:256])


def pick_at(u_ref, at):
    def pick(place):
        return u_ref[place, at, 0:128], u_ref[place, at, 128:256]

    return pick


def first_kernel(taps_ref, x_ref, *rest):
    filt_ref, w0_ref, w_ref, ww_ref, *outs = rest[:-2]
    hi_ref, lo_ref = rest[-2:]
    write_filters(taps_ref, filt_ref)
    flags = edge_flags()
    write_weights(filt_ref, w0_ref, w_ref, ww_ref)

    def chunk(c, carry):
        start = pl.multiple_of(c * (16 * ROWS), 16 * ROWS)
        rows = {r: x_ref[pl.ds(start + r, 16, stride=ROWS), :] for r in range(ROWS)}
        at = pl.ds(pl.multiple_of(c * 16, 16), 16)
        store_split(hi_ref, lo_ref, latitude_analysis(rows, filt_ref, flags), at)
        return carry

    lax.fori_loop(0, 8, chunk, 0)
    top = lax.broadcasted_iota(jnp.int32, (8, LANES), 0) == 0
    rows = {}
    for r in range(ROWS):
        head = x_ref[pl.ds(128 * ROWS + r, 8, stride=ROWS), :]
        tail = jnp.where(top, x_ref[136 * ROWS + r : 136 * ROWS + r + 1, :], 0.0)
        rows[r] = jnp.concatenate([head, tail], axis=0)
    store_split(hi_ref, lo_ref, latitude_analysis(rows, filt_ref, flags), slice(128, 144))
    longitude_analysis(hi_ref, lo_ref, w0_ref, w_ref, *outs)


def vertical_kernel(m_ref, c0_ref, c1_ref, c2_ref, c3_ref, below_ref, above_ref, far_ref, y0_ref, y1_ref, y2_ref, y3_ref,
                    up_ref, down_ref, far_out_ref):
    below = unpack(below_ref)
    above = unpack(above_ref)
    far = unpack_coarse(far_ref)

    def apply(band, values):
        high, low = split(values)
        zeros = jnp.zeros((KPAD - PAD, values.shape[1]), BF16)
        high = jnp.concatenate([high, zeros], axis=0)
        low = jnp.concatenate([low, zeros], axis=0)
        both = dot(m_ref[band], high)
        return both[0:PAD] + both[PAD:] + dot(m_ref[band, 0:PAD], low)

    c3 = c3_ref[...] + below[3] + above[3] + far
    lane = lane_ids(PAD)
    y3 = jnp.where(lane < 24, apply(3, c3), apply(4, c3))
    y3_ref[...] = y3
    far_out_ref[...] = pack_coarse(y3)
    c2 = c2_ref[...]
    y2 = apply(2, jnp.concatenate([c2[:, 0:128] + below[2], c2[:, 128:256] + below[5] + above[2]], axis=1))
    y2_ref[...] = y2
    c1 = c1_ref[0]
    y1_low = apply(1, jnp.concatenate([c1[:, 0:128] + below[1], c1[:, 128:256] + below[4]], axis=1))
    c1 = c1_ref[1]
    y1_high = apply(1, jnp.concatenate([c1[:, 0:128], c1[:, 128:256] + above[1]], axis=1))
    y1_ref[0] = y1_low
    y1_ref[1] = y1_high
    first = apply(0, c0_ref[0] + below[0])
    last = apply(0, c0_ref[7] + above[0])
    y0_ref[0] = first
    y0_ref[7] = last
    down = pack(first, y1_low[:, 0:128], y2[:, 0:128], y3, y1_low[:, 128:256], y2[:, 128:256])
    for t, tile in enumerate(down):
        down_ref[:, t * LANES : t * LANES + LANES] = tile
    up = pack(last, y1_high[:, 128:256], y2[:, 128:256], y3)
    for t, tile in enumerate(up):
        up_ref[:, t * LANES : t * LANES + LANES] = tile
    for i in range(1, 7):
        y0_ref[i] = apply(0, c0_ref[i])


def middle_kernel(filt_ref, w0_ref, w_ref, ww_ref, y0_ref, y1_ref, y2_ref, y3_ref, below_ref, above_ref, far_ref, *rest):
    *outs, u_ref, hi_ref, lo_ref = rest
    flags = edge_flags()
    longitude_synthesis(y0_ref, y1_ref, y2_ref, y3_ref, below_ref, above_ref, far_ref, w0_ref, w_ref, ww_ref, u_ref)

    def chunk(c, carry):
        at = pl.ds(pl.multiple_of(c * 16, 16), 16)
        rows = latitude_synthesis(pick_at(u_ref, at), filt_ref, flags)
        store_split(hi_ref, lo_ref, latitude_analysis(rows, filt_ref, flags), at)
        return carry

    lax.fori_loop(0, 9, chunk, 0)
    longitude_analysis(hi_ref, lo_ref, w0_ref, w_ref, *outs)


def last_kernel(filt_ref, w0_ref, w_ref, ww_ref, y0_ref, y1_ref, y2_ref, y3_ref, below_ref, above_ref, far_ref, out_ref,
                u_ref):
    flags = edge_flags()
    longitude_synthesis(y0_ref, y1_ref, y2_ref, y3_ref, below_ref, above_ref, far_ref, w0_ref, w_ref, ww_ref, u_ref)

    def chunk(c, carry):
        at = pl.ds(pl.multiple_of(c * 16, 16), 16)
        rows = latitude_synthesis(pick_at(u_ref, at), filt_ref, flags)
        start = pl.multiple_of(c * (16 * ROWS), 16 * ROWS)
        for r, values in rows.items():
            out_ref[pl.ds(start + r, 16, stride=ROWS), :] = values
        return carry

    lax.fori_loop(0, 8, chunk, 0)
    rows = latitude_synthesis(pick_at(u_ref, slice(128, 144)), filt_ref, flags)
    for r, values in rows.items():
        out_ref[pl.ds(128 * ROWS + r, 8, stride=ROWS), :] = values[0:8]
        out_ref[136 * ROWS + r : 136 * ROWS + r + 1, :] = values[8:9]


def prepare_kernel(m_ref, after_ref, plain_ref, turned_ref, wide_ref):
    del after_ref
    levels = m_ref.shape[1]
    wide_ref[...] = jnp.zeros_like(wide_ref)
    for band in range(m_ref.shape[0]):
        wide_ref[0:levels, 0:levels] = m_ref[band]
        values = wide_ref[...]
        for ref, matrix in ((plain_ref, values), (turned_ref, values.T)):
            high, low = split(matrix[0:PAD])
            ref[band, 0:PAD, :] = high
            ref[band, PAD : 2 * PAD, :] = low


VMEM = pl.BlockSpec(memory_space=pltpu.VMEM)
SMEM = pl.BlockSpec(memory_space=pltpu.SMEM)
ANY = pl.BlockSpec(memory_space=pl.ANY)


def shapes(*items):
    return [jax.ShapeDtypeStruct(shape, dtype) for shape, dtype in items]


COEFFICIENTS = (((8, PAD, 256), F32), ((2, PAD, 256), F32), ((PAD, 256), F32), ((PAD, LANES), F32))
WIDE_FIRST = (((PAD, 512), F32), ((PAD, 384), F32), ((40, LANES), F32))
WIDE_SECOND = (((PAD, 384), F32), ((PAD, 512), F32), ((40, LANES), F32))
WEIGHTS = (((80, LANES), F32), ((256, 512), BF16), ((3, 256, 256), BF16), ((3, 256, 256), BF16))


def call(kernel, in_specs, outs, scratch, name, limit, flops):
    return pl.pallas_call(
        kernel,
        out_shape=shapes(*outs),
        in_specs=in_specs,
        out_specs=[VMEM] * len(outs),
        scratch_shapes=scratch,
        compiler_params=pltpu.CompilerParams(vmem_limit_bytes=limit * MIB),
        cost_estimate=pl.CostEstimate(flops=flops, bytes_accessed=8 * MIB, transcendentals=0),
        name=name,
    )


def shift(values, by):
    count = lax.axis_size("lat")
    return lax.ppermute(values, "lat", [(i, i + by) for i in range(count) if 0 <= i + by < count])


def on_device(increment, filter_taps, band_roots):
    levels, rows, columns = increment.shape
    flat = increment.reshape(levels * rows, columns)
    halves = [pltpu.VMEM((SLOTS, PAD, 256), BF16)] * 2
    spread = [pltpu.VMEM((SLOTS, PAD, 256), F32)]
    filt, w0, w, ww, *rest = call(
        first_kernel, [SMEM, VMEM], WEIGHTS + COEFFICIENTS + WIDE_FIRST, halves, "first", 24, 10**9
    )(filter_taps, flat)
    plain, turned = call(
        prepare_kernel, [VMEM, ANY], (((5, 2 * PAD, 256), BF16),) * 2, [pltpu.VMEM((256, 256), F32)], "prepare", 16, 10**9
    )(band_roots, rest[-1])
    weights = [filt, w0, w, ww]

    def exchange_sums(up, down, far):
        return shift(up, 1), shift(down, -1), shift(far, 2)

    def exchange_values(up, down, far):
        return shift(up, 1), shift(down, -1), shift(far, -2)

    def vertical(matrix, own, received):
        return call(
            vertical_kernel, [VMEM] * 8, COEFFICIENTS + WIDE_SECOND, [], "vertical", 24, 10**9
        )(matrix, *own, *received)

    own, wide = rest[:4], rest[4:]
    *own, up, down, far = vertical(plain, own, exchange_sums(*wide))
    *own, up, down, far = call(
        middle_kernel, [VMEM] * 11, COEFFICIENTS + WIDE_FIRST, spread + halves, "middle", 32, 10**9
    )(*weights, *own, *exchange_values(up, down, far))
    *own, up, down, far = vertical(turned, own, exchange_sums(up, down, far))
    (out,) = call(
        last_kernel, [VMEM] * 11, (((levels * rows, columns), F32),), spread, "last", 24, 10**9
    )(*weights, *own, *exchange_values(up, down, far))
    return out.reshape(levels, rows, columns)


def solution(mesh):
    placed = (P("member", "lat", None), P(), P())
    return jax.shard_map(
        on_device, mesh=mesh, in_specs=placed, out_specs=P("member", "lat", None), check_vma=False
    )
```

profile of v0, /device:TPU:431, one launch (start us, length us, event | category | flops | bytes accessed | tf_op | source)
XLA Modules:
  0.0 83.3 jit_solution(16168673682750499423)
XLA Ops:
  0.0 0.0 copy-start
  0.0 1.2 %copy-done = f32[137,16,128]{2,1,0:T(8,128)S(1)} copy-done((f32[137,16,128]{2,1,0:T(8,128)S(1)}, f32[137,16,128]{2,1,0:T(8,128)}, u32[]{:S(2)}) %copy-start) | copy-done | bytes 1122328
  1.3 0.0 copy-start.2
  1.3 0.7 copy-done.2
  1.9 0.0 copy-start.1
  2.0 4.4 %first.1 = (f32[80,128]{1,0:T(8,128)S(1)}, bf16[256,512]{1,0:T(8,128)(2,1)S(1)}, bf16[3,256,256]{2,1,0:T(8,128)(2,1)S(1)}, bf16[3,256,256]{2,1,0:T(8,128)(2,1)S(...) custom-call(s32[4,2,2,5]{3,2,1,0:T(2,128)S(1)} %copy-done.2, ...), custom_call_target="tpu_custom_call" | custom-call | flops 1000000000 | bytes 8388608 | tf_op jit(solution)/shard_map/first/pallas_call | solution.py:452
  6.4 5.6 %collective-permute-start = (f32[144,512]{1,0:T(8,128)S(1)}, f32[144,512]{1,0:T(8,128)S(1)}, u32[]{:S(2)}, u32[]{:S(2)}) collective-permute-start(f32[144,512]{1,0:T(8,128)S(1)} %get-tuple-element.50), channel_id=1, source_target_pairs={{0,1},{1,2},{2,3},{3,4},{4,5},{5,6},{6,7},{7,8},{8,9},{9,10},{10,1... | collective-permute-start | bytes 884744 | tf_op jit(solution)/shard_map/ppermute | solution.py:444
  12.0 2.0 %collective-permute-start.1 = (f32[144,384]{1,0:T(8,128)S(1)}, f32[144,384]{1,0:T(8,128)S(1)}, u32[]{:S(2)}, u32[]{:S(2)}) collective-permute-start(f32[144,384]{1,0:T(8,128)S(1)} %get-tuple-element.51), channel_id=1, source_target_pairs={{1,0},{2,1},{3,2},{4,3},{5,4},{6,5},{7,6},{8,7},{9,8},{10,9},{11,1... | collective-permute-start | bytes 663560 | tf_op jit(solution)/shard_map/ppermute | solution.py:444
  14.0 3.3 %collective-permute-start.2 = (f32[40,128]{1,0:T(8,128)S(1)}, f32[40,128]{1,0:T(8,128)S(1)}, u32[]{:S(2)}, u32[]{:S(2)}) collective-permute-start(f32[40,128]{1,0:T(8,128)S(1)} %get-tuple-element.43.after_ref), channel_id=1, source_target_pairs={{0,2},{1,3},{2,4},{3,5},{4,6},{5,7},{6,8},{7,9},{8,10},{9,11},{10,... | collective-permute-start | bytes 61448 | tf_op jit(solution)/shard_map/ppermute | solution.py:444
  17.3 0.0 copy-done.1
  17.3 0.4 prepare.1
  17.7 0.8 %collective-permute-done.2.far_ref = f32[40,128]{1,0:T(8,128)S(1)} collective-permute-done((f32[40,128]{1,0:T(8,128)S(1)}, f32[40,128]{1,0:T(8,128)S(1)}, u32[]{:S(2)}, u32[]{:S(2)}) %collective-permute-start.2) | collective-permute-done | bytes 20512 | tf_op jit(solution)/shard_map/ppermute | solution.py:444
  18.5 4.1 %collective-permute-done.1.above_ref = f32[144,384]{1,0:T(8,128)S(1)} collective-permute-done((f32[144,384]{1,0:T(8,128)S(1)}, f32[144,384]{1,0:T(8,128)S(1)}, u32[]{:S(2)}, u32[]{:S(2)}) %collective-permute-start.1) | collective-permute-done | bytes 221216 | tf_op jit(solution)/shard_map/ppermute | solution.py:444
  22.6 0.0 collective-permute-done.below_ref
  22.6 1.1 %vertical.2 = (f32[8,144,256]{2,1,0:T(8,128)S(1)}, f32[2,144,256]{2,1,0:T(8,128)S(1)}, f32[144,256]{1,0:T(8,128)S(1)}, f32[144,128]{1,0:T(8,128)S(1)}, f32[144,3...) custom-call(bf16[5,288,256]{2,1,0:T(8,128)(2,1)S(1)} %get-tuple-element.45.m_ref, ...), custom_call_target="tpu_custom_call" | custom-call | flops 1000000000 | bytes 8388608 | tf_op jit(solution)/shard_map/vertical/pallas_call | solution.py:467
  23.7 2.2 %collective-permute-start.4 = (f32[144,512]{1,0:T(8,128)S(1)}, f32[144,512]{1,0:T(8,128)S(1)}, u32[]{:S(2)}, u32[]{:S(2)}) collective-permute-start(f32[144,512]{1,0:T(8,128)S(1)} %get-tuple-element.57), channel_id=1, source_target_pairs={{1,0},{2,1},{3,2},{4,3},{5,4},{6,5},{7,6},{8,7},{9,8},{10,9},{11,1... | collective-permute-start | bytes 884744 | tf_op jit(solution)/shard_map/ppermute | solution.py:444
  25.9 7.2 %collective-permute-start.3 = (f32[144,384]{1,0:T(8,128)S(1)}, f32[144,384]{1,0:T(8,128)S(1)}, u32[]{:S(2)}, u32[]{:S(2)}) collective-permute-start(f32[144,384]{1,0:T(8,128)S(1)} %get-tuple-element.56), channel_id=1, source_target_pairs={{0,1},{1,2},{2,3},{3,4},{4,5},{5,6},{6,7},{7,8},{8,9},{9,10},{10,1... | collective-permute-start | bytes 663560 | tf_op jit(solution)/shard_map/ppermute | solution.py:444
  33.1 2.0 %collective-permute-start.5 = (f32[40,128]{1,0:T(8,128)S(1)}, f32[40,128]{1,0:T(8,128)S(1)}, u32[]{:S(2)}, u32[]{:S(2)}) collective-permute-start(f32[40,128]{1,0:T(8,128)S(1)} %get-tuple-element.58), channel_id=1, source_target_pairs={{2,0},{3,1},{4,2},{5,3},{6,4},{7,5},{8,6},{9,7},{10,8},{11,9},{12,... | collective-permute-start | bytes 61448 | tf_op jit(solution)/shard_map/ppermute | solution.py:444
  35.0 5.9 %collective-permute-done.5.far_ref = f32[40,128]{1,0:T(8,128)S(1)} collective-permute-done((f32[40,128]{1,0:T(8,128)S(1)}, f32[40,128]{1,0:T(8,128)S(1)}, u32[]{:S(2)}, u32[]{:S(2)}) %collective-permute-start.5) | collective-permute-done | bytes 20512 | tf_op jit(solution)/shard_map/ppermute | solution.py:444
  41.0 0.0 collective-permute-done.3.below_ref
  41.0 0.0 collective-permute-done.4.above_ref
  41.0 6.2 %middle.1 = (f32[8,144,256]{2,1,0:T(8,128)S(1)}, f32[2,144,256]{2,1,0:T(8,128)S(1)}, f32[144,256]{1,0:T(8,128)S(1)}, f32[144,128]{1,0:T(8,128)S(1)}, f32[144,512...) custom-call(f32[80,128]{1,0:T(8,128)S(1)} %get-tuple-element.39.filt_ref, ...), custom_call_target="tpu_custom_call" | custom-call | flops 1000000000 | bytes 8388608 | tf_op jit(solution)/shard_map/middle/pallas_call | solution.py:473
  47.1 2.7 %collective-permute-start.6 = (f32[144,512]{1,0:T(8,128)S(1)}, f32[144,512]{1,0:T(8,128)S(1)}, u32[]{:S(2)}, u32[]{:S(2)}) collective-permute-start(f32[144,512]{1,0:T(8,128)S(1)} %get-tuple-element.63), channel_id=1, source_target_pairs={{0,1},{1,2},{2,3},{3,4},{4,5},{5,6},{6,7},{7,8},{8,9},{9,10},{10,1... | collective-permute-start | bytes 884744 | tf_op jit(solution)/shard_map/ppermute | solution.py:444
  49.9 2.0 %collective-permute-start.7 = (f32[144,384]{1,0:T(8,128)S(1)}, f32[144,384]{1,0:T(8,128)S(1)}, u32[]{:S(2)}, u32[]{:S(2)}) collective-permute-start(f32[144,384]{1,0:T(8,128)S(1)} %get-tuple-element.64), channel_id=1, source_target_pairs={{1,0},{2,1},{3,2},{4,3},{5,4},{6,5},{7,6},{8,7},{9,8},{10,9},{11,1... | collective-permute-start | bytes 663560 | tf_op jit(solution)/shard_map/ppermute | solution.py:444
  51.8 2.1 %collective-permute-start.8 = (f32[40,128]{1,0:T(8,128)S(1)}, f32[40,128]{1,0:T(8,128)S(1)}, u32[]{:S(2)}, u32[]{:S(2)}) collective-permute-start(f32[40,128]{1,0:T(8,128)S(1)} %get-tuple-element.65), channel_id=1, source_target_pairs={{0,2},{1,3},{2,4},{3,5},{4,6},{5,7},{6,8},{7,9},{8,10},{9,11},{10,... | collective-permute-start | bytes 61448 | tf_op jit(solution)/shard_map/ppermute | solution.py:444
  53.9 2.8 %collective-permute-done.8.far_ref = f32[40,128]{1,0:T(8,128)S(1)} collective-permute-done((f32[40,128]{1,0:T(8,128)S(1)}, f32[40,128]{1,0:T(8,128)S(1)}, u32[]{:S(2)}, u32[]{:S(2)}) %collective-permute-start.8) | collective-permute-done | bytes 20512 | tf_op jit(solution)/shard_map/ppermute | solution.py:444
  56.7 3.8 %collective-permute-done.7.above_ref = f32[144,384]{1,0:T(8,128)S(1)} collective-permute-done((f32[144,384]{1,0:T(8,128)S(1)}, f32[144,384]{1,0:T(8,128)S(1)}, u32[]{:S(2)}, u32[]{:S(2)}) %collective-permute-start.7) | collective-permute-done | bytes 221216 | tf_op jit(solution)/shard_map/ppermute | solution.py:444
  60.5 0.0 collective-permute-done.6.below_ref
  60.5 1.1 %vertical.3 = (f32[8,144,256]{2,1,0:T(8,128)S(1)}, f32[2,144,256]{2,1,0:T(8,128)S(1)}, f32[144,256]{1,0:T(8,128)S(1)}, f32[144,128]{1,0:T(8,128)S(1)}, f32[144,3...) custom-call(bf16[5,288,256]{2,1,0:T(8,128)(2,1)S(1)} %get-tuple-element.44.m_ref, ...), custom_call_target="tpu_custom_call" | custom-call | flops 1000000000 | bytes 8388608 | tf_op jit(solution)/shard_map/vertical/pallas_call | solution.py:467
  61.6 2.1 %collective-permute-start.10 = (f32[144,512]{1,0:T(8,128)S(1)}, f32[144,512]{1,0:T(8,128)S(1)}, u32[]{:S(2)}, u32[]{:S(2)}) collective-permute-start(f32[144,512]{1,0:T(8,128)S(1)} %get-tuple-element.71), channel_id=1, source_target_pairs={{1,0},{2,1},{3,2},{4,3},{5,4},{6,5},{7,6},{8,7},{9,8},{10,9},{11,1... | collective-permute-start | bytes 884744 | tf_op jit(solution)/shard_map/ppermute | solution.py:444
  63.7 7.2 %collective-permute-start.9 = (f32[144,384]{1,0:T(8,128)S(1)}, f32[144,384]{1,0:T(8,128)S(1)}, u32[]{:S(2)}, u32[]{:S(2)}) collective-permute-start(f32[144,384]{1,0:T(8,128)S(1)} %get-tuple-element.70), channel_id=1, source_target_pairs={{0,1},{1,2},{2,3},{3,4},{4,5},{5,6},{6,7},{7,8},{8,9},{9,10},{10,1... | collective-permute-start | bytes 663560 | tf_op jit(solution)/shard_map/ppermute | solution.py:444
  70.9 2.0 %collective-permute-start.11 = (f32[40,128]{1,0:T(8,128)S(1)}, f32[40,128]{1,0:T(8,128)S(1)}, u32[]{:S(2)}, u32[]{:S(2)}) collective-permute-start(f32[40,128]{1,0:T(8,128)S(1)} %get-tuple-element.72), channel_id=1, source_target_pairs={{2,0},{3,1},{4,2},{5,3},{6,4},{7,5},{8,6},{9,7},{10,8},{11,9},{12,... | collective-permute-start | bytes 61448 | tf_op jit(solution)/shard_map/ppermute | solution.py:444
  72.9 5.9 %collective-permute-done.11.far_ref = f32[40,128]{1,0:T(8,128)S(1)} collective-permute-done((f32[40,128]{1,0:T(8,128)S(1)}, f32[40,128]{1,0:T(8,128)S(1)}, u32[]{:S(2)}, u32[]{:S(2)}) %collective-permute-start.11) | collective-permute-done | bytes 20512 | tf_op jit(solution)/shard_map/ppermute | solution.py:444
  78.8 0.0 collective-permute-done.9.below_ref
  78.8 0.0 collective-permute-done.10.above_ref
  78.8 4.5 %last.1 = f32[2192,128]{1,0:T(8,128)} custom-call(f32[80,128]{1,0:T(8,128)S(1)} %get-tuple-element.39.filt_ref, bf16[256,512]{1,0:T(8,128)(2,1)S(1)} %get-tuple-element.40.w0_ref, bf16[3,256,256]{2,1,0:T(8,128)(2,1)S(1)} %get-tuple-element.41.w_ref, bf16[3,256,256]{2,1,0:T(8,128)(2,1)S(1)} %get-tuple-element.42.ww_ref, ...), custom_call_target="tpu_custom_call" | custom-call | flops 1000000000 | bytes 8388608 | tf_op jit(solution)/shard_map/last/pallas_call | solution.py:477
Async XLA Ops:
  0.0 1.3 %copy-start = (f32[137,16,128]{2,1,0:T(8,128)S(1)}, f32[137,16,128]{2,1,0:T(8,128)}, u32[]{:S(2)}) copy-start(f32[137,16,128]{2,1,0:T(8,128)} %param.3) | copy-start | bytes 3366916
  1.3 0.7 copy-start.2
  1.9 15.3 %copy-start.1 = (f32[5,137,137]{2,1,0:T(8,128)S(1)}, f32[5,137,137]{2,1,0:T(8,128)}, u32[]{:S(2)}) copy-start(f32[5,137,137]{2,1,0:T(8,128)} %m_ref.1) | copy-start | bytes 1126144
  6.4 16.3 %collective-permute-start = (f32[144,512]{1,0:T(8,128)S(1)}, f32[144,512]{1,0:T(8,128)S(1)}, u32[]{:S(2)}, u32[]{:S(2)}) collective-permute-start(f32[144,512]{1,0:T(8,128)S(1)} %get-tuple-element.50), channel_id=1, source_target_pairs={{0,1},{1,2},{2,3},{3,4},{4,5},{5,6},{6,7},{7,8},{8,9},{9,10},{10,1... | collective-permute-start | bytes 884744 | tf_op jit(solution)/shard_map/ppermute | solution.py:444
  12.0 10.6 %collective-permute-start.1 = (f32[144,384]{1,0:T(8,128)S(1)}, f32[144,384]{1,0:T(8,128)S(1)}, u32[]{:S(2)}, u32[]{:S(2)}) collective-permute-start(f32[144,384]{1,0:T(8,128)S(1)} %get-tuple-element.51), channel_id=1, source_target_pairs={{1,0},{2,1},{3,2},{4,3},{5,4},{6,5},{7,6},{8,7},{9,8},{10,9},{11,1... | collective-permute-start | bytes 663560 | tf_op jit(solution)/shard_map/ppermute | solution.py:444
  14.0 4.6 %collective-permute-start.2 = (f32[40,128]{1,0:T(8,128)S(1)}, f32[40,128]{1,0:T(8,128)S(1)}, u32[]{:S(2)}, u32[]{:S(2)}) collective-permute-start(f32[40,128]{1,0:T(8,128)S(1)} %get-tuple-element.43.after_ref), channel_id=1, source_target_pairs={{0,2},{1,3},{2,4},{3,5},{4,6},{5,7},{6,8},{7,9},{8,10},{9,11},{10,... | collective-permute-start | bytes 61448 | tf_op jit(solution)/shard_map/ppermute | solution.py:444
  23.7 17.2 %collective-permute-start.4 = (f32[144,512]{1,0:T(8,128)S(1)}, f32[144,512]{1,0:T(8,128)S(1)}, u32[]{:S(2)}, u32[]{:S(2)}) collective-permute-start(f32[144,512]{1,0:T(8,128)S(1)} %get-tuple-element.57), channel_id=1, source_target_pairs={{1,0},{2,1},{3,2},{4,3},{5,4},{6,5},{7,6},{8,7},{9,8},{10,9},{11,1... | collective-permute-start | bytes 884744 | tf_op jit(solution)/shard_map/ppermute | solution.py:444
  25.9 15.1 %collective-permute-start.3 = (f32[144,384]{1,0:T(8,128)S(1)}, f32[144,384]{1,0:T(8,128)S(1)}, u32[]{:S(2)}, u32[]{:S(2)}) collective-permute-start(f32[144,384]{1,0:T(8,128)S(1)} %get-tuple-element.56), channel_id=1, source_target_pairs={{0,1},{1,2},{2,3},{3,4},{4,5},{5,6},{6,7},{7,8},{8,9},{9,10},{10,1... | collective-permute-start | bytes 663560 | tf_op jit(solution)/shard_map/ppermute | solution.py:444
  33.1 7.9 %collective-permute-start.5 = (f32[40,128]{1,0:T(8,128)S(1)}, f32[40,128]{1,0:T(8,128)S(1)}, u32[]{:S(2)}, u32[]{:S(2)}) collective-permute-start(f32[40,128]{1,0:T(8,128)S(1)} %get-tuple-element.58), channel_id=1, source_target_pairs={{2,0},{3,1},{4,2},{5,3},{6,4},{7,5},{8,6},{9,7},{10,8},{11,9},{12,... | collective-permute-start | bytes 61448 | tf_op jit(solution)/shard_map/ppermute | solution.py:444
  47.1 13.3 %collective-permute-start.6 = (f32[144,512]{1,0:T(8,128)S(1)}, f32[144,512]{1,0:T(8,128)S(1)}, u32[]{:S(2)}, u32[]{:S(2)}) collective-permute-start(f32[144,512]{1,0:T(8,128)S(1)} %get-tuple-element.63), channel_id=1, source_target_pairs={{0,1},{1,2},{2,3},{3,4},{4,5},{5,6},{6,7},{7,8},{8,9},{9,10},{10,1... | collective-permute-start | bytes 884744 | tf_op jit(solution)/shard_map/ppermute | solution.py:444
  49.9 10.6 %collective-permute-start.7 = (f32[144,384]{1,0:T(8,128)S(1)}, f32[144,384]{1,0:T(8,128)S(1)}, u32[]{:S(2)}, u32[]{:S(2)}) collective-permute-start(f32[144,384]{1,0:T(8,128)S(1)} %get-tuple-element.64), channel_id=1, source_target_pairs={{1,0},{2,1},{3,2},{4,3},{5,4},{6,5},{7,6},{8,7},{9,8},{10,9},{11,1... | collective-permute-start | bytes 663560 | tf_op jit(solution)/shard_map/ppermute | solution.py:444
  51.8 4.9 %collective-permute-start.8 = (f32[40,128]{1,0:T(8,128)S(1)}, f32[40,128]{1,0:T(8,128)S(1)}, u32[]{:S(2)}, u32[]{:S(2)}) collective-permute-start(f32[40,128]{1,0:T(8,128)S(1)} %get-tuple-element.65), channel_id=1, source_target_pairs={{0,2},{1,3},{2,4},{3,5},{4,6},{5,7},{6,8},{7,9},{8,10},{9,11},{10,... | collective-permute-start | bytes 61448 | tf_op jit(solution)/shard_map/ppermute | solution.py:444
  61.6 17.2 %collective-permute-start.10 = (f32[144,512]{1,0:T(8,128)S(1)}, f32[144,512]{1,0:T(8,128)S(1)}, u32[]{:S(2)}, u32[]{:S(2)}) collective-permute-start(f32[144,512]{1,0:T(8,128)S(1)} %get-tuple-element.71), channel_id=1, source_target_pairs={{1,0},{2,1},{3,2},{4,3},{5,4},{6,5},{7,6},{8,7},{9,8},{10,9},{11,1... | collective-permute-start | bytes 884744 | tf_op jit(solution)/shard_map/ppermute | solution.py:444
  63.7 15.1 %collective-permute-start.9 = (f32[144,384]{1,0:T(8,128)S(1)}, f32[144,384]{1,0:T(8,128)S(1)}, u32[]{:S(2)}, u32[]{:S(2)}) collective-permute-start(f32[144,384]{1,0:T(8,128)S(1)} %get-tuple-element.70), channel_id=1, source_target_pairs={{0,1},{1,2},{2,3},{3,4},{4,5},{5,6},{6,7},{7,8},{8,9},{9,10},{10,1... | collective-permute-start | bytes 663560 | tf_op jit(solution)/shard_map/ppermute | solution.py:444
  70.9 7.9 %collective-permute-start.11 = (f32[40,128]{1,0:T(8,128)S(1)}, f32[40,128]{1,0:T(8,128)S(1)}, u32[]{:S(2)}, u32[]{:S(2)}) collective-permute-start(f32[40,128]{1,0:T(8,128)S(1)} %get-tuple-element.72), channel_id=1, source_target_pairs={{2,0},{3,1},{4,2},{5,3},{6,4},{7,5},{8,6},{9,7},{10,8},{11,9},{12,... | collective-permute-start | bytes 61448 | tf_op jit(solution)/shard_map/ppermute | solution.py:444
where the time goes:
time: 83.8 us; the launch traced here: 83.3 us
  starting transfers between devices  40.2 us (48%)
  waiting for transfers between devices  23.4 us (28%)
  Pallas kernels  17.7 us (21%)
  local copies, waits for them, and re-layouts  1.95 us (2%)
    ppermute x12, starting transfers between devices, shift(): lax.ppermute(values, 'lat', [(i, i + by) for i in range(count) if 0 <= i...  40.2 us
    ppermute x12, waiting for transfers between devices, shift(): lax.ppermute(values, 'lat', [(i, i + by) for i in range(count) if 0 <= i...  23.4 us
    pallas_call x1, Pallas kernels, on_device(): call(middle_kernel, [VMEM] * 11, COEFFICIENTS + WIDE_FIRST, spread + halv...  6.18 us
    pallas_call x1, Pallas kernels, on_device(): call(last_kernel, [VMEM] * 11, (((levels * rows, columns), F32),), spread...  4.54 us
    pallas_call x1, Pallas kernels, on_device(): call(first_kernel, [SMEM, VMEM], WEIGHTS + COEFFICIENTS + WIDE_FIRST, hal...  4.41 us
    pallas_call x2, Pallas kernels, vertical(): call(vertical_kernel, [VMEM] * 8, COEFFICIENTS + WIDE_SECOND, [], 'vertic...  2.19 us
    unnamed x6, local copies, waits for them, and re-layouts  1.95 us
  transfers between devices with their start and end apart: 12, of which 6 were waited for; matrix products, arithmetic and copies ran while one was open for 0% of the time, Pallas kernels for 0%

commit v1 on v0

--- a/solution.py
+++ b/solution.py
@@ -180,27 +180,26 @@
     return rows
 
 
-def pack(c0, c1, c2, c3, c1b=None, c2b=None):
+def pack(c0, c1, c2, c3, c1b, c2b):
     lane = lane_ids(PAD)
-    extra = jnp.zeros((PAD, LANES), F32) if c2b is None else pltpu.roll(c2b, 80, 1)
-    tiles = [
+    return [
         c0[:, 0:128],
-        jnp.where(lane < 64, c0[:, 128:256], jnp.where(lane < 112, pltpu.roll(c2, 64, 1), extra)),
+        jnp.where(lane < 64, c0[:, 128:256], jnp.where(lane < 112, pltpu.roll(c2, 64, 1), pltpu.roll(c2b, 80, 1))),
         jnp.where(lane < 96, c1, pltpu.roll(c3, 96, 1)),
+        jnp.where(lane < 96, c1b, pltpu.roll(c2b, 96, 1)),
     ]
-    if c1b is not None:
-        tiles.append(jnp.where(lane < 96, c1b, pltpu.roll(c2b, 96, 1)))
-    return tiles
-
-
-def unpack(ref):
-    tile1 = ref[:, 128:256]
-    tile2 = ref[:, 256:384]
-    parts = [ref[:, 0:256], tile2, pltpu.roll(tile1, 64, 1), pltpu.roll(tile2, 32, 1)]
-    if ref.shape[1] > 384:
-        tile3 = ref[:, 384:512]
+
+
+def unpack(tiles):
+    parts = [
+        jnp.concatenate([tiles[0], tiles[1]], axis=1),
+        tiles[2],
+        pltpu.roll(tiles[1], 64, 1),
+        pltpu.roll(tiles[2], 32, 1),
+    ]
+    if len(tiles) > 3:
         lane = lane_ids(PAD)
-        parts += [tile3, jnp.where(lane < 32, pltpu.roll(tile3, 32, 1), pltpu.roll(tile1, 48, 1))]
+        parts += [tiles[3], jnp.where(lane < 32, pltpu.roll(tiles[3], 32, 1), pltpu.roll(tiles[1], 48, 1))]
     return parts
 
 
@@ -224,6 +223,31 @@
     return jnp.concatenate(parts[:3] + [parts[3][0:24]], axis=0)
 
 
+def is_even():
+    return lax.rem(lax.axis_index("lat"), 2) == 0
+
+
+def put(ref, tiles):
+    for t, tile in enumerate(tiles):
+        ref[t * PAD : t * PAD + PAD, :] = tile
+
+
+def received(mate_ref, side_ref, n_below, n_above):
+    even = is_even()
+    place = lax.axis_index("lat")
+    no_below = place == 0
+    no_above = place == lax.axis_size("lat") - 1
+    below, above = [], []
+    for t in range(max(n_below, n_above)):
+        mate = mate_ref[t * PAD : t * PAD + PAD, :]
+        side = side_ref[t * PAD : t * PAD + PAD, :]
+        if t < n_below:
+            below.append(jnp.where(no_below, 0.0, jnp.where(even, side, mate)))
+        if t < n_above:
+            above.append(jnp.where(no_above, 0.0, jnp.where(even, mate, side)))
+    return below, above
+
+
 def store_split(hi_ref, lo_ref, out, at):
     for place, (a, d) in out.items():
         for part, values in ((0, a), (1, d)):
@@ -233,75 +257,96 @@
             lo_ref[place, at, lanes] = low
 
 
-def longitude_analysis(hi_ref, lo_ref, w0_ref, w_ref, c0_ref, c1_ref, c2_ref, c3_ref, up_ref, down_ref, far_ref):
-    def level0(index):
-        s = slot(0, index)
+def bands(hi_ref, lo_ref, w0_ref, w_ref):
+    def level0(s):
         w_high, w_low = w0_ref[:, 0:256], w0_ref[:, 256:512]
         high = hi_ref[s]
         return dot(high, w_high) + dot(high, w_low) + dot(lo_ref[s], w_high)
 
-    def others(level, index):
-        s = slot(level, index)
+    def others(level, s):
         both = dot(hi_ref[s], w_ref[level - 1])
         return both[:, 0:128] + both[:, 128:256] + dot(lo_ref[s], w_ref[level - 1, :, 0:128])
 
-    c3 = {i: others(3, i) for i in range(-1, 3)}
-    far_ref[...] = pack_coarse(c3[2])
-    up = pack(level0(8), others(1, 4), others(2, 2), c3[1], others(1, 5), others(2, 3))
-    for t, tile in enumerate(up):
-        up_ref[:, t * LANES : t * LANES + LANES] = tile
-    down = pack(level0(-1), others(1, -1), others(2, -1), c3[-1])
-    for t, tile in enumerate(down):
-        down_ref[:, t * LANES : t * LANES + LANES] = tile
-    c3_ref[...] = c3[0]
-    for i in range(8):
-        c0_ref[i] = level0(i)
-    for i in range(4):
-        c1_ref[i // 2, :, (i % 2) * 128 : (i % 2) * 128 + 128] = others(1, i)
-    for i in range(2):
-        c2_ref[:, i * 128 : i * 128 + 128] = others(2, i)
-
-
-def longitude_synthesis(
-    y0_ref, y1_ref, y2_ref, y3_ref, below_ref, above_ref, far_ref, w0_ref, w_ref, ww_ref, u_ref
-):
-    below = unpack(below_ref)
-    above = unpack(above_ref)
+    return level0, others
+
+
+def sums_message(hi_ref, lo_ref, w0_ref, w_ref, upward):
+    level0, others = bands(hi_ref, lo_ref, w0_ref, w_ref)
+
+    def chosen(level, up_index):
+        return jnp.where(upward, slot(level, up_index), slot(level, -1))
+
+    return pack(
+        level0(chosen(0, 8)),
+        others(1, chosen(1, 4)),
+        others(2, chosen(2, 2)),
+        others(3, chosen(3, 1)),
+        others(1, slot(1, 5)),
+        others(2, slot(2, 3)),
+    )
+
+
+def apply_vertical(m_ref, band, values):
+    high, low = split(values)
+    zeros = jnp.zeros((KPAD - PAD, values.shape[1]), BF16)
+    high = jnp.concatenate([high, zeros], axis=0)
+    low = jnp.concatenate([low, zeros], axis=0)
+    both = dot(m_ref[band], high)
+    return both[0:PAD] + both[PAD:] + dot(m_ref[band, 0:PAD], low)
+
+
+def spread_level0(values, w0_ref):
+    high, low = split(values)
+    w_high, w_low = w0_ref[:, 0:256], w0_ref[:, 256:512]
+    return dot_t(high, w_high) + dot_t(low, w_high) + dot_t(high, w_low)
+
+
+def spread_other(level, values, w_ref, ww_ref):
+    high, low = split(values)
+    pair = jnp.concatenate([high, low], axis=1)
+    return dot_t(pair, ww_ref[level - 1]) + dot_t(high, w_ref[level - 1, :, 128:256])
+
+
+OWN_BASE = (0, 8, 12, 14)
+GOT = {(0, -1): 0, (0, 8): 1, (1, -1): 2, (1, 4): 3, (1, 5): 4, (2, -1): 5, (2, 2): 6, (2, 3): 7, (3, -1): 8, (3, 1): 9, (3, 2): 10}
+
+
+def spread_received(mate_ref, side_ref, far_ref, w0_ref, w_ref, ww_ref, got_ref):
+    below, above = received(mate_ref, side_ref, 3, 4)
+    below, above = unpack(below), unpack(above)
     far = unpack_coarse(far_ref)
-    c0 = {-1: below[0], 8: above[0]}
-    c1 = {-1: below[1], 4: above[1], 5: above[4]}
-    c2 = {-1: below[2], 2: above[2], 3: above[5]}
-    c3 = {-1: below[3], 1: above[3], 2: far, 0: y3_ref[...]}
-    for i in range(8):
-        c0[i] = y0_ref[i]
-    for i in range(4):
-        c1[i] = y1_ref[i // 2, :, (i % 2) * 128 : (i % 2) * 128 + 128]
-    for i in range(2):
-        c2[i] = y2_ref[:, i * 128 : i * 128 + 128]
-    for i, values in c0.items():
-        high, low = split(values)
-        w_high, w_low = w0_ref[:, 0:256], w0_ref[:, 256:512]
-        u_ref[slot(0, i)] = dot_t(high, w_high) + dot_t(low, w_high) + dot_t(high, w_low)
-    for level, group in ((1, c1), (2, c2), (3, c3)):
-        for i, values in group.items():
-            high, low = split(values)
-            pair = jnp.concatenate([high, low], axis=1)
-            u_ref[slot(level, i)] = dot_t(pair, ww_ref[level - 1]) + dot_t(high, w_ref[level - 1, :, 128:256])
-
-
-def pick_at(u_ref, at):
+    values = {(0, -1): below[0], (0, 8): above[0], (1, -1): below[1], (1, 4): above[1], (1, 5): above[4],
+              (2, -1): below[2], (2, 2): above[2], (2, 3): above[5], (3, -1): below[3], (3, 1): above[3], (3, 2): far}
+    for (level, index), v in values.items():
+        if level == 0:
+            got_ref[GOT[level, index]] = spread_level0(v, w0_ref)
+        else:
+            got_ref[GOT[level, index]] = spread_other(level, v, w_ref, ww_ref)
+
+
+def pick_at(own_ref, got_ref, at):
+    table = {}
+    for level in range(LEVELS):
+        for index in range(FIRST, LAST[level] + 1):
+            if 0 <= index < OWN[level]:
+                table[slot(level, index)] = (own_ref, OWN_BASE[level] + index)
+            else:
+                table[slot(level, index)] = (got_ref, GOT[level, index])
+
     def pick(place):
-        return u_ref[place, at, 0:128], u_ref[place, at, 128:256]
+        ref, i = table[place]
+        return ref[i, at, 0:128], ref[i, at, 128:256]
 
     return pick
 
 
-def first_kernel(taps_ref, x_ref, *rest):
-    filt_ref, w0_ref, w_ref, ww_ref, *outs = rest[:-2]
-    hi_ref, lo_ref = rest[-2:]
+def first_kernel(taps_ref, x_hbm, filt_ref, w0_ref, w_ref, ww_ref, hi_ref, lo_ref, side_ref, x_ref, sem):
+    fetch = pltpu.make_async_copy(x_hbm, x_ref, sem)
+    fetch.start()
     write_filters(taps_ref, filt_ref)
     flags = edge_flags()
     write_weights(filt_ref, w0_ref, w_ref, ww_ref)
+    fetch.wait()
 
     def chunk(c, carry):
         start = pl.multiple_of(c * (16 * ROWS), 16 * ROWS)
@@ -318,84 +363,113 @@
         tail = jnp.where(top, x_ref[136 * ROWS + r : 136 * ROWS + r + 1, :], 0.0)
         rows[r] = jnp.concatenate([head, tail], axis=0)
     store_split(hi_ref, lo_ref, latitude_analysis(rows, filt_ref, flags), slice(128, 144))
-    longitude_analysis(hi_ref, lo_ref, w0_ref, w_ref, *outs)
-
-
-def vertical_kernel(m_ref, c0_ref, c1_ref, c2_ref, c3_ref, below_ref, above_ref, far_ref, y0_ref, y1_ref, y2_ref, y3_ref,
-                    up_ref, down_ref, far_out_ref):
-    below = unpack(below_ref)
-    above = unpack(above_ref)
+    put(side_ref, sums_message(hi_ref, lo_ref, w0_ref, w_ref, jnp.logical_not(is_even())))
+
+
+def mate_kernel(hi_ref, lo_ref, w0_ref, w_ref, mate_ref, far_ref):
+    put(mate_ref, sums_message(hi_ref, lo_ref, w0_ref, w_ref, is_even()))
+    _, others = bands(hi_ref, lo_ref, w0_ref, w_ref)
+    far_ref[...] = pack_coarse(others(3, slot(3, 2)))
+
+
+def own_kernel(hi_ref, lo_ref, w0_ref, w_ref, m_ref, c0_ref, c1_ref, c1b_ref, c2_ref, c3_ref, y0_ref, y1_ref):
+    level0, others = bands(hi_ref, lo_ref, w0_ref, w_ref)
+    c0_ref[0] = level0(slot(0, 0))
+    c0_ref[1] = level0(slot(0, 7))
+    c1_ref[:, 0:128] = others(1, slot(1, 0))
+    c1_ref[:, 128:256] = others(1, slot(1, 1))
+    c1b_ref[...] = others(1, slot(1, 3))
+    c2_ref[:, 0:128] = others(2, slot(2, 0))
+    c2_ref[:, 128:256] = others(2, slot(2, 1))
+    c3_ref[...] = others(3, slot(3, 0))
+    y1_ref[...] = apply_vertical(m_ref, 1, others(1, slot(1, 2)))
+    for i in range(1, 7):
+        y0_ref[i - 1] = apply_vertical(m_ref, 0, level0(slot(0, i)))
+
+
+def vertical_kernel(m_ref, c0_ref, c1_ref, c1b_ref, c2_ref, c3_ref, mate_ref, side_ref, far_ref,
+                    y0_ref, y1_ref, y1b_ref, y2_ref, y3_ref, mate_out_ref, side_out_ref, far_out_ref):
+    below, above = received(mate_ref, side_ref, 4, 3)
+    below, above = unpack(below), unpack(above)
     far = unpack_coarse(far_ref)
-
-    def apply(band, values):
-        high, low = split(values)
-        zeros = jnp.zeros((KPAD - PAD, values.shape[1]), BF16)
-        high = jnp.concatenate([high, zeros], axis=0)
-        low = jnp.concatenate([low, zeros], axis=0)
-        both = dot(m_ref[band], high)
-        return both[0:PAD] + both[PAD:] + dot(m_ref[band, 0:PAD], low)
-
     c3 = c3_ref[...] + below[3] + above[3] + far
     lane = lane_ids(PAD)
-    y3 = jnp.where(lane < 24, apply(3, c3), apply(4, c3))
+    y3 = jnp.where(lane < 24, apply_vertical(m_ref, 3, c3), apply_vertical(m_ref, 4, c3))
+    c2 = c2_ref[...]
+    y2 = apply_vertical(m_ref, 2, jnp.concatenate([c2[:, 0:128] + below[2], c2[:, 128:256] + below[5] + above[2]], axis=1))
+    c1 = c1_ref[...]
+    y1 = apply_vertical(m_ref, 1, jnp.concatenate([c1[:, 0:128] + below[1], c1[:, 128:256] + below[4]], axis=1))
+    y1b = apply_vertical(m_ref, 1, c1b_ref[...] + above[1])
+    first = apply_vertical(m_ref, 0, c0_ref[0] + below[0])
+    last = apply_vertical(m_ref, 0, c0_ref[1] + above[0])
+    y0_ref[0] = first
+    y0_ref[1] = last
+    y1_ref[...] = y1
+    y1b_ref[...] = y1b
+    y2_ref[...] = y2
     y3_ref[...] = y3
     far_out_ref[...] = pack_coarse(y3)
-    c2 = c2_ref[...]
-    y2 = apply(2, jnp.concatenate([c2[:, 0:128] + below[2], c2[:, 128:256] + below[5] + above[2]], axis=1))
-    y2_ref[...] = y2
-    c1 = c1_ref[0]
-    y1_low = apply(1, jnp.concatenate([c1[:, 0:128] + below[1], c1[:, 128:256] + below[4]], axis=1))
-    c1 = c1_ref[1]
-    y1_high = apply(1, jnp.concatenate([c1[:, 0:128], c1[:, 128:256] + above[1]], axis=1))
-    y1_ref[0] = y1_low
-    y1_ref[1] = y1_high
-    first = apply(0, c0_ref[0] + below[0])
-    last = apply(0, c0_ref[7] + above[0])
-    y0_ref[0] = first
-    y0_ref[7] = last
-    down = pack(first, y1_low[:, 0:128], y2[:, 0:128], y3, y1_low[:, 128:256], y2[:, 128:256])
-    for t, tile in enumerate(down):
-        down_ref[:, t * LANES : t * LANES + LANES] = tile
-    up = pack(last, y1_high[:, 128:256], y2[:, 128:256], y3)
-    for t, tile in enumerate(up):
-        up_ref[:, t * LANES : t * LANES + LANES] = tile
-    for i in range(1, 7):
-        y0_ref[i] = apply(0, c0_ref[i])
-
-
-def middle_kernel(filt_ref, w0_ref, w_ref, ww_ref, y0_ref, y1_ref, y2_ref, y3_ref, below_ref, above_ref, far_ref, *rest):
-    *outs, u_ref, hi_ref, lo_ref = rest
+    down = pack(first, y1[:, 0:128], y2[:, 0:128], y3, y1[:, 128:256], y2[:, 128:256])
+    up = pack(last, y1b, y2[:, 128:256], y3, y1[:, 128:256], y2[:, 128:256])
+    even = is_even()
+    put(side_out_ref, [jnp.where(even, d, u) for d, u in zip(down, up)])
+    put(mate_out_ref, [jnp.where(even, u, d) for d, u in zip(down, up)])
+
+
+def spread_kernel(w0_ref, w_ref, ww_ref, y0c_ref, y1c_ref, y0_ref, y1_ref, y1b_ref, y2_ref, y3_ref, own_ref):
+    for i in range(8):
+        values = y0_ref[i // 7] if i in (0, 7) else y0c_ref[i - 1]
+        own_ref[i] = spread_level0(values, w0_ref)
+    for i, values in enumerate((y1_ref[:, 0:128], y1_ref[:, 128:256], y1c_ref[...], y1b_ref[...])):
+        own_ref[8 + i] = spread_other(1, values, w_ref, ww_ref)
+    for i in range(2):
+        own_ref[12 + i] = spread_other(2, y2_ref[:, i * 128 : i * 128 + 128], w_ref, ww_ref)
+    own_ref[14] = spread_other(3, y3_ref[...], w_ref, ww_ref)
+
+
+def middle_kernel(filt_ref, w0_ref, w_ref, ww_ref, own_ref, mate_ref, side_ref, far_ref, hi_ref, lo_ref, side_out_ref,
+                  got_ref):
     flags = edge_flags()
-    longitude_synthesis(y0_ref, y1_ref, y2_ref, y3_ref, below_ref, above_ref, far_ref, w0_ref, w_ref, ww_ref, u_ref)
+    spread_received(mate_ref, side_ref, far_ref, w0_ref, w_ref, ww_ref, got_ref)
 
     def chunk(c, carry):
         at = pl.ds(pl.multiple_of(c * 16, 16), 16)
-        rows = latitude_synthesis(pick_at(u_ref, at), filt_ref, flags)
+        rows = latitude_synthesis(pick_at(own_ref, got_ref, at), filt_ref, flags)
         store_split(hi_ref, lo_ref, latitude_analysis(rows, filt_ref, flags), at)
         return carry
 
     lax.fori_loop(0, 9, chunk, 0)
-    longitude_analysis(hi_ref, lo_ref, w0_ref, w_ref, *outs)
-
-
-def last_kernel(filt_ref, w0_ref, w_ref, ww_ref, y0_ref, y1_ref, y2_ref, y3_ref, below_ref, above_ref, far_ref, out_ref,
-                u_ref):
+    put(side_out_ref, sums_message(hi_ref, lo_ref, w0_ref, w_ref, jnp.logical_not(is_even())))
+
+
+def last_kernel(filt_ref, w0_ref, w_ref, ww_ref, own_ref, mate_ref, side_ref, far_ref, out_hbm, got_ref, out_ref, sems):
     flags = edge_flags()
-    longitude_synthesis(y0_ref, y1_ref, y2_ref, y3_ref, below_ref, above_ref, far_ref, w0_ref, w_ref, ww_ref, u_ref)
+    spread_received(mate_ref, side_ref, far_ref, w0_ref, w_ref, ww_ref, got_ref)
+
+    def leave(c):
+        part = pl.ds(pl.multiple_of(c * (16 * ROWS), 16 * ROWS), 16 * ROWS)
+        return pltpu.make_async_copy(out_ref.at[part, :], out_hbm.at[part, :], sems.at[c])
 
     def chunk(c, carry):
         at = pl.ds(pl.multiple_of(c * 16, 16), 16)
-        rows = latitude_synthesis(pick_at(u_ref, at), filt_ref, flags)
+        rows = latitude_synthesis(pick_at(own_ref, got_ref, at), filt_ref, flags)
         start = pl.multiple_of(c * (16 * ROWS), 16 * ROWS)
         for r, values in rows.items():
             out_ref[pl.ds(start + r, 16, stride=ROWS), :] = values
+        leave(c).start()
         return carry
 
     lax.fori_loop(0, 8, chunk, 0)
-    rows = latitude_synthesis(pick_at(u_ref, slice(128, 144)), filt_ref, flags)
+    rows = latitude_synthesis(pick_at(own_ref, got_ref, slice(128, 144)), filt_ref, flags)
     for r, values in rows.items():
         out_ref[pl.ds(128 * ROWS + r, 8, stride=ROWS), :] = values[0:8]
         out_ref[136 * ROWS + r : 136 * ROWS + r + 1, :] = values[8:9]
+    rest = pl.ds(128 * ROWS, 9 * ROWS)
+    tail = pltpu.make_async_copy(out_ref.at[rest, :], out_hbm.at[rest, :], sems.at[8])
+    tail.start()
+    for c in range(8):
+        leave(c).wait()
+    tail.wait()
 
 
 def prepare_kernel(m_ref, after_ref, plain_ref, turned_ref, wide_ref):
@@ -413,30 +487,38 @@
 
 VMEM = pl.BlockSpec(memory_space=pltpu.VMEM)
 SMEM = pl.BlockSpec(memory_space=pltpu.SMEM)
+HBM = pl.BlockSpec(memory_space=pltpu.HBM)
 ANY = pl.BlockSpec(memory_space=pl.ANY)
 
-
-def shapes(*items):
-    return [jax.ShapeDtypeStruct(shape, dtype) for shape, dtype in items]
-
-
-COEFFICIENTS = (((8, PAD, 256), F32), ((2, PAD, 256), F32), ((PAD, 256), F32), ((PAD, LANES), F32))
-WIDE_FIRST = (((PAD, 512), F32), ((PAD, 384), F32), ((40, LANES), F32))
-WIDE_SECOND = (((PAD, 384), F32), ((PAD, 512), F32), ((40, LANES), F32))
+MESSAGE = ((4 * PAD, LANES), F32)
+FAR = ((40, LANES), F32)
 WEIGHTS = (((80, LANES), F32), ((256, 512), BF16), ((3, 256, 256), BF16), ((3, 256, 256), BF16))
-
-
-def call(kernel, in_specs, outs, scratch, name, limit, flops):
+HALVES = (((SLOTS, PAD, 256), BF16),) * 2
+EDGES = (((2, PAD, 256), F32), ((PAD, 256), F32), ((PAD, LANES), F32), ((PAD, 256), F32), ((PAD, LANES), F32))
+INNER = (((6, PAD, 256), F32), ((PAD, LANES), F32))
+OWN_WIDE = ((15, PAD, 256), F32)
+GOT_WIDE = pltpu.VMEM((11, PAD, 256), F32)
+
+
+def call(kernel, in_specs, outs, scratch, name, limit, out_spec=VMEM):
     return pl.pallas_call(
         kernel,
-        out_shape=shapes(*outs),
+        out_shape=[jax.ShapeDtypeStruct(shape, dtype) for shape, dtype in outs],
         in_specs=in_specs,
-        out_specs=[VMEM] * len(outs),
+        out_specs=[out_spec] * len(outs),
         scratch_shapes=scratch,
         compiler_params=pltpu.CompilerParams(vmem_limit_bytes=limit * MIB),
-        cost_estimate=pl.CostEstimate(flops=flops, bytes_accessed=8 * MIB, transcendentals=0),
+        cost_estimate=pl.CostEstimate(flops=10**9, bytes_accessed=8 * MIB, transcendentals=0),
         name=name,
     )
+
+
+def swap(values, phase):
+    count = lax.axis_size("lat")
+    partner = {}
+    for i in range(phase, count - 1, 2):
+        partner[i], partner[i + 1] = i + 1, i
+    return lax.ppermute(values, "lat", [(i, partner.get(i, i)) for i in range(count)])
 
 
 def shift(values, by):
@@ -447,36 +529,33 @@
 def on_device(increment, filter_taps, band_roots):
     levels, rows, columns = increment.shape
     flat = increment.reshape(levels * rows, columns)
-    halves = [pltpu.VMEM((SLOTS, PAD, 256), BF16)] * 2
-    spread = [pltpu.VMEM((SLOTS, PAD, 256), F32)]
-    filt, w0, w, ww, *rest = call(
-        first_kernel, [SMEM, VMEM], WEIGHTS + COEFFICIENTS + WIDE_FIRST, halves, "first", 24, 10**9
+    filt, w0, w, ww, hi, lo, side = call(
+        first_kernel, [SMEM, HBM], WEIGHTS + HALVES + (MESSAGE,),
+        [pltpu.VMEM((levels * rows, columns), F32), pltpu.SemaphoreType.DMA], "first", 16,
     )(filter_taps, flat)
     plain, turned = call(
-        prepare_kernel, [VMEM, ANY], (((5, 2 * PAD, 256), BF16),) * 2, [pltpu.VMEM((256, 256), F32)], "prepare", 16, 10**9
-    )(band_roots, rest[-1])
-    weights = [filt, w0, w, ww]
-
-    def exchange_sums(up, down, far):
-        return shift(up, 1), shift(down, -1), shift(far, 2)
-
-    def exchange_values(up, down, far):
-        return shift(up, 1), shift(down, -1), shift(far, -2)
-
-    def vertical(matrix, own, received):
-        return call(
-            vertical_kernel, [VMEM] * 8, COEFFICIENTS + WIDE_SECOND, [], "vertical", 24, 10**9
-        )(matrix, *own, *received)
-
-    own, wide = rest[:4], rest[4:]
-    *own, up, down, far = vertical(plain, own, exchange_sums(*wide))
-    *own, up, down, far = call(
-        middle_kernel, [VMEM] * 11, COEFFICIENTS + WIDE_FIRST, spread + halves, "middle", 32, 10**9
-    )(*weights, *own, *exchange_values(up, down, far))
-    *own, up, down, far = vertical(turned, own, exchange_sums(up, down, far))
+        prepare_kernel, [VMEM, ANY], (((5, 2 * PAD, 256), BF16),) * 2, [pltpu.VMEM((256, 256), F32)], "prepare", 12
+    )(band_roots, side)
+
+    def half(matrix, hi, lo, side):
+        side = swap(side, 1)
+        mate, far = call(mate_kernel, [VMEM] * 4, (MESSAGE, FAR), [], "mate", 12)(hi, lo, w0, w)
+        mate, far = swap(mate, 0), shift(far, 2)
+        *edges, y0c, y1c = call(own_kernel, [VMEM] * 5, EDGES + INNER, [], "own", 12)(hi, lo, w0, w, matrix)
+        *edges, mate, side, far = call(
+            vertical_kernel, [VMEM] * 9, EDGES + (MESSAGE, MESSAGE, FAR), [], "vertical", 12
+        )(matrix, *edges, mate, side, far)
+        side, mate, far = swap(side, 1), swap(mate, 0), shift(far, -2)
+        (own,) = call(spread_kernel, [VMEM] * 10, (OWN_WIDE,), [], "spread", 12)(w0, w, ww, y0c, y1c, *edges)
+        return filt, w0, w, ww, own, mate, side, far
+
+    hi, lo, side = call(middle_kernel, [VMEM] * 8, HALVES + (MESSAGE,), [GOT_WIDE], "middle", 16)(
+        *half(plain, hi, lo, side)
+    )
     (out,) = call(
-        last_kernel, [VMEM] * 11, (((levels * rows, columns), F32),), spread, "last", 24, 10**9
-    )(*weights, *own, *exchange_values(up, down, far))
+        last_kernel, [VMEM] * 8, (((levels * rows, columns), F32),),
+        [GOT_WIDE, pltpu.VMEM((levels * rows, columns), F32), pltpu.SemaphoreType.DMA((9,))], "last", 16, HBM,
+    )(*half(turned, hi, lo, side))
     return out.reshape(levels, rows, columns)
 
 

time: 83.8 us -> 68.1 us (0.81)
  waiting for transfers between devices: 23.4 us -> 8.73 us
  starting transfers between devices: 40.2 us -> 36.9 us
  Pallas kernels: 17.7 us -> 19.9 us
    ppermute x12 -> x4, starting transfers between devices: 40.2 us -> 12.8 us  [shift(): lax.ppermute(values, 'lat', [(i, i + by) for i in range(count) if 0 <= i...]
    ppermute x0 -> x8, starting transfers between devices: none -> 24.1 us  [swap(): lax.ppermute(values, 'lat', [(i, partner.get(i, i)) for i in range(count)])]
    ppermute x12 -> x4, waiting for transfers between devices: 23.4 us -> 8.7 us  [shift(): lax.ppermute(values, 'lat', [(i, i + by) for i in range(count) if 0 <= i...]
    pallas_call x5 -> x11, Pallas kernels: 17.3 us -> 19.5 us  [the longest x1 3.97 us: on_device(): call(middle_kernel, [VMEM] * 8, HALVES + (MESSAGE,), [GOT_WIDE], 'middle'...]
  transfers between devices with their start and end apart: 12 -> 12, of which waited for: 6 -> 2; matrix products, arithmetic and copies ran while one was open for 0% -> 0% of each run, Pallas kernels for 0% -> 12%
where the time goes in v1:
time: 68.1 us; the launch traced here: 67.7 us
  starting transfers between devices  36.9 us (54%)
  Pallas kernels  19.9 us (29%)
  waiting for transfers between devices  8.73 us (13%)
  local copies, waits for them, and re-layouts  1.95 us (3%)
    ppermute x8, starting transfers between devices, swap(): lax.ppermute(values, 'lat', [(i, partner.get(i, i)) for i in range(count)])  24.1 us
    ppermute x4, starting transfers between devices, shift(): lax.ppermute(values, 'lat', [(i, i + by) for i in range(count) if 0 <= i...  12.8 us
    ppermute x4, waiting for transfers between devices, shift(): lax.ppermute(values, 'lat', [(i, i + by) for i in range(count) if 0 <= i...  8.7 us
    pallas_call x1, Pallas kernels, on_device(): call(middle_kernel, [VMEM] * 8, HALVES + (MESSAGE,), [GOT_WIDE], 'middle'...  3.97 us
    pallas_call x1, Pallas kernels, on_device(): call(first_kernel, [SMEM, HBM], WEIGHTS + HALVES + (MESSAGE,), [pltpu.VME...  3.77 us
    pallas_call x2, Pallas kernels, half(): call(own_kernel, [VMEM] * 5, EDGES + INNER, [], 'own', 12)  3.36 us
    pallas_call x2, Pallas kernels, half(): call(spread_kernel, [VMEM] * 10, (OWN_WIDE,), [], 'spread', 12)  3.13 us
    pallas_call x1, Pallas kernels, on_device(): call(last_kernel, [VMEM] * 8, (((levels * rows, columns), F32),), [GOT_WI...  2.75 us
  transfers between devices with their start and end apart: 12, of which 2 were waited for; matrix products, arithmetic and copies ran while one was open for 0% of the time, Pallas kernels for 12%

profile of v1, /device:TPU:431, one launch (start us, length us, event | category | flops | bytes accessed | tf_op | source)
XLA Modules:
  0.0 67.7 jit_solution(11097736873239017283)
XLA Ops:
  0.0 0.0 copy-start
  0.0 1.2 %copy-done = f32[137,16,128]{2,1,0:T(8,128)S(1)} copy-done((f32[137,16,128]{2,1,0:T(8,128)S(1)}, f32[137,16,128]{2,1,0:T(8,128)}, u32[]{:S(2)}) %copy-start) | copy-done | bytes 1122328
  1.3 0.0 copy-start.2
  1.3 0.7 %copy-done.2 = s32[4,2,2,5]{3,2,1,0:T(2,128)S(1)} copy-done((s32[4,2,2,5]{3,2,1,0:T(2,128)S(1)}, s32[4,2,2,5]{3,2,1,0:T(2,128)}, u32[]{:S(2)}) %copy-start.2) | copy-done | bytes 344
  1.9 3.8 %first.1 = (f32[80,128]{1,0:T(8,128)S(1)}, bf16[256,512]{1,0:T(8,128)(2,1)S(1)}, bf16[3,256,256]{2,1,0:T(8,128)(2,1)S(1)}, bf16[3,256,256]{2,1,0:T(8,128)(2,1)S(...) custom-call(s32[4,2,2,5]{3,2,1,0:T(2,128)S(1)} %copy-done.2, ...), custom_call_target="tpu_custom_call" | custom-call | flops 1000000000 | bytes 8388608 | tf_op jit(solution)/shard_map/first/pallas_call | solution.py:532
  5.7 5.6 %collective-permute-start.1 = (f32[576,128]{1,0:T(8,128)S(1)}, f32[576,128]{1,0:T(8,128)S(1)}, u32[]{:S(2)}, u32[]{:S(2)}) collective-permute-start(f32[576,128]{1,0:T(8,128)S(1)} %get-tuple-element.57.after_ref), channel_id=1, source_target_pairs={{0,0},{1,2},{2,1},{3,4},{4,3},{5,6},{6,5},{7,8},{8,7},{9,10},{10,9... | collective-permute-start | bytes 884744 | tf_op jit(solution)/shard_map/ppermute | solution.py:521
  11.4 0.0 copy-start.1
  11.4 0.5 mate.2
  11.9 0.1 collective-permute-start
  12.1 3.4 %collective-permute-start.2 = (f32[40,128]{1,0:T(8,128)S(1)}, f32[40,128]{1,0:T(8,128)S(1)}, u32[]{:S(2)}, u32[]{:S(2)}) collective-permute-start(f32[40,128]{1,0:T(8,128)S(1)} %get-tuple-element.67), channel_id=1, source_target_pairs={{0,2},{1,3},{2,4},{3,5},{4,6},{5,7},{6,8},{7,9},{8,10},{9,11},{10,... | collective-permute-start | bytes 61448 | tf_op jit(solution)/shard_map/ppermute | solution.py:526
  15.5 0.0 copy-done.1
  15.5 0.4 prepare.1
  15.9 1.7 %own.2 = (f32[2,144,256]{2,1,0:T(8,128)S(1)}, f32[144,256]{1,0:T(8,128)S(1)}, f32[144,128]{1,0:T(8,128)S(1)}, f32[144,256]{1,0:T(8,128)S(1)}, f32[144,128]{1,0:T...) custom-call(bf16[26,144,256]{2,1,0:T(8,128)(2,1)S(1)} %get-tuple-element.55.hi_ref, ...), custom_call_target="tpu_custom_call" | custom-call | flops 1000000000 | bytes 8388608 | tf_op jit(solution)/shard_map/own/pallas_call | solution.py:544
  17.6 0.0 collective-permute-done.2.far_ref
  17.6 0.0 collective-permute-done.1.side_ref
  17.6 0.0 collective-permute-done.mate_ref
  17.6 0.7 %vertical.2 = (f32[2,144,256]{2,1,0:T(8,128)S(1)}, f32[144,256]{1,0:T(8,128)S(1)}, f32[144,128]{1,0:T(8,128)S(1)}, f32[144,256]{1,0:T(8,128)S(1)}, f32[144,128]{...) custom-call(bf16[5,288,256]{2,1,0:T(8,128)(2,1)S(1)} %get-tuple-element.58.m_ref, ...), custom_call_target="tpu_custom_call" | custom-call | flops 1000000000 | bytes 8388608 | tf_op jit(solution)/shard_map/vertical/pallas_call | solution.py:545
  18.4 0.8 %collective-permute-start.3 = (f32[576,128]{1,0:T(8,128)S(1)}, f32[576,128]{1,0:T(8,128)S(1)}, u32[]{:S(2)}, u32[]{:S(2)}) collective-permute-start(f32[576,128]{1,0:T(8,128)S(1)} %get-tuple-element.73), channel_id=1, source_target_pairs={{0,1},{1,0},{2,3},{3,2},{4,5},{5,4},{6,7},{7,6},{8,9},{9,8},{10,11... | collective-permute-start | bytes 884744 | tf_op jit(solution)/shard_map/ppermute | solution.py:521
  19.1 6.5 %collective-permute-start.4 = (f32[576,128]{1,0:T(8,128)S(1)}, f32[576,128]{1,0:T(8,128)S(1)}, u32[]{:S(2)}, u32[]{:S(2)}) collective-permute-start(f32[576,128]{1,0:T(8,128)S(1)} %get-tuple-element.74), channel_id=1, source_target_pairs={{0,0},{1,2},{2,1},{3,4},{4,3},{5,6},{6,5},{7,8},{8,7},{9,10},{10,9... | collective-permute-start | bytes 884744 | tf_op jit(solution)/shard_map/ppermute | solution.py:521
  25.7 2.0 %collective-permute-start.5 = (f32[40,128]{1,0:T(8,128)S(1)}, f32[40,128]{1,0:T(8,128)S(1)}, u32[]{:S(2)}, u32[]{:S(2)}) collective-permute-start(f32[40,128]{1,0:T(8,128)S(1)} %get-tuple-element.75), channel_id=1, source_target_pairs={{2,0},{3,1},{4,2},{5,3},{6,4},{7,5},{8,6},{9,7},{10,8},{11,9},{12,... | collective-permute-start | bytes 61448 | tf_op jit(solution)/shard_map/ppermute | solution.py:526
  27.6 1.6 %spread.2.own_ref = f32[15,144,256]{2,1,0:T(8,128)S(1)} custom-call(bf16[256,512]{1,0:T(8,128)(2,1)S(1)} %get-tuple-element.52.w0_ref, bf16[3,256,256]{2,1,0:T(8,128)(2,1)S(1)} %get-tuple-element.53.w_ref, bf16[3,256,256]{2,1,0:T(8,128)(2,1)S(1)} %get-tuple-element.54.ww_ref, f32[6,144,256]{2,1,0:T(8,128)S(1)} %get-tuple-element.59.y0c_ref, ...), custom_call_target="tpu_custom_call" | custom-call | flops 1000000000 | bytes 8388608 | tf_op jit(solution)/shard_map/spread/pallas_call | solution.py:549
  29.2 4.3 %collective-permute-done.5.far_ref = f32[40,128]{1,0:T(8,128)S(1)} collective-permute-done((f32[40,128]{1,0:T(8,128)S(1)}, f32[40,128]{1,0:T(8,128)S(1)}, u32[]{:S(2)}, u32[]{:S(2)}) %collective-permute-start.5) | collective-permute-done | bytes 20512 | tf_op jit(solution)/shard_map/ppermute | solution.py:526
  33.5 0.0 collective-permute-done.3.mate_ref
  33.5 0.0 collective-permute-done.4.side_ref
  33.5 4.0 %middle.1 = (bf16[26,144,256]{2,1,0:T(8,128)(2,1)S(1)}, bf16[26,144,256]{2,1,0:T(8,128)(2,1)S(1)}, f32[576,128]{1,0:T(8,128)S(1)}) custom-call(f32[80,128]{1,0:T(8,128)S(1)} %get-tuple-element.51.filt_ref, bf16[256,512]{1,0:T(8,128)(2,1)S(1)} %get-tuple-element.52.w0_ref, bf16[3,256,256]{2,1,0:T(8,128)(2,1)S(1)} %get-tuple-element.53.w_ref, ...), custom_call_target="tpu_custom_call" | custom-call | flops 1000000000 | bytes 8388608 | tf_op jit(solution)/shard_map/middle/pallas_call | solution.py:552
  37.5 3.5 %collective-permute-start.7 = (f32[576,128]{1,0:T(8,128)S(1)}, f32[576,128]{1,0:T(8,128)S(1)}, u32[]{:S(2)}, u32[]{:S(2)}) collective-permute-start(f32[576,128]{1,0:T(8,128)S(1)} %get-tuple-element.87), channel_id=1, source_target_pairs={{0,0},{1,2},{2,1},{3,4},{4,3},{5,6},{6,5},{7,8},{8,7},{9,10},{10,9... | collective-permute-start | bytes 884744 | tf_op jit(solution)/shard_map/ppermute | solution.py:521
  41.0 0.5 mate.3
  41.6 0.1 collective-permute-start.6
  41.7 5.5 %collective-permute-start.8 = (f32[40,128]{1,0:T(8,128)S(1)}, f32[40,128]{1,0:T(8,128)S(1)}, u32[]{:S(2)}, u32[]{:S(2)}) collective-permute-start(f32[40,128]{1,0:T(8,128)S(1)} %get-tuple-element.88), channel_id=1, source_target_pairs={{0,2},{1,3},{2,4},{3,5},{4,6},{5,7},{6,8},{7,9},{8,10},{9,11},{10,... | collective-permute-start | bytes 61448 | tf_op jit(solution)/shard_map/ppermute | solution.py:526
  47.2 1.7 %own.3 = (f32[2,144,256]{2,1,0:T(8,128)S(1)}, f32[144,256]{1,0:T(8,128)S(1)}, f32[144,128]{1,0:T(8,128)S(1)}, f32[144,256]{1,0:T(8,128)S(1)}, f32[144,128]{1,0:T...) custom-call(bf16[26,144,256]{2,1,0:T(8,128)(2,1)S(1)} %get-tuple-element.76.hi_ref, ...), custom_call_target="tpu_custom_call" | custom-call | flops 1000000000 | bytes 8388608 | tf_op jit(solution)/shard_map/own/pallas_call | solution.py:544
  48.9 0.0 collective-permute-done.8.far_ref
  48.9 0.0 collective-permute-done.7.side_ref
  48.9 0.0 collective-permute-done.6.mate_ref
  49.0 0.7 %vertical.3 = (f32[2,144,256]{2,1,0:T(8,128)S(1)}, f32[144,256]{1,0:T(8,128)S(1)}, f32[144,128]{1,0:T(8,128)S(1)}, f32[144,256]{1,0:T(8,128)S(1)}, f32[144,128]{...) custom-call(bf16[5,288,256]{2,1,0:T(8,128)(2,1)S(1)} %get-tuple-element.78.m_ref, ...), custom_call_target="tpu_custom_call" | custom-call | flops 1000000000 | bytes 8388608 | tf_op jit(solution)/shard_map/vertical/pallas_call | solution.py:545
  49.7 0.4 collective-permute-start.9
  50.1 6.9 %collective-permute-start.10 = (f32[576,128]{1,0:T(8,128)S(1)}, f32[576,128]{1,0:T(8,128)S(1)}, u32[]{:S(2)}, u32[]{:S(2)}) collective-permute-start(f32[576,128]{1,0:T(8,128)S(1)} %get-tuple-element.95), channel_id=1, source_target_pairs={{0,0},{1,2},{2,1},{3,4},{4,3},{5,6},{6,5},{7,8},{8,7},{9,10},{10,9... | collective-permute-start | bytes 884744 | tf_op jit(solution)/shard_map/ppermute | solution.py:521
  57.1 2.0 %collective-permute-start.11 = (f32[40,128]{1,0:T(8,128)S(1)}, f32[40,128]{1,0:T(8,128)S(1)}, u32[]{:S(2)}, u32[]{:S(2)}) collective-permute-start(f32[40,128]{1,0:T(8,128)S(1)} %get-tuple-element.96), channel_id=1, source_target_pairs={{2,0},{3,1},{4,2},{5,3},{6,4},{7,5},{8,6},{9,7},{10,8},{11,9},{12,... | collective-permute-start | bytes 61448 | tf_op jit(solution)/shard_map/ppermute | solution.py:526
  59.0 1.6 %spread.3.own_ref = f32[15,144,256]{2,1,0:T(8,128)S(1)} custom-call(bf16[256,512]{1,0:T(8,128)(2,1)S(1)} %get-tuple-element.52.w0_ref, bf16[3,256,256]{2,1,0:T(8,128)(2,1)S(1)} %get-tuple-element.53.w_ref, bf16[3,256,256]{2,1,0:T(8,128)(2,1)S(1)} %get-tuple-element.54.ww_ref, f32[6,144,256]{2,1,0:T(8,128)S(1)} %get-tuple-element.79.y0c_ref, ...), custom_call_target="tpu_custom_call" | custom-call | flops 1000000000 | bytes 8388608 | tf_op jit(solution)/shard_map/spread/pallas_call | solution.py:549
  60.6 4.4 %collective-permute-done.11.far_ref = f32[40,128]{1,0:T(8,128)S(1)} collective-permute-done((f32[40,128]{1,0:T(8,128)S(1)}, f32[40,128]{1,0:T(8,128)S(1)}, u32[]{:S(2)}, u32[]{:S(2)}) %collective-permute-start.11) | collective-permute-done | bytes 20512 | tf_op jit(solution)/shard_map/ppermute | solution.py:526
  65.0 0.0 collective-permute-done.9.mate_ref
  65.0 0.0 collective-permute-done.10.side_ref
  65.0 2.8 %last.1 = f32[2192,128]{1,0:T(8,128)} custom-call(f32[80,128]{1,0:T(8,128)S(1)} %get-tuple-element.51.filt_ref, bf16[256,512]{1,0:T(8,128)(2,1)S(1)} %get-tuple-element.52.w0_ref, bf16[3,256,256]{2,1,0:T(8,128)(2,1)S(1)} %get-tuple-element.53.w_ref, bf16[3,256,256]{2,1,0:T(8,128)(2,1)S(1)} %get-tuple-element.54.ww_ref, f32[15,144,256]{2,1,0:T(8,128)S(1)} %spread.3.own_ref, ...), custom_call_target="tpu_custom_call" | custom-call | flops 1000000000 | bytes 8388608 | tf_op jit(solution)/shard_map/last/pallas_call | solution.py:555
Async XLA Ops:
  0.0 1.3 %copy-start = (f32[137,16,128]{2,1,0:T(8,128)S(1)}, f32[137,16,128]{2,1,0:T(8,128)}, u32[]{:S(2)}) copy-start(f32[137,16,128]{2,1,0:T(8,128)} %param.3) | copy-start | bytes 3366916
  1.3 0.7 %copy-start.2 = (s32[4,2,2,5]{3,2,1,0:T(2,128)S(1)}, s32[4,2,2,5]{3,2,1,0:T(2,128)}, u32[]{:S(2)}) copy-start(s32[4,2,2,5]{3,2,1,0:T(2,128)} %taps_ref.1) | copy-start | bytes 964
  5.7 11.9 %collective-permute-start.1 = (f32[576,128]{1,0:T(8,128)S(1)}, f32[576,128]{1,0:T(8,128)S(1)}, u32[]{:S(2)}, u32[]{:S(2)}) collective-permute-start(f32[576,128]{1,0:T(8,128)S(1)} %get-tuple-element.57.after_ref), channel_id=1, source_target_pairs={{0,0},{1,2},{2,1},{3,4},{4,3},{5,6},{6,5},{7,8},{8,7},{9,10},{10,9... | collective-permute-start | bytes 884744 | tf_op jit(solution)/shard_map/ppermute | solution.py:521
  11.4 4.1 %copy-start.1 = (f32[5,137,137]{2,1,0:T(8,128)S(1)}, f32[5,137,137]{2,1,0:T(8,128)}, u32[]{:S(2)}) copy-start(f32[5,137,137]{2,1,0:T(8,128)} %m_ref.1) | copy-start | bytes 1126144
  11.9 5.7 %collective-permute-start = (f32[576,128]{1,0:T(8,128)S(1)}, f32[576,128]{1,0:T(8,128)S(1)}, u32[]{:S(2)}, u32[]{:S(2)}) collective-permute-start(f32[576,128]{1,0:T(8,128)S(1)} %get-tuple-element.66), channel_id=1, source_target_pairs={{0,1},{1,0},{2,3},{3,2},{4,5},{5,4},{6,7},{7,6},{8,9},{9,8},{10,11... | collective-permute-start | bytes 884744 | tf_op jit(solution)/shard_map/ppermute | solution.py:521
  12.1 5.5 %collective-permute-start.2 = (f32[40,128]{1,0:T(8,128)S(1)}, f32[40,128]{1,0:T(8,128)S(1)}, u32[]{:S(2)}, u32[]{:S(2)}) collective-permute-start(f32[40,128]{1,0:T(8,128)S(1)} %get-tuple-element.67), channel_id=1, source_target_pairs={{0,2},{1,3},{2,4},{3,5},{4,6},{5,7},{6,8},{7,9},{8,10},{9,11},{10,... | collective-permute-start | bytes 61448 | tf_op jit(solution)/shard_map/ppermute | solution.py:526
  18.4 15.2 %collective-permute-start.3 = (f32[576,128]{1,0:T(8,128)S(1)}, f32[576,128]{1,0:T(8,128)S(1)}, u32[]{:S(2)}, u32[]{:S(2)}) collective-permute-start(f32[576,128]{1,0:T(8,128)S(1)} %get-tuple-element.73), channel_id=1, source_target_pairs={{0,1},{1,0},{2,3},{3,2},{4,5},{5,4},{6,7},{7,6},{8,9},{9,8},{10,11... | collective-permute-start | bytes 884744 | tf_op jit(solution)/shard_map/ppermute | solution.py:521
  19.1 14.4 %collective-permute-start.4 = (f32[576,128]{1,0:T(8,128)S(1)}, f32[576,128]{1,0:T(8,128)S(1)}, u32[]{:S(2)}, u32[]{:S(2)}) collective-permute-start(f32[576,128]{1,0:T(8,128)S(1)} %get-tuple-element.74), channel_id=1, source_target_pairs={{0,0},{1,2},{2,1},{3,4},{4,3},{5,6},{6,5},{7,8},{8,7},{9,10},{10,9... | collective-permute-start | bytes 884744 | tf_op jit(solution)/shard_map/ppermute | solution.py:521
  25.7 7.9 %collective-permute-start.5 = (f32[40,128]{1,0:T(8,128)S(1)}, f32[40,128]{1,0:T(8,128)S(1)}, u32[]{:S(2)}, u32[]{:S(2)}) collective-permute-start(f32[40,128]{1,0:T(8,128)S(1)} %get-tuple-element.75), channel_id=1, source_target_pairs={{2,0},{3,1},{4,2},{5,3},{6,4},{7,5},{8,6},{9,7},{10,8},{11,9},{12,... | collective-permute-start | bytes 61448 | tf_op jit(solution)/shard_map/ppermute | solution.py:526
  37.5 11.4 %collective-permute-start.7 = (f32[576,128]{1,0:T(8,128)S(1)}, f32[576,128]{1,0:T(8,128)S(1)}, u32[]{:S(2)}, u32[]{:S(2)}) collective-permute-start(f32[576,128]{1,0:T(8,128)S(1)} %get-tuple-element.87), channel_id=1, source_target_pairs={{0,0},{1,2},{2,1},{3,4},{4,3},{5,6},{6,5},{7,8},{8,7},{9,10},{10,9... | collective-permute-start | bytes 884744 | tf_op jit(solution)/shard_map/ppermute | solution.py:521
  41.6 7.4 %collective-permute-start.6 = (f32[576,128]{1,0:T(8,128)S(1)}, f32[576,128]{1,0:T(8,128)S(1)}, u32[]{:S(2)}, u32[]{:S(2)}) collective-permute-start(f32[576,128]{1,0:T(8,128)S(1)} %get-tuple-element.86), channel_id=1, source_target_pairs={{0,1},{1,0},{2,3},{3,2},{4,5},{5,4},{6,7},{7,6},{8,9},{9,8},{10,11... | collective-permute-start | bytes 884744 | tf_op jit(solution)/shard_map/ppermute | solution.py:521
  41.7 7.2 %collective-permute-start.8 = (f32[40,128]{1,0:T(8,128)S(1)}, f32[40,128]{1,0:T(8,128)S(1)}, u32[]{:S(2)}, u32[]{:S(2)}) collective-permute-start(f32[40,128]{1,0:T(8,128)S(1)} %get-tuple-element.88), channel_id=1, source_target_pairs={{0,2},{1,3},{2,4},{3,5},{4,6},{5,7},{6,8},{7,9},{8,10},{9,11},{10,... | collective-permute-start | bytes 61448 | tf_op jit(solution)/shard_map/ppermute | solution.py:526
  49.7 15.3 %collective-permute-start.9 = (f32[576,128]{1,0:T(8,128)S(1)}, f32[576,128]{1,0:T(8,128)S(1)}, u32[]{:S(2)}, u32[]{:S(2)}) collective-permute-start(f32[576,128]{1,0:T(8,128)S(1)} %get-tuple-element.94), channel_id=1, source_target_pairs={{0,1},{1,0},{2,3},{3,2},{4,5},{5,4},{6,7},{7,6},{8,9},{9,8},{10,11... | collective-permute-start | bytes 884744 | tf_op jit(solution)/shard_map/ppermute | solution.py:521
  50.1 14.8 %collective-permute-start.10 = (f32[576,128]{1,0:T(8,128)S(1)}, f32[576,128]{1,0:T(8,128)S(1)}, u32[]{:S(2)}, u32[]{:S(2)}) collective-permute-start(f32[576,128]{1,0:T(8,128)S(1)} %get-tuple-element.95), channel_id=1, source_target_pairs={{0,0},{1,2},{2,1},{3,4},{4,3},{5,6},{6,5},{7,8},{8,7},{9,10},{10,9... | collective-permute-start | bytes 884744 | tf_op jit(solution)/shard_map/ppermute | solution.py:521
  57.1 7.9 %collective-permute-start.11 = (f32[40,128]{1,0:T(8,128)S(1)}, f32[40,128]{1,0:T(8,128)S(1)}, u32[]{:S(2)}, u32[]{:S(2)}) collective-permute-start(f32[40,128]{1,0:T(8,128)S(1)} %get-tuple-element.96), channel_id=1, source_target_pairs={{2,0},{3,1},{4,2},{5,3},{6,4},{7,5},{8,6},{9,7},{10,8},{11,9},{12,... | collective-permute-start | bytes 61448 | tf_op jit(solution)/shard_map/ppermute | solution.py:526

commit v2 on v1

--- a/solution.py
+++ b/solution.py
@@ -8,6 +8,7 @@
 from jax.experimental.pallas import tpu as pltpu
 from jax.sharding import PartitionSpec as P
 
+
 LEVELS = 4
 TAPS = 5
 ROOT_TWO = math.sqrt(2.0)
@@ -19,7 +20,6 @@
 OWN = (8, 4, 2, 1)
 FIRST = -1
 LAST = (8, 5, 3, 2)
-COUNT = (10, 7, 5, 4)
 BASE = (0, 10, 17, 22)
 SLOTS = 26
 LANES = 128
@@ -217,8 +217,7 @@
     )
 
 
-def unpack_coarse(ref):
-    values = ref[...]
+def unpack_coarse(values):
     parts = [values] + [pltpu.roll(values, LANES - 32 * q, 1) for q in (1, 2, 3)]
     return jnp.concatenate(parts[:3] + [parts[3][0:24]], axis=0)
 
@@ -227,9 +226,17 @@
     return lax.rem(lax.axis_index("lat"), 2) == 0
 
 
+AT = (0, PAD, 3 * PAD, 2 * PAD)
+COARSE = slice(4 * PAD, 4 * PAD + 40)
+
+
+def part(ref, t):
+    return ref[AT[t] : AT[t] + PAD, :]
+
+
 def put(ref, tiles):
     for t, tile in enumerate(tiles):
-        ref[t * PAD : t * PAD + PAD, :] = tile
+        ref[AT[t] : AT[t] + PAD, :] = tile
 
 
 def received(mate_ref, side_ref, n_below, n_above):
@@ -239,8 +246,7 @@
     no_above = place == lax.axis_size("lat") - 1
     below, above = [], []
     for t in range(max(n_below, n_above)):
-        mate = mate_ref[t * PAD : t * PAD + PAD, :]
-        side = side_ref[t * PAD : t * PAD + PAD, :]
+        mate, side = part(mate_ref, t), part(side_ref, t)
         if t < n_below:
             below.append(jnp.where(no_below, 0.0, jnp.where(even, side, mate)))
         if t < n_above:
@@ -308,30 +314,19 @@
 
 
 OWN_BASE = (0, 8, 12, 14)
-GOT = {(0, -1): 0, (0, 8): 1, (1, -1): 2, (1, 4): 3, (1, 5): 4, (2, -1): 5, (2, 2): 6, (2, 3): 7, (3, -1): 8, (3, 1): 9, (3, 2): 10}
-
-
-def spread_received(mate_ref, side_ref, far_ref, w0_ref, w_ref, ww_ref, got_ref):
-    below, above = received(mate_ref, side_ref, 3, 4)
-    below, above = unpack(below), unpack(above)
-    far = unpack_coarse(far_ref)
-    values = {(0, -1): below[0], (0, 8): above[0], (1, -1): below[1], (1, 4): above[1], (1, 5): above[4],
-              (2, -1): below[2], (2, 2): above[2], (2, 3): above[5], (3, -1): below[3], (3, 1): above[3], (3, 2): far}
-    for (level, index), v in values.items():
-        if level == 0:
-            got_ref[GOT[level, index]] = spread_level0(v, w0_ref)
-        else:
-            got_ref[GOT[level, index]] = spread_other(level, v, w_ref, ww_ref)
-
-
-def pick_at(own_ref, got_ref, at):
+GOT = {(0, -1): 0, (0, 8): 1, (1, -1): 2, (1, 4): 3, (1, 5): 4, (2, -1): 5, (2, 2): 6, (2, 3): 7, (3, -1): 8, (3, 1): 9}
+
+
+def pick_at(own_ref, got_ref, far_ref, at):
     table = {}
     for level in range(LEVELS):
         for index in range(FIRST, LAST[level] + 1):
             if 0 <= index < OWN[level]:
                 table[slot(level, index)] = (own_ref, OWN_BASE[level] + index)
+            elif (level, index) in GOT:
+                table[slot(level, index)] = (got_ref, GOT[level, index])
             else:
-                table[slot(level, index)] = (got_ref, GOT[level, index])
+                table[slot(level, index)] = (far_ref, 0)
 
     def pick(place):
         ref, i = table[place]
@@ -340,13 +335,13 @@
     return pick
 
 
-def first_kernel(taps_ref, x_hbm, filt_ref, w0_ref, w_ref, ww_ref, hi_ref, lo_ref, side_ref, x_ref, sem):
-    fetch = pltpu.make_async_copy(x_hbm, x_ref, sem)
-    fetch.start()
+def weights_kernel(taps_ref, filt_ref, w0_ref, w_ref, ww_ref):
     write_filters(taps_ref, filt_ref)
+    write_weights(filt_ref, w0_ref, w_ref, ww_ref)
+
+
+def first_kernel(filt_ref, x_ref, hi_ref, lo_ref):
     flags = edge_flags()
-    write_weights(filt_ref, w0_ref, w_ref, ww_ref)
-    fetch.wait()
 
     def chunk(c, carry):
         start = pl.multiple_of(c * (16 * ROWS), 16 * ROWS)
@@ -363,16 +358,26 @@
         tail = jnp.where(top, x_ref[136 * ROWS + r : 136 * ROWS + r + 1, :], 0.0)
         rows[r] = jnp.concatenate([head, tail], axis=0)
     store_split(hi_ref, lo_ref, latitude_analysis(rows, filt_ref, flags), slice(128, 144))
+
+
+def side_kernel(hi_ref, lo_ref, w0_ref, w_ref, side_ref, far_ref):
     put(side_ref, sums_message(hi_ref, lo_ref, w0_ref, w_ref, jnp.logical_not(is_even())))
-
-
-def mate_kernel(hi_ref, lo_ref, w0_ref, w_ref, mate_ref, far_ref):
-    put(mate_ref, sums_message(hi_ref, lo_ref, w0_ref, w_ref, is_even()))
     _, others = bands(hi_ref, lo_ref, w0_ref, w_ref)
-    far_ref[...] = pack_coarse(others(3, slot(3, 2)))
-
-
-def own_kernel(hi_ref, lo_ref, w0_ref, w_ref, m_ref, c0_ref, c1_ref, c1b_ref, c2_ref, c3_ref, y0_ref, y1_ref):
+    far = pack_coarse(others(3, slot(3, 2)))
+    far_ref[...] = far
+    side_ref[COARSE, :] = far
+
+
+def mate_kernel(hi_ref, lo_ref, w0_ref, w_ref, after_ref, mate_ref):
+    del after_ref
+    even = is_even()
+    tiles = sums_message(hi_ref, lo_ref, w0_ref, w_ref, even)
+    _, others = bands(hi_ref, lo_ref, w0_ref, w_ref)
+    tiles[3] = jnp.where(even, tiles[3], others(3, slot(3, 0)))
+    put(mate_ref, tiles)
+
+
+def own_kernel(hi_ref, lo_ref, w0_ref, w_ref, m_ref, c0_ref, c1_ref, c1b_ref, c2_ref, c3_ref, c3up_ref, y0_ref, y1_ref):
     level0, others = bands(hi_ref, lo_ref, w0_ref, w_ref)
     c0_ref[0] = level0(slot(0, 0))
     c0_ref[1] = level0(slot(0, 7))
@@ -382,19 +387,16 @@
     c2_ref[:, 0:128] = others(2, slot(2, 0))
     c2_ref[:, 128:256] = others(2, slot(2, 1))
     c3_ref[...] = others(3, slot(3, 0))
+    c3up_ref[...] = others(3, slot(3, 1))
     y1_ref[...] = apply_vertical(m_ref, 1, others(1, slot(1, 2)))
     for i in range(1, 7):
         y0_ref[i - 1] = apply_vertical(m_ref, 0, level0(slot(0, i)))
 
 
-def vertical_kernel(m_ref, c0_ref, c1_ref, c1b_ref, c2_ref, c3_ref, mate_ref, side_ref, far_ref,
-                    y0_ref, y1_ref, y1b_ref, y2_ref, y3_ref, mate_out_ref, side_out_ref, far_out_ref):
+def vertical_kernel(m_ref, c0_ref, c1_ref, c1b_ref, c2_ref, mate_ref, side_ref,
+                    y0_ref, y1_ref, y1b_ref, y2_ref, mate_out_ref, side_out_ref):
     below, above = received(mate_ref, side_ref, 4, 3)
     below, above = unpack(below), unpack(above)
-    far = unpack_coarse(far_ref)
-    c3 = c3_ref[...] + below[3] + above[3] + far
-    lane = lane_ids(PAD)
-    y3 = jnp.where(lane < 24, apply_vertical(m_ref, 3, c3), apply_vertical(m_ref, 4, c3))
     c2 = c2_ref[...]
     y2 = apply_vertical(m_ref, 2, jnp.concatenate([c2[:, 0:128] + below[2], c2[:, 128:256] + below[5] + above[2]], axis=1))
     c1 = c1_ref[...]
@@ -407,13 +409,37 @@
     y1_ref[...] = y1
     y1b_ref[...] = y1b
     y2_ref[...] = y2
-    y3_ref[...] = y3
-    far_out_ref[...] = pack_coarse(y3)
-    down = pack(first, y1[:, 0:128], y2[:, 0:128], y3, y1[:, 128:256], y2[:, 128:256])
-    up = pack(last, y1b, y2[:, 128:256], y3, y1[:, 128:256], y2[:, 128:256])
+    none = jnp.zeros((PAD, LANES), F32)
+    down = pack(first, y1[:, 0:128], y2[:, 0:128], none, y1[:, 128:256], y2[:, 128:256])
+    up = pack(last, y1b, y2[:, 128:256], none, y1[:, 128:256], y2[:, 128:256])
     even = is_even()
     put(side_out_ref, [jnp.where(even, d, u) for d, u in zip(down, up)])
     put(mate_out_ref, [jnp.where(even, u, d) for d, u in zip(down, up)])
+
+
+def coarse_kernel(m_ref, c3_ref, c3up_ref, far_ref, mate_ref, side_ref, passed_ref, mate_in_ref, side_in_ref,
+                  y3_ref, mate_out_ref, side_out_ref):
+    even = is_even()
+    place = lax.axis_index("lat")
+    last = lax.axis_size("lat") - 1
+    lane = lane_ids(PAD)
+    from_side = jnp.where((place == 0) | (place == last), 0.0, pltpu.roll(part(side_ref, 2), 32, 1))
+    passed = unpack_coarse(passed_ref[PAD : PAD + 40, :])
+    passed = jnp.where(even, unpack_coarse(far_ref[...]), jnp.where(place == 1, 0.0, passed))
+    mine = c3_ref[...] + pltpu.roll(part(mate_ref, 2), 32, 1) + from_side + passed
+    coarse = jnp.where(place == 0, 0.0, unpack_coarse(side_ref[COARSE, :]))
+    above = jnp.where(place == last - 1, 0.0, pltpu.roll(passed_ref[0:PAD, :], 32, 1))
+    other = part(mate_ref, 3) + c3up_ref[...] + coarse + above
+    both = jnp.concatenate([mine, other], axis=1)
+    detail, smooth = apply_vertical(m_ref, 3, both), apply_vertical(m_ref, 4, both)
+    y3 = jnp.where(lane < 24, detail[:, 0:128], smooth[:, 0:128])
+    y3_ref[...] = y3
+    moved = pltpu.roll(y3, 96, 1)
+    mate_out_ref[...] = mate_in_ref[...]
+    mate_out_ref[AT[2] : AT[2] + PAD, :] = jnp.where(lane < 96, part(mate_in_ref, 2), moved)
+    side_out_ref[0 : 4 * PAD, :] = side_in_ref[...]
+    side_out_ref[AT[2] : AT[2] + PAD, :] = jnp.where(lane < 96, part(side_in_ref, 2), moved)
+    side_out_ref[COARSE, :] = pack_coarse(jnp.where(lane < 24, detail[:, 128:256], smooth[:, 128:256]))
 
 
 def spread_kernel(w0_ref, w_ref, ww_ref, y0c_ref, y1c_ref, y0_ref, y1_ref, y1b_ref, y2_ref, y3_ref, own_ref):
@@ -427,32 +453,48 @@
     own_ref[14] = spread_other(3, y3_ref[...], w_ref, ww_ref)
 
 
-def middle_kernel(filt_ref, w0_ref, w_ref, ww_ref, own_ref, mate_ref, side_ref, far_ref, hi_ref, lo_ref, side_out_ref,
-                  got_ref):
+def received_kernel(w0_ref, w_ref, ww_ref, mate_ref, side_ref, got_ref):
+    below, above = received(mate_ref, side_ref, 3, 4)
+    below, above = unpack(below), unpack(above)
+    values = {(0, -1): below[0], (0, 8): above[0], (1, -1): below[1], (1, 4): above[1], (1, 5): above[4],
+              (2, -1): below[2], (2, 2): above[2], (2, 3): above[5], (3, -1): below[3], (3, 1): above[3]}
+    for (level, index), v in values.items():
+        if level == 0:
+            got_ref[GOT[level, index]] = spread_level0(v, w0_ref)
+        else:
+            got_ref[GOT[level, index]] = spread_other(level, v, w_ref, ww_ref)
+
+
+def spread_coarse(side_ref, passed_ref, w_ref, ww_ref, far_ref):
+    value = jnp.where(is_even(), pltpu.roll(passed_ref[...], 32, 1), unpack_coarse(side_ref[COARSE, :]))
+    value = jnp.where(lax.axis_index("lat") >= lax.axis_size("lat") - 2, 0.0, value)
+    far_ref[0] = spread_other(3, value, w_ref, ww_ref)
+
+
+def middle_kernel(filt_ref, w_ref, ww_ref, own_ref, got_ref, side_ref, passed_ref, hi_ref, lo_ref, far_ref):
     flags = edge_flags()
-    spread_received(mate_ref, side_ref, far_ref, w0_ref, w_ref, ww_ref, got_ref)
+    spread_coarse(side_ref, passed_ref, w_ref, ww_ref, far_ref)
 
     def chunk(c, carry):
         at = pl.ds(pl.multiple_of(c * 16, 16), 16)
-        rows = latitude_synthesis(pick_at(own_ref, got_ref, at), filt_ref, flags)
+        rows = latitude_synthesis(pick_at(own_ref, got_ref, far_ref, at), filt_ref, flags)
         store_split(hi_ref, lo_ref, latitude_analysis(rows, filt_ref, flags), at)
         return carry
 
     lax.fori_loop(0, 9, chunk, 0)
-    put(side_out_ref, sums_message(hi_ref, lo_ref, w0_ref, w_ref, jnp.logical_not(is_even())))
-
-
-def last_kernel(filt_ref, w0_ref, w_ref, ww_ref, own_ref, mate_ref, side_ref, far_ref, out_hbm, got_ref, out_ref, sems):
+
+
+def last_kernel(filt_ref, w_ref, ww_ref, own_ref, got_ref, side_ref, passed_ref, out_hbm, far_ref, out_ref, sems):
     flags = edge_flags()
-    spread_received(mate_ref, side_ref, far_ref, w0_ref, w_ref, ww_ref, got_ref)
+    spread_coarse(side_ref, passed_ref, w_ref, ww_ref, far_ref)
 
     def leave(c):
-        part = pl.ds(pl.multiple_of(c * (16 * ROWS), 16 * ROWS), 16 * ROWS)
-        return pltpu.make_async_copy(out_ref.at[part, :], out_hbm.at[part, :], sems.at[c])
+        piece = pl.ds(pl.multiple_of(c * (16 * ROWS), 16 * ROWS), 16 * ROWS)
+        return pltpu.make_async_copy(out_ref.at[piece, :], out_hbm.at[piece, :], sems.at[c])
 
     def chunk(c, carry):
         at = pl.ds(pl.multiple_of(c * 16, 16), 16)
-        rows = latitude_synthesis(pick_at(own_ref, got_ref, at), filt_ref, flags)
+        rows = latitude_synthesis(pick_at(own_ref, got_ref, far_ref, at), filt_ref, flags)
         start = pl.multiple_of(c * (16 * ROWS), 16 * ROWS)
         for r, values in rows.items():
             out_ref[pl.ds(start + r, 16, stride=ROWS), :] = values
@@ -460,7 +502,7 @@
         return carry
 
     lax.fori_loop(0, 8, chunk, 0)
-    rows = latitude_synthesis(pick_at(own_ref, got_ref, slice(128, 144)), filt_ref, flags)
+    rows = latitude_synthesis(pick_at(own_ref, got_ref, far_ref, slice(128, 144)), filt_ref, flags)
     for r, values in rows.items():
         out_ref[pl.ds(128 * ROWS + r, 8, stride=ROWS), :] = values[0:8]
         out_ref[136 * ROWS + r : 136 * ROWS + r + 1, :] = values[8:9]
@@ -491,16 +533,19 @@
 ANY = pl.BlockSpec(memory_space=pl.ANY)
 
 MESSAGE = ((4 * PAD, LANES), F32)
+SIDE = ((4 * PAD + 40, LANES), F32)
 FAR = ((40, LANES), F32)
 WEIGHTS = (((80, LANES), F32), ((256, 512), BF16), ((3, 256, 256), BF16), ((3, 256, 256), BF16))
 HALVES = (((SLOTS, PAD, 256), BF16),) * 2
-EDGES = (((2, PAD, 256), F32), ((PAD, 256), F32), ((PAD, LANES), F32), ((PAD, 256), F32), ((PAD, LANES), F32))
+EDGES = (((2, PAD, 256), F32), ((PAD, 256), F32), ((PAD, LANES), F32), ((PAD, 256), F32))
+COARSEST = ((PAD, LANES), F32)
 INNER = (((6, PAD, 256), F32), ((PAD, LANES), F32))
 OWN_WIDE = ((15, PAD, 256), F32)
-GOT_WIDE = pltpu.VMEM((11, PAD, 256), F32)
-
-
-def call(kernel, in_specs, outs, scratch, name, limit, out_spec=VMEM):
+GOT_WIDE = ((10, PAD, 256), F32)
+FAR_WIDE = pltpu.VMEM((1, PAD, 256), F32)
+
+
+def call(kernel, in_specs, outs, scratch, limit, out_spec=VMEM):
     return pl.pallas_call(
         kernel,
         out_shape=[jax.ShapeDtypeStruct(shape, dtype) for shape, dtype in outs],
@@ -509,7 +554,6 @@
         scratch_shapes=scratch,
         compiler_params=pltpu.CompilerParams(vmem_limit_bytes=limit * MIB),
         cost_estimate=pl.CostEstimate(flops=10**9, bytes_accessed=8 * MIB, transcendentals=0),
-        name=name,
     )
 
 
@@ -521,41 +565,49 @@
     return lax.ppermute(values, "lat", [(i, partner.get(i, i)) for i in range(count)])
 
 
-def shift(values, by):
+def pass_up(values):
     count = lax.axis_size("lat")
-    return lax.ppermute(values, "lat", [(i, i + by) for i in range(count) if 0 <= i + by < count])
+    return lax.ppermute(values, "lat", [(i, i + 2) for i in range(0, count - 2, 2)])
 
 
 def on_device(increment, filter_taps, band_roots):
     levels, rows, columns = increment.shape
     flat = increment.reshape(levels * rows, columns)
-    filt, w0, w, ww, hi, lo, side = call(
-        first_kernel, [SMEM, HBM], WEIGHTS + HALVES + (MESSAGE,),
-        [pltpu.VMEM((levels * rows, columns), F32), pltpu.SemaphoreType.DMA], "first", 16,
-    )(filter_taps, flat)
+    filt, w0, w, ww = call(weights_kernel, [SMEM], WEIGHTS, [], 12)(filter_taps)
+    hi, lo = call(first_kernel, [VMEM] * 2, HALVES, [], 12)(filt, flat)
     plain, turned = call(
-        prepare_kernel, [VMEM, ANY], (((5, 2 * PAD, 256), BF16),) * 2, [pltpu.VMEM((256, 256), F32)], "prepare", 12
-    )(band_roots, side)
-
-    def half(matrix, hi, lo, side):
-        side = swap(side, 1)
-        mate, far = call(mate_kernel, [VMEM] * 4, (MESSAGE, FAR), [], "mate", 12)(hi, lo, w0, w)
-        mate, far = swap(mate, 0), shift(far, 2)
-        *edges, y0c, y1c = call(own_kernel, [VMEM] * 5, EDGES + INNER, [], "own", 12)(hi, lo, w0, w, matrix)
-        *edges, mate, side, far = call(
-            vertical_kernel, [VMEM] * 9, EDGES + (MESSAGE, MESSAGE, FAR), [], "vertical", 12
-        )(matrix, *edges, mate, side, far)
-        side, mate, far = swap(side, 1), swap(mate, 0), shift(far, -2)
-        (own,) = call(spread_kernel, [VMEM] * 10, (OWN_WIDE,), [], "spread", 12)(w0, w, ww, y0c, y1c, *edges)
-        return filt, w0, w, ww, own, mate, side, far
-
-    hi, lo, side = call(middle_kernel, [VMEM] * 8, HALVES + (MESSAGE,), [GOT_WIDE], "middle", 16)(
-        *half(plain, hi, lo, side)
-    )
+        prepare_kernel, [VMEM, ANY], (((5, 2 * PAD, 256), BF16),) * 2, [pltpu.VMEM((256, 256), F32)], 12
+    )(band_roots, hi)
+
+    def half(matrix, hi, lo):
+        side, far = call(side_kernel, [VMEM] * 4, (SIDE, FAR), [], 12)(hi, lo, w0, w)
+        (mate,) = call(mate_kernel, [VMEM] * 4 + [ANY], (MESSAGE,), [], 12)(hi, lo, w0, w, side)
+        side, mate, far = swap(side, 1), swap(mate, 0), pass_up(far)
+        *edges, c3, c3up, y0c, y1c = call(
+            own_kernel, [VMEM] * 5, EDGES + (COARSEST, COARSEST) + INNER, [], 12
+        )(hi, lo, w0, w, matrix)
+        side, y1c = lax.optimization_barrier((side, y1c))
+        passed = swap(side[3 * PAD :], 0)
+        *edges, mate_out, side_out = call(
+            vertical_kernel, [VMEM] * 7, EDGES + (MESSAGE, MESSAGE), [], 12
+        )(matrix, *edges, mate, side)
+        y3, mate, side = call(coarse_kernel, [VMEM] * 9, (COARSEST, MESSAGE, SIDE), [], 12)(
+            matrix, c3, c3up, far, mate, side, passed, mate_out, side_out
+        )
+        side, mate = swap(side, 1), swap(mate, 0)
+        (own,) = call(spread_kernel, [VMEM] * 10, (OWN_WIDE,), [], 12)(w0, w, ww, y0c, y1c, *edges, y3)
+        side, own = lax.optimization_barrier((side, own))
+        passed = swap(side[3 * PAD : 4 * PAD], 0)
+        (got,) = call(received_kernel, [VMEM] * 5, (GOT_WIDE,), [], 12)(w0, w, ww, mate, side)
+        return filt, w, ww, own, got, side, passed
+
+    ready = half(plain, hi, lo)
+    hi, lo = call(middle_kernel, [VMEM] * 7, HALVES, [FAR_WIDE], 12)(*ready)
+    ready = half(turned, hi, lo)
     (out,) = call(
-        last_kernel, [VMEM] * 8, (((levels * rows, columns), F32),),
-        [GOT_WIDE, pltpu.VMEM((levels * rows, columns), F32), pltpu.SemaphoreType.DMA((9,))], "last", 16, HBM,
-    )(*half(turned, hi, lo, side))
+        last_kernel, [VMEM] * 7, (((levels * rows, columns), F32),),
+        [FAR_WIDE, pltpu.VMEM((levels * rows, columns), F32), pltpu.SemaphoreType.DMA((9,))], 12, HBM,
+    )(*ready)
     return out.reshape(levels, rows, columns)
 
 

time: 68.1 us -> 78.9 us (1.16)
  the two profiles are of different devices: /device:TPU:431 before, /device:TPU:1057 now
where the time goes in v2:
time: 78.9 us; the launch traced here: 78.6 us
  starting transfers between devices  50.7 us (64%)
  Pallas kernels  20.9 us (26%)
  waiting for transfers between devices  5.8 us (7%)
  local copies, waits for them, and re-layouts  0.83 us (1%)
    ppermute x12, starting transfers between devices, swap(): lax.ppermute(values, 'lat', [(i, partner.get(i, i)) for i in range(count)])  49.4 us
    ppermute x12, waiting for transfers between devices, swap(): lax.ppermute(values, 'lat', [(i, partner.get(i, i)) for i in range(count)])  5.79 us
    pallas_call x2, Pallas kernels, half(): call(own_kernel, [VMEM] * 5, EDGES + (COARSEST, COARSEST) + INNER, [], 12)  3.42 us
    pallas_call x2, Pallas kernels, half(): call(spread_kernel, [VMEM] * 10, (OWN_WIDE,), [], 12)  3.11 us
    pallas_call x1, Pallas kernels, on_device(): hi, lo = call(middle_kernel, [VMEM] * 7, HALVES, [FAR_WIDE], 12)(*ready)  2.58 us
    pallas_call x1, Pallas kernels, on_device(): call(last_kernel, [VMEM] * 7, (((levels * rows, columns), F32),), [FAR_WI...  2.1 us
    pallas_call x2, Pallas kernels, half(): call(received_kernel, [VMEM] * 5, (GOT_WIDE,), [], 12)  1.87 us
  transfers between devices with their start and end apart: 14, of which 2 were waited for; matrix products, arithmetic and copies ran while one was open for 0% of the time, Pallas kernels for 14%

profile of v2, /device:TPU:1057, one launch (start us, length us, event | category | flops | bytes accessed | tf_op | source)
XLA Modules:
  0.0 78.6 jit_solution(13595957222088508699)
XLA Ops:
  0.0 0.8 %copy-done.2 = s32[4,2,2,5]{3,2,1,0:T(2,128)S(1)} copy-done((s32[4,2,2,5]{3,2,1,0:T(2,128)S(1)}, s32[4,2,2,5]{3,2,1,0:T(2,128)}, u32[]{:S(2)}) %copy-start.2) | copy-done | bytes 344
  0.8 1.5 %shard_map.37 = (f32[80,128]{1,0:T(8,128)S(1)}, bf16[256,512]{1,0:T(8,128)(2,1)S(1)}, bf16[3,256,256]{2,1,0:T(8,128)(2,1)S(1)}, bf16[3,256,256]{2,1,0:T(8,128)(2,1)S(1)}) custom-call(s32[4,2,2,5]{3,2,1,0:T(2,128)S(1)} %copy-done.2), custom_call_target="tpu_custom_call" | custom-call | flops 1000000000 | bytes 8388608 | tf_op jit(solution)/shard_map/pallas_call | solution.py:576
  2.3 1.6 %shard_map.38 = (bf16[26,144,256]{2,1,0:T(8,128)(2,1)S(1)}, bf16[26,144,256]{2,1,0:T(8,128)(2,1)S(1)}) custom-call(f32[80,128]{1,0:T(8,128)S(1)} %get-tuple-element.61.filt_ref, f32[2192,128]{1,0:T(8,128)S(1)} %bitcast.2), custom_call_target="tpu_custom_call" | custom-call | flops 1000000000 | bytes 8388608 | tf_op jit(solution)/shard_map/pallas_call | solution.py:577
  3.9 0.5 shard_map.41
  4.4 0.0 copy-start.1
  4.4 3.9 %collective-permute-start.2 = (f32[616,128]{1,0:T(8,128)S(1)}, f32[616,128]{1,0:T(8,128)S(1)}, u32[]{:S(2)}, u32[]{:S(2)}) collective-permute-start(f32[616,128]{1,0:T(8,128)S(1)} %get-tuple-element.72.after_ref), channel_id=1, source_target_pairs={{0,0},{1,2},{2,1},{3,4},{4,3},{5,6},{6,5},{7,8},{8,7},{9,10},{10,9... | collective-permute-start | bytes 946184 | tf_op jit(solution)/shard_map/ppermute | solution.py:565
  8.4 0.5 shard_map.42
  8.9 0.3 collective-permute-start.1
  9.1 0.4 shard_map.39
  9.6 1.7 %shard_map.40 = (f32[2,144,256]{2,1,0:T(8,128)S(1)}, f32[144,256]{1,0:T(8,128)S(1)}, f32[144,128]{1,0:T(8,128)S(1)}, f32[144,256]{1,0:T(8,128)S(1)}, f32[144,128...) custom-call(bf16[26,144,256]{2,1,0:T(8,128)(2,1)S(1)} %get-tuple-element.64.after_ref, ...), custom_call_target="tpu_custom_call" | custom-call | flops 1000000000 | bytes 8388608 | tf_op jit(solution)/shard_map/pallas_call | solution.py:586
  11.3 2.0 %collective-permute-done.2.side_ref = f32[616,128]{1,0:T(8,128)S(1)} collective-permute-done((f32[616,128]{1,0:T(8,128)S(1)}, f32[616,128]{1,0:T(8,128)S(1)}, u32[]{:S(2)}, u32[]{:S(2)}) %collective-permute-start.2) | collective-permute-done | bytes 315424 | tf_op jit(solution)/shard_map/ppermute | solution.py:565
  13.3 3.7 %collective-permute-start.3 = (f32[184,128]{1,0:T(8,128)S(1)}, f32[184,128]{1,0:T(8,128)S(1)}, u32[]{:S(2)}, u32[]{:S(2)}) collective-permute-start(f32[184,128]{1,0:T(8,128)S(1)} %slice.12), channel_id=1, source_target_pairs={{0,1},{1,0},{2,3},{3,2},{4,5},{5,4},{6,7},{7,6},{8,9},{9,8},{10,11... | collective-permute-start | bytes 282632 | tf_op jit(solution)/shard_map/ppermute | solution.py:565
  16.9 0.7 collective-permute-start
  17.6 0.0 collective-permute-done.1.mate_ref
  17.6 0.6 shard_map.43
  18.2 0.0 collective-permute-done.far_ref
  18.2 0.0 collective-permute-done.3.passed_ref
  18.2 0.5 shard_map.44
  18.7 6.0 %collective-permute-start.4 = (f32[616,128]{1,0:T(8,128)S(1)}, f32[616,128]{1,0:T(8,128)S(1)}, u32[]{:S(2)}, u32[]{:S(2)}) collective-permute-start(f32[616,128]{1,0:T(8,128)S(1)} %get-tuple-element.81), channel_id=1, source_target_pairs={{0,0},{1,2},{2,1},{3,4},{4,3},{5,6},{6,5},{7,8},{8,7},{9,10},{10,9... | collective-permute-start | bytes 946184 | tf_op jit(solution)/shard_map/ppermute | solution.py:565
  24.7 3.8 %collective-permute-start.5 = (f32[576,128]{1,0:T(8,128)S(1)}, f32[576,128]{1,0:T(8,128)S(1)}, u32[]{:S(2)}, u32[]{:S(2)}) collective-permute-start(f32[576,128]{1,0:T(8,128)S(1)} %get-tuple-element.90), channel_id=1, source_target_pairs={{0,1},{1,0},{2,3},{3,2},{4,5},{5,4},{6,7},{7,6},{8,9},{9,8},{10,11... | collective-permute-start | bytes 884744 | tf_op jit(solution)/shard_map/ppermute | solution.py:565
  28.6 1.6 %shard_map.45.own_ref = f32[15,144,256]{2,1,0:T(8,128)S(1)} custom-call(bf16[256,512]{1,0:T(8,128)(2,1)S(1)} %get-tuple-element.68.w0_ref, bf16[3,256,256]{2,1,0:T(8,128)(2,1)S(1)} %get-tuple-element.62.w_ref, bf16[3,256,256]{2,1,0:T(8,128)(2,1)S(1)} %get-tuple-element.63.ww_ref, f32[6,144,256]{2,1,0:T(8,128)S(1)} %get-tuple-element.82.y0c_ref, ...), custom_call_target="tpu_custom_call" | custom-call | flops 1000000000 | bytes 8388608 | tf_op jit(solution)/shard_map/pallas_call | solution.py:598
  30.1 0.0 collective-permute-done.4.side_ref
  30.1 8.0 %collective-permute-start.6 = (f32[144,128]{1,0:T(8,128)S(1)}, f32[144,128]{1,0:T(8,128)S(1)}, u32[]{:S(2)}, u32[]{:S(2)}) collective-permute-start(f32[144,128]{1,0:T(8,128)S(1)} %slice.13), channel_id=1, source_target_pairs={{0,1},{1,0},{2,3},{3,2},{4,5},{5,4},{6,7},{7,6},{8,9},{9,8},{10,11... | collective-permute-start | bytes 221192 | tf_op jit(solution)/shard_map/ppermute | solution.py:565
  38.1 0.0 collective-permute-done.5.mate_ref
  38.1 0.9 %shard_map.46.got_ref = f32[10,144,256]{2,1,0:T(8,128)S(1)} custom-call(bf16[256,512]{1,0:T(8,128)(2,1)S(1)} %get-tuple-element.68.w0_ref, bf16[3,256,256]{2,1,0:T(8,128)(2,1)S(1)} %get-tuple-element.62.w_ref, bf16[3,256,256]{2,1,0:T(8,128)(2,1)S(1)} %get-tuple-element.63.ww_ref, f32[576,128]{1,0:T(8,128)S(1)} %collective-permute-done.5.mate_ref, ...), custom_call_target="tpu_custom_call" | custom-call | flops 1000000000 | bytes 8388608 | tf_op jit(solution)/shard_map/pallas_call | solution.py:601
  39.0 0.0 collective-permute-done.6.passed_ref
  39.0 2.6 %shard_map.47 = (bf16[26,144,256]{2,1,0:T(8,128)(2,1)S(1)}, bf16[26,144,256]{2,1,0:T(8,128)(2,1)S(1)}) custom-call(f32[80,128]{1,0:T(8,128)S(1)} %get-tuple-element.61.filt_ref, bf16[3,256,256]{2,1,0:T(8,128)(2,1)S(1)} %get-tuple-element.62.w_ref, bf16[3,256,256]{2,1,0:T(8,128)(2,1)S(1)} %get-tuple-element.63.ww_ref, f32[15,144,256]{2,1,0:T(8,128)S(1)} %shard_map.45.own_ref, ...), custom_call_target="tpu_custom_call" | custom-call | flops 1000000000 | bytes 8388608 | tf_op jit(solution)/shard_map/pallas_call | solution.py:605
  41.6 0.5 shard_map.49
  42.2 2.0 %collective-permute-start.9 = (f32[616,128]{1,0:T(8,128)S(1)}, f32[616,128]{1,0:T(8,128)S(1)}, u32[]{:S(2)}, u32[]{:S(2)}) collective-permute-start(f32[616,128]{1,0:T(8,128)S(1)} %get-tuple-element.97.after_ref), channel_id=1, source_target_pairs={{0,0},{1,2},{2,1},{3,4},{4,3},{5,6},{6,5},{7,8},{8,7},{9,10},{10,9... | collective-permute-start | bytes 946184 | tf_op jit(solution)/shard_map/ppermute | solution.py:565
  44.1 0.5 shard_map.50
  44.7 0.6 collective-permute-start.8
  45.3 1.7 %shard_map.48 = (f32[2,144,256]{2,1,0:T(8,128)S(1)}, f32[144,256]{1,0:T(8,128)S(1)}, f32[144,128]{1,0:T(8,128)S(1)}, f32[144,256]{1,0:T(8,128)S(1)}, f32[144,128...) custom-call(bf16[26,144,256]{2,1,0:T(8,128)(2,1)S(1)} %get-tuple-element.92.hi_ref, ...), custom_call_target="tpu_custom_call" | custom-call | flops 1000000000 | bytes 8388608 | tf_op jit(solution)/shard_map/pallas_call | solution.py:586
  47.0 3.8 %collective-permute-done.9.side_ref = f32[616,128]{1,0:T(8,128)S(1)} collective-permute-done((f32[616,128]{1,0:T(8,128)S(1)}, f32[616,128]{1,0:T(8,128)S(1)}, u32[]{:S(2)}, u32[]{:S(2)}) %collective-permute-start.9) | collective-permute-done | bytes 315424 | tf_op jit(solution)/shard_map/ppermute | solution.py:565
  50.8 3.5 %collective-permute-start.10 = (f32[184,128]{1,0:T(8,128)S(1)}, f32[184,128]{1,0:T(8,128)S(1)}, u32[]{:S(2)}, u32[]{:S(2)}) collective-permute-start(f32[184,128]{1,0:T(8,128)S(1)} %slice.14), channel_id=1, source_target_pairs={{0,1},{1,0},{2,3},{3,2},{4,5},{5,4},{6,7},{7,6},{8,9},{9,8},{10,11... | collective-permute-start | bytes 282632 | tf_op jit(solution)/shard_map/ppermute | solution.py:565
  54.2 0.7 collective-permute-start.7
  54.9 0.0 collective-permute-done.8.mate_ref
  54.9 0.6 shard_map.51
  55.5 0.0 collective-permute-done.7.far_ref
  55.5 0.0 collective-permute-done.10.passed_ref
  55.6 0.5 shard_map.52
  56.1 6.0 %collective-permute-start.11 = (f32[616,128]{1,0:T(8,128)S(1)}, f32[616,128]{1,0:T(8,128)S(1)}, u32[]{:S(2)}, u32[]{:S(2)}) collective-permute-start(f32[616,128]{1,0:T(8,128)S(1)} %get-tuple-element.106), channel_id=1, source_target_pairs={{0,0},{1,2},{2,1},{3,4},{4,3},{5,6},{6,5},{7,8},{8,7},{9,10},{10,9... | collective-permute-start | bytes 946184 | tf_op jit(solution)/shard_map/ppermute | solution.py:565
  62.0 3.8 %collective-permute-start.12 = (f32[576,128]{1,0:T(8,128)S(1)}, f32[576,128]{1,0:T(8,128)S(1)}, u32[]{:S(2)}, u32[]{:S(2)}) collective-permute-start(f32[576,128]{1,0:T(8,128)S(1)} %get-tuple-element.115), channel_id=1, source_target_pairs={{0,1},{1,0},{2,3},{3,2},{4,5},{5,4},{6,7},{7,6},{8,9},{9,8},{10,11... | collective-permute-start | bytes 884744 | tf_op jit(solution)/shard_map/ppermute | solution.py:565
  65.9 1.6 %shard_map.53.own_ref = f32[15,144,256]{2,1,0:T(8,128)S(1)} custom-call(bf16[256,512]{1,0:T(8,128)(2,1)S(1)} %get-tuple-element.68.w0_ref, bf16[3,256,256]{2,1,0:T(8,128)(2,1)S(1)} %get-tuple-element.62.w_ref, bf16[3,256,256]{2,1,0:T(8,128)(2,1)S(1)} %get-tuple-element.63.ww_ref, f32[6,144,256]{2,1,0:T(8,128)S(1)} %get-tuple-element.107.y0c_ref, ...), custom_call_target="tpu_custom_call" | custom-call | flops 1000000000 | bytes 8388608 | tf_op jit(solution)/shard_map/pallas_call | solution.py:598
  67.4 0.0 collective-permute-done.11.side_ref
  67.4 8.0 %collective-permute-start.13 = (f32[144,128]{1,0:T(8,128)S(1)}, f32[144,128]{1,0:T(8,128)S(1)}, u32[]{:S(2)}, u32[]{:S(2)}) collective-permute-start(f32[144,128]{1,0:T(8,128)S(1)} %slice.15), channel_id=1, source_target_pairs={{0,1},{1,0},{2,3},{3,2},{4,5},{5,4},{6,7},{7,6},{8,9},{9,8},{10,11... | collective-permute-start | bytes 221192 | tf_op jit(solution)/shard_map/ppermute | solution.py:565
  75.4 0.9 %shard_map.54.got_ref = f32[10,144,256]{2,1,0:T(8,128)S(1)} custom-call(bf16[256,512]{1,0:T(8,128)(2,1)S(1)} %get-tuple-element.68.w0_ref, bf16[3,256,256]{2,1,0:T(8,128)(2,1)S(1)} %get-tuple-element.62.w_ref, bf16[3,256,256]{2,1,0:T(8,128)(2,1)S(1)} %get-tuple-element.63.ww_ref, f32[576,128]{1,0:T(8,128)S(1)} %collective-permute-done.12.mate_ref, ...), custom_call_target="tpu_custom_call" | custom-call | flops 1000000000 | bytes 8388608 | tf_op jit(solution)/shard_map/pallas_call | solution.py:601
  76.3 0.0 collective-permute-done.13.passed_ref
  76.4 2.1 %shard_map.55 = f32[2192,128]{1,0:T(8,128)} custom-call(f32[80,128]{1,0:T(8,128)S(1)} %get-tuple-element.61.filt_ref, bf16[3,256,256]{2,1,0:T(8,128)(2,1)S(1)} %get-tuple-element.62.w_ref, bf16[3,256,256]{2,1,0:T(8,128)(2,1)S(1)} %get-tuple-element.63.ww_ref, f32[15,144,256]{2,1,0:T(8,128)S(1)} %shard_map.53.own_ref, f32[10,144,256]{2,1,0:T(8,128)S(1)} %shard_map.54.got_ref, ...), custom_call_target="tpu_custom_call" | custom-call | flops 1000000000 | bytes 8388608 | tf_op jit(solution)/shard_map/pallas_call | solution.py:607
  (9 shorter events, 0.0 us)
Async XLA Ops:
  0.0 2.3 %copy-start = (f32[137,16,128]{2,1,0:T(8,128)S(1)}, f32[137,16,128]{2,1,0:T(8,128)}, u32[]{:S(2)}) copy-start(f32[137,16,128]{2,1,0:T(8,128)} %param.3) | copy-start | bytes 3366916
  0.0 0.8 %copy-start.2 = (s32[4,2,2,5]{3,2,1,0:T(2,128)S(1)}, s32[4,2,2,5]{3,2,1,0:T(2,128)}, u32[]{:S(2)}) copy-start(s32[4,2,2,5]{3,2,1,0:T(2,128)} %taps_ref.1) | copy-start | bytes 964
  4.4 4.7 %copy-start.1 = (f32[5,137,137]{2,1,0:T(8,128)S(1)}, f32[5,137,137]{2,1,0:T(8,128)}, u32[]{:S(2)}) copy-start(f32[5,137,137]{2,1,0:T(8,128)} %m_ref.1) | copy-start | bytes 1126144
  4.4 8.8 %collective-permute-start.2 = (f32[616,128]{1,0:T(8,128)S(1)}, f32[616,128]{1,0:T(8,128)S(1)}, u32[]{:S(2)}, u32[]{:S(2)}) collective-permute-start(f32[616,128]{1,0:T(8,128)S(1)} %get-tuple-element.72.after_ref), channel_id=1, source_target_pairs={{0,0},{1,2},{2,1},{3,4},{4,3},{5,6},{6,5},{7,8},{8,7},{9,10},{10,9... | collective-permute-start | bytes 946184 | tf_op jit(solution)/shard_map/ppermute | solution.py:565
  8.9 8.7 %collective-permute-start.1 = (f32[576,128]{1,0:T(8,128)S(1)}, f32[576,128]{1,0:T(8,128)S(1)}, u32[]{:S(2)}, u32[]{:S(2)}) collective-permute-start(f32[576,128]{1,0:T(8,128)S(1)} %shard_map.42), channel_id=1, source_target_pairs={{0,1},{1,0},{2,3},{3,2},{4,5},{5,4},{6,7},{7,6},{8,9},{9,8},{10,11... | collective-permute-start | bytes 884744 | tf_op jit(solution)/shard_map/ppermute | solution.py:565
  13.3 5.0 %collective-permute-start.3 = (f32[184,128]{1,0:T(8,128)S(1)}, f32[184,128]{1,0:T(8,128)S(1)}, u32[]{:S(2)}, u32[]{:S(2)}) collective-permute-start(f32[184,128]{1,0:T(8,128)S(1)} %slice.12), channel_id=1, source_target_pairs={{0,1},{1,0},{2,3},{3,2},{4,5},{5,4},{6,7},{7,6},{8,9},{9,8},{10,11... | collective-permute-start | bytes 282632 | tf_op jit(solution)/shard_map/ppermute | solution.py:565
  16.9 1.3 %collective-permute-start = (f32[40,128]{1,0:T(8,128)S(1)}, f32[40,128]{1,0:T(8,128)S(1)}, u32[]{:S(2)}, u32[]{:S(2)}) collective-permute-start(f32[40,128]{1,0:T(8,128)S(1)} %get-tuple-element.71), channel_id=1, source_target_pairs={{0,2},{2,4},{4,6},{6,8},{8,10},{10,12},{12,14},{14,16},{16,18},{18... | collective-permute-start | bytes 61448 | tf_op jit(solution)/shard_map/ppermute | solution.py:570
  18.7 11.4 %collective-permute-start.4 = (f32[616,128]{1,0:T(8,128)S(1)}, f32[616,128]{1,0:T(8,128)S(1)}, u32[]{:S(2)}, u32[]{:S(2)}) collective-permute-start(f32[616,128]{1,0:T(8,128)S(1)} %get-tuple-element.81), channel_id=1, source_target_pairs={{0,0},{1,2},{2,1},{3,4},{4,3},{5,6},{6,5},{7,8},{8,7},{9,10},{10,9... | collective-permute-start | bytes 946184 | tf_op jit(solution)/shard_map/ppermute | solution.py:565
  24.7 13.4 %collective-permute-start.5 = (f32[576,128]{1,0:T(8,128)S(1)}, f32[576,128]{1,0:T(8,128)S(1)}, u32[]{:S(2)}, u32[]{:S(2)}) collective-permute-start(f32[576,128]{1,0:T(8,128)S(1)} %get-tuple-element.90), channel_id=1, source_target_pairs={{0,1},{1,0},{2,3},{3,2},{4,5},{5,4},{6,7},{7,6},{8,9},{9,8},{10,11... | collective-permute-start | bytes 884744 | tf_op jit(solution)/shard_map/ppermute | solution.py:565
  30.1 8.9 %collective-permute-start.6 = (f32[144,128]{1,0:T(8,128)S(1)}, f32[144,128]{1,0:T(8,128)S(1)}, u32[]{:S(2)}, u32[]{:S(2)}) collective-permute-start(f32[144,128]{1,0:T(8,128)S(1)} %slice.13), channel_id=1, source_target_pairs={{0,1},{1,0},{2,3},{3,2},{4,5},{5,4},{6,7},{7,6},{8,9},{9,8},{10,11... | collective-permute-start | bytes 221192 | tf_op jit(solution)/shard_map/ppermute | solution.py:565
  42.2 8.6 %collective-permute-start.9 = (f32[616,128]{1,0:T(8,128)S(1)}, f32[616,128]{1,0:T(8,128)S(1)}, u32[]{:S(2)}, u32[]{:S(2)}) collective-permute-start(f32[616,128]{1,0:T(8,128)S(1)} %get-tuple-element.97.after_ref), channel_id=1, source_target_pairs={{0,0},{1,2},{2,1},{3,4},{4,3},{5,6},{6,5},{7,8},{8,7},{9,10},{10,9... | collective-permute-start | bytes 946184 | tf_op jit(solution)/shard_map/ppermute | solution.py:565
  44.7 10.2 %collective-permute-start.8 = (f32[576,128]{1,0:T(8,128)S(1)}, f32[576,128]{1,0:T(8,128)S(1)}, u32[]{:S(2)}, u32[]{:S(2)}) collective-permute-start(f32[576,128]{1,0:T(8,128)S(1)} %shard_map.50), channel_id=1, source_target_pairs={{0,1},{1,0},{2,3},{3,2},{4,5},{5,4},{6,7},{7,6},{8,9},{9,8},{10,11... | collective-permute-start | bytes 884744 | tf_op jit(solution)/shard_map/ppermute | solution.py:565
  50.8 4.8 %collective-permute-start.10 = (f32[184,128]{1,0:T(8,128)S(1)}, f32[184,128]{1,0:T(8,128)S(1)}, u32[]{:S(2)}, u32[]{:S(2)}) collective-permute-start(f32[184,128]{1,0:T(8,128)S(1)} %slice.14), channel_id=1, source_target_pairs={{0,1},{1,0},{2,3},{3,2},{4,5},{5,4},{6,7},{7,6},{8,9},{9,8},{10,11... | collective-permute-start | bytes 282632 | tf_op jit(solution)/shard_map/ppermute | solution.py:565
  54.2 1.3 %collective-permute-start.7 = (f32[40,128]{1,0:T(8,128)S(1)}, f32[40,128]{1,0:T(8,128)S(1)}, u32[]{:S(2)}, u32[]{:S(2)}) collective-permute-start(f32[40,128]{1,0:T(8,128)S(1)} %get-tuple-element.96), channel_id=1, source_target_pairs={{0,2},{2,4},{4,6},{6,8},{8,10},{10,12},{12,14},{14,16},{16,18},{18... | collective-permute-start | bytes 61448 | tf_op jit(solution)/shard_map/ppermute | solution.py:570
  56.1 11.4 %collective-permute-start.11 = (f32[616,128]{1,0:T(8,128)S(1)}, f32[616,128]{1,0:T(8,128)S(1)}, u32[]{:S(2)}, u32[]{:S(2)}) collective-permute-start(f32[616,128]{1,0:T(8,128)S(1)} %get-tuple-element.106), channel_id=1, source_target_pairs={{0,0},{1,2},{2,1},{3,4},{4,3},{5,6},{6,5},{7,8},{8,7},{9,10},{10,9... | collective-permute-start | bytes 946184 | tf_op jit(solution)/shard_map/ppermute | solution.py:565
  62.0 13.4 %collective-permute-start.12 = (f32[576,128]{1,0:T(8,128)S(1)}, f32[576,128]{1,0:T(8,128)S(1)}, u32[]{:S(2)}, u32[]{:S(2)}) collective-permute-start(f32[576,128]{1,0:T(8,128)S(1)} %get-tuple-element.115), channel_id=1, source_target_pairs={{0,1},{1,0},{2,3},{3,2},{4,5},{5,4},{6,7},{7,6},{8,9},{9,8},{10,11... | collective-permute-start | bytes 884744 | tf_op jit(solution)/shard_map/ppermute | solution.py:565
  67.4 8.9 %collective-permute-start.13 = (f32[144,128]{1,0:T(8,128)S(1)}, f32[144,128]{1,0:T(8,128)S(1)}, u32[]{:S(2)}, u32[]{:S(2)}) collective-permute-start(f32[144,128]{1,0:T(8,128)S(1)} %slice.15), channel_id=1, source_target_pairs={{0,1},{1,0},{2,3},{3,2},{4,5},{5,4},{6,7},{7,6},{8,9},{9,8},{10,11... | collective-permute-start | bytes 221192 | tf_op jit(solution)/shard_map/ppermute | solution.py:565

commit v3 on v2

--- a/solution.py
+++ b/solution.py
@@ -68,10 +68,16 @@
     return [filt_ref[row + k : row + k + 1, :] for k in range(TAPS)]
 
 
+def product(a, b):
+    a_high, a_low = split(a)
+    b_high, b_low = split(b)
+    return dot(a_high, b_high) + dot(a_low, b_high) + dot(a_high, b_low)
+
+
 def write_weights(filt_ref, w0_ref, w_ref, ww_ref):
     row = lax.broadcasted_iota(jnp.int32, (LANES, LANES), 0)
     lane = lax.broadcasted_iota(jnp.int32, (LANES, LANES), 1)
-    composed = None
+    steps = []
     for level in range(LEVELS):
         half = (LANES // 2) >> level
         low = coeffs(filt_ref, level, 1, 0)
@@ -81,16 +87,14 @@
         inside = (lane < 2 * half) & (row < 2 * half)
         step = jnp.zeros((LANES, LANES), F32)
         for k in range(TAPS):
-            chosen = jnp.where(is_low, low[k], high[k])
-            step = jnp.where(inside & (tap == k), chosen, step)
-        if composed is None:
-            composed = step
-        else:
-            composed = lax.dot_general(
-                composed, step, (((1,), (0,)), ((), ())),
-                precision=lax.Precision.HIGHEST, preferred_element_type=F32,
-            )
-        zeros = jnp.zeros((LANES, LANES), BF16)
+            chosen = jnp.where(is_low[0:1], low[k], high[k])
+            step = jnp.where(tap == k, chosen, step)
+        steps.append(jnp.where(inside, step, 0.0))
+    second = product(steps[0], steps[1])
+    composed_steps = [steps[0], second, product(second, steps[2]), product(second, product(steps[2], steps[3]))]
+    zeros = jnp.zeros((LANES, LANES), BF16)
+    for level, composed in enumerate(composed_steps):
+        half = (LANES // 2) >> level
         if level == 0:
             d_high, d_low = split(composed)
             moved = jnp.where(lane < half, pltpu.roll(composed, LANES - half, 1), 0.0)
@@ -109,8 +113,8 @@
                 moved = moved + jnp.where(
                     (lane >= 3 * half) & (lane < 4 * half), pltpu.roll(composed, 3 * half, 1), 0.0
                 )
-            for part, values in ((0, moved), (1, composed)):
-                rows = slice(part * LANES, part * LANES + LANES)
+            for which, values in ((0, moved), (1, composed)):
+                rows = slice(which * LANES, which * LANES + LANES)
                 v_high, v_low = split(values)
                 w_ref[level - 1, rows, 0:128] = v_high
                 w_ref[level - 1, rows, 128:256] = v_low
@@ -180,14 +184,26 @@
     return rows
 
 
-def pack(c0, c1, c2, c3, c1b, c2b):
+def pack(c0, c1, c2, c3, c1b, c2b, c3b=None):
     lane = lane_ids(PAD)
+    last = jnp.where(lane < 64, c1b, pltpu.roll(c2b, 96, 1))
+    if c3b is not None:
+        last = with_far(last, c3b)
     return [
         c0[:, 0:128],
         jnp.where(lane < 64, c0[:, 128:256], jnp.where(lane < 112, pltpu.roll(c2, 64, 1), pltpu.roll(c2b, 80, 1))),
         jnp.where(lane < 96, c1, pltpu.roll(c3, 96, 1)),
-        jnp.where(lane < 96, c1b, pltpu.roll(c2b, 96, 1)),
+        last,
     ]
+
+
+def with_far(tile, c3b):
+    lane = lane_ids(PAD)
+    return jnp.where((lane >= 64) & (lane < 96), pltpu.roll(c3b, 64, 1), tile)
+
+
+def far_of(tile):
+    return pltpu.roll(tile, 64, 1)
 
 
 def unpack(tiles):
@@ -201,6 +217,21 @@
         lane = lane_ids(PAD)
         parts += [tiles[3], jnp.where(lane < 32, pltpu.roll(tiles[3], 32, 1), pltpu.roll(tiles[1], 48, 1))]
     return parts
+
+
+def three_bands(tile, filt_ref):
+    low, high = coeffs(filt_ref, 1, 0, 0)[0], coeffs(filt_ref, 1, 0, 1)[0]
+    return jnp.where(lane_ids(PAD) < 64, high * tile, pltpu.roll(low * tile, 32, 1))
+
+
+def two_sums(values, filt_ref):
+    ratio = coeffs(filt_ref, 1, 0, 1)[0] / coeffs(filt_ref, 1, 0, 0)[0]
+    return jnp.where(lane_ids(PAD) < 32, values, pltpu.roll(values, 96, 1) + ratio * values)
+
+
+def bands_of_sums(tile):
+    lane = lane_ids(PAD)
+    return jnp.where(lane < 32, tile, jnp.where(lane < 64, 0.0, pltpu.roll(tile, 32, 1)))
 
 
 def pack_coarse(c3):
@@ -226,17 +257,33 @@
     return lax.rem(lax.axis_index("lat"), 2) == 0
 
 
-AT = (0, PAD, 3 * PAD, 2 * PAD)
-COARSE = slice(4 * PAD, 4 * PAD + 40)
-
-
-def part(ref, t):
-    return ref[AT[t] : AT[t] + PAD, :]
+MAIN = 136
+ORDERED = (0, 1, 3, 2)
+ENDS = 4 * MAIN
+TAIL = 2 * MAIN
+END_TILE = 3 * MAIN
+
+
+def join(main, end):
+    top = lax.broadcasted_iota(jnp.int32, (8, LANES), 0) == 0
+    return jnp.concatenate([main, jnp.where(top, end, 0.0)], axis=0)
+
+
+def part(ref, t, start=0):
+    at = ORDERED[t] * MAIN - start
+    end = ENDS + t - start
+    return join(ref[at : at + MAIN, :], ref[end : end + 1, :])
+
+
+def put_one(ref, t, tile):
+    ref[ORDERED[t] * MAIN : ORDERED[t] * MAIN + MAIN, :] = tile[0:MAIN]
+    ref[ENDS + t : ENDS + t + 1, :] = tile[MAIN : MAIN + 1]
 
 
 def put(ref, tiles):
+    ref[ENDS : ENDS + 8, :] = jnp.zeros((8, LANES), F32)
     for t, tile in enumerate(tiles):
-        ref[AT[t] : AT[t] + PAD, :] = tile
+        put_one(ref, t, tile)
 
 
 def received(mate_ref, side_ref, n_below, n_above):
@@ -263,33 +310,40 @@
             lo_ref[place, at, lanes] = low
 
 
+def stack(parts):
+    return jnp.concatenate(parts, axis=0)
+
+
 def bands(hi_ref, lo_ref, w0_ref, w_ref):
-    def level0(s):
+    def level0(*slots):
         w_high, w_low = w0_ref[:, 0:256], w0_ref[:, 256:512]
-        high = hi_ref[s]
-        return dot(high, w_high) + dot(high, w_low) + dot(lo_ref[s], w_high)
-
-    def others(level, s):
-        both = dot(hi_ref[s], w_ref[level - 1])
-        return both[:, 0:128] + both[:, 128:256] + dot(lo_ref[s], w_ref[level - 1, :, 0:128])
+        high, low = stack([hi_ref[s] for s in slots]), stack([lo_ref[s] for s in slots])
+        out = dot(high, w_high) + dot(high, w_low) + dot(low, w_high)
+        return [out[i * PAD : i * PAD + PAD] for i in range(len(slots))]
+
+    def others(level, *slots):
+        high, low = stack([hi_ref[s] for s in slots]), stack([lo_ref[s] for s in slots])
+        both = dot(high, w_ref[level - 1])
+        out = both[:, 0:128] + both[:, 128:256] + dot(low, w_ref[level - 1, :, 0:128])
+        return [out[i * PAD : i * PAD + PAD] for i in range(len(slots))]
 
     return level0, others
 
 
-def sums_message(hi_ref, lo_ref, w0_ref, w_ref, upward):
+def sums_message(hi_ref, lo_ref, w0_ref, w_ref, upward, extra):
     level0, others = bands(hi_ref, lo_ref, w0_ref, w_ref)
 
     def chosen(level, up_index):
         return jnp.where(upward, slot(level, up_index), slot(level, -1))
 
-    return pack(
-        level0(chosen(0, 8)),
-        others(1, chosen(1, 4)),
-        others(2, chosen(2, 2)),
-        others(3, chosen(3, 1)),
-        others(1, slot(1, 5)),
-        others(2, slot(2, 3)),
-    )
+    (c0,) = level0(chosen(0, 8))
+    (c1,) = others(1, chosen(1, 4))
+    row = slot(0, 8)
+    both = dot(hi_ref[row, :, 0:128], w_ref[0, 128:256, :])
+    c1b = both[:, 0:128] + both[:, 128:256] + dot(lo_ref[row, :, 0:128], w_ref[0, 128:256, 0:128])
+    c2, c2b = others(2, chosen(2, 2), slot(2, 3))
+    c3, more = others(3, chosen(3, 1), slot(3, extra))
+    return pack(c0, c1, c2, c3, c1b, c2b, more), more
 
 
 def apply_vertical(m_ref, band, values):
@@ -302,15 +356,17 @@
 
 
 def spread_level0(values, w0_ref):
-    high, low = split(values)
+    high, low = split(stack(values))
     w_high, w_low = w0_ref[:, 0:256], w0_ref[:, 256:512]
-    return dot_t(high, w_high) + dot_t(low, w_high) + dot_t(high, w_low)
+    out = dot_t(high, w_high) + dot_t(low, w_high) + dot_t(high, w_low)
+    return [out[i * PAD : i * PAD + PAD] for i in range(len(values))]
 
 
 def spread_other(level, values, w_ref, ww_ref):
-    high, low = split(values)
+    high, low = split(stack(values))
     pair = jnp.concatenate([high, low], axis=1)
-    return dot_t(pair, ww_ref[level - 1]) + dot_t(high, w_ref[level - 1, :, 128:256])
+    out = dot_t(pair, ww_ref[level - 1]) + dot_t(high, w_ref[level - 1, :, 128:256])
+    return [out[i * PAD : i * PAD + PAD] for i in range(len(values))]
 
 
 OWN_BASE = (0, 8, 12, 14)
@@ -361,46 +417,41 @@
 
 
 def side_kernel(hi_ref, lo_ref, w0_ref, w_ref, side_ref, far_ref):
-    put(side_ref, sums_message(hi_ref, lo_ref, w0_ref, w_ref, jnp.logical_not(is_even())))
-    _, others = bands(hi_ref, lo_ref, w0_ref, w_ref)
-    far = pack_coarse(others(3, slot(3, 2)))
-    far_ref[...] = far
-    side_ref[COARSE, :] = far
+    tiles, share = sums_message(hi_ref, lo_ref, w0_ref, w_ref, jnp.logical_not(is_even()), 2)
+    put(side_ref, tiles)
+    far_ref[...] = pack_coarse(share)
 
 
 def mate_kernel(hi_ref, lo_ref, w0_ref, w_ref, after_ref, mate_ref):
     del after_ref
-    even = is_even()
-    tiles = sums_message(hi_ref, lo_ref, w0_ref, w_ref, even)
-    _, others = bands(hi_ref, lo_ref, w0_ref, w_ref)
-    tiles[3] = jnp.where(even, tiles[3], others(3, slot(3, 0)))
+    tiles, _ = sums_message(hi_ref, lo_ref, w0_ref, w_ref, is_even(), 0)
     put(mate_ref, tiles)
 
 
-def own_kernel(hi_ref, lo_ref, w0_ref, w_ref, m_ref, c0_ref, c1_ref, c1b_ref, c2_ref, c3_ref, c3up_ref, y0_ref, y1_ref):
+def own_kernel(hi_ref, lo_ref, w0_ref, w_ref, c0_ref, c1_ref, c1b_ref, c2_ref, c3_ref, c3up_ref):
     level0, others = bands(hi_ref, lo_ref, w0_ref, w_ref)
-    c0_ref[0] = level0(slot(0, 0))
-    c0_ref[1] = level0(slot(0, 7))
-    c1_ref[:, 0:128] = others(1, slot(1, 0))
-    c1_ref[:, 128:256] = others(1, slot(1, 1))
-    c1b_ref[...] = others(1, slot(1, 3))
-    c2_ref[:, 0:128] = others(2, slot(2, 0))
-    c2_ref[:, 128:256] = others(2, slot(2, 1))
-    c3_ref[...] = others(3, slot(3, 0))
-    c3up_ref[...] = others(3, slot(3, 1))
-    y1_ref[...] = apply_vertical(m_ref, 1, others(1, slot(1, 2)))
-    for i in range(1, 7):
-        y0_ref[i - 1] = apply_vertical(m_ref, 0, level0(slot(0, i)))
-
-
-def vertical_kernel(m_ref, c0_ref, c1_ref, c1b_ref, c2_ref, mate_ref, side_ref,
+    c0_ref[0], c0_ref[1] = level0(slot(0, 0), slot(0, 7))
+    c1_ref[:, 0:128], c1_ref[:, 128:256], c1b_ref[...] = others(1, slot(1, 0), slot(1, 1), slot(1, 3))
+    c2_ref[:, 0:128], c2_ref[:, 128:256] = others(2, slot(2, 0), slot(2, 1))
+    c3_ref[...], c3up_ref[...] = others(3, slot(3, 0), slot(3, 1))
+
+
+def inner_kernel(hi_ref, lo_ref, w0_ref, w_ref, m_ref, after_ref, y0_ref, y1_ref):
+    del after_ref
+    level0, others = bands(hi_ref, lo_ref, w0_ref, w_ref)
+    y1_ref[...] = apply_vertical(m_ref, 1, others(1, slot(1, 2))[0])
+    for i, c0 in enumerate(level0(*[slot(0, i) for i in range(1, 7)])):
+        y0_ref[i] = apply_vertical(m_ref, 0, c0)
+
+
+def vertical_kernel(m_ref, filt_ref, c0_ref, c1_ref, c1b_ref, c2_ref, mate_ref, side_ref,
                     y0_ref, y1_ref, y1b_ref, y2_ref, mate_out_ref, side_out_ref):
     below, above = received(mate_ref, side_ref, 4, 3)
     below, above = unpack(below), unpack(above)
     c2 = c2_ref[...]
     y2 = apply_vertical(m_ref, 2, jnp.concatenate([c2[:, 0:128] + below[2], c2[:, 128:256] + below[5] + above[2]], axis=1))
     c1 = c1_ref[...]
-    y1 = apply_vertical(m_ref, 1, jnp.concatenate([c1[:, 0:128] + below[1], c1[:, 128:256] + below[4]], axis=1))
+    y1 = apply_vertical(m_ref, 1, jnp.concatenate([c1[:, 0:128] + below[1], c1[:, 128:256] + three_bands(below[4], filt_ref)], axis=1))
     y1b = apply_vertical(m_ref, 1, c1b_ref[...] + above[1])
     first = apply_vertical(m_ref, 0, c0_ref[0] + below[0])
     last = apply_vertical(m_ref, 0, c0_ref[1] + above[0])
@@ -410,8 +461,9 @@
     y1b_ref[...] = y1b
     y2_ref[...] = y2
     none = jnp.zeros((PAD, LANES), F32)
-    down = pack(first, y1[:, 0:128], y2[:, 0:128], none, y1[:, 128:256], y2[:, 128:256])
-    up = pack(last, y1b, y2[:, 128:256], none, y1[:, 128:256], y2[:, 128:256])
+    sums = two_sums(y1[:, 128:256], filt_ref)
+    down = pack(first, y1[:, 0:128], y2[:, 0:128], none, sums, y2[:, 128:256])
+    up = pack(last, y1b, y2[:, 128:256], none, sums, y2[:, 128:256])
     even = is_even()
     put(side_out_ref, [jnp.where(even, d, u) for d, u in zip(down, up)])
     put(mate_out_ref, [jnp.where(even, u, d) for d, u in zip(down, up)])
@@ -424,51 +476,51 @@
     last = lax.axis_size("lat") - 1
     lane = lane_ids(PAD)
     from_side = jnp.where((place == 0) | (place == last), 0.0, pltpu.roll(part(side_ref, 2), 32, 1))
-    passed = unpack_coarse(passed_ref[PAD : PAD + 40, :])
+    passed = far_of(part(passed_ref, 3, TAIL))
     passed = jnp.where(even, unpack_coarse(far_ref[...]), jnp.where(place == 1, 0.0, passed))
     mine = c3_ref[...] + pltpu.roll(part(mate_ref, 2), 32, 1) + from_side + passed
-    coarse = jnp.where(place == 0, 0.0, unpack_coarse(side_ref[COARSE, :]))
-    above = jnp.where(place == last - 1, 0.0, pltpu.roll(passed_ref[0:PAD, :], 32, 1))
-    other = part(mate_ref, 3) + c3up_ref[...] + coarse + above
+    coarse = jnp.where(place == 0, 0.0, far_of(part(side_ref, 3)))
+    above = jnp.where(place == last - 1, 0.0, pltpu.roll(part(passed_ref, 2, TAIL), 32, 1))
+    other = far_of(part(mate_ref, 3)) + c3up_ref[...] + coarse + above
     both = jnp.concatenate([mine, other], axis=1)
     detail, smooth = apply_vertical(m_ref, 3, both), apply_vertical(m_ref, 4, both)
     y3 = jnp.where(lane < 24, detail[:, 0:128], smooth[:, 0:128])
     y3_ref[...] = y3
     moved = pltpu.roll(y3, 96, 1)
     mate_out_ref[...] = mate_in_ref[...]
-    mate_out_ref[AT[2] : AT[2] + PAD, :] = jnp.where(lane < 96, part(mate_in_ref, 2), moved)
-    side_out_ref[0 : 4 * PAD, :] = side_in_ref[...]
-    side_out_ref[AT[2] : AT[2] + PAD, :] = jnp.where(lane < 96, part(side_in_ref, 2), moved)
-    side_out_ref[COARSE, :] = pack_coarse(jnp.where(lane < 24, detail[:, 128:256], smooth[:, 128:256]))
+    put_one(mate_out_ref, 2, jnp.where(lane < 96, part(mate_in_ref, 2), moved))
+    side_out_ref[...] = side_in_ref[...]
+    put_one(side_out_ref, 2, jnp.where(lane < 96, part(side_in_ref, 2), moved))
+    y3_other = jnp.where(lane < 24, detail[:, 128:256], smooth[:, 128:256])
+    put_one(side_out_ref, 3, with_far(part(side_in_ref, 3), y3_other))
 
 
 def spread_kernel(w0_ref, w_ref, ww_ref, y0c_ref, y1c_ref, y0_ref, y1_ref, y1b_ref, y2_ref, y3_ref, own_ref):
-    for i in range(8):
-        values = y0_ref[i // 7] if i in (0, 7) else y0c_ref[i - 1]
-        own_ref[i] = spread_level0(values, w0_ref)
-    for i, values in enumerate((y1_ref[:, 0:128], y1_ref[:, 128:256], y1c_ref[...], y1b_ref[...])):
-        own_ref[8 + i] = spread_other(1, values, w_ref, ww_ref)
-    for i in range(2):
-        own_ref[12 + i] = spread_other(2, y2_ref[:, i * 128 : i * 128 + 128], w_ref, ww_ref)
-    own_ref[14] = spread_other(3, y3_ref[...], w_ref, ww_ref)
+    level0 = [y0_ref[i // 7] if i in (0, 7) else y0c_ref[i - 1] for i in range(8)]
+    level1 = [y1_ref[:, 0:128], y1_ref[:, 128:256], y1c_ref[...], y1b_ref[...]]
+    level2 = [y2_ref[:, 0:128], y2_ref[:, 128:256]]
+    wide = spread_level0(level0, w0_ref)
+    for level, values in ((1, level1), (2, level2), (3, [y3_ref[...]])):
+        wide += spread_other(level, values, w_ref, ww_ref)
+    for i, values in enumerate(wide):
+        own_ref[i] = values
 
 
 def received_kernel(w0_ref, w_ref, ww_ref, mate_ref, side_ref, got_ref):
     below, above = received(mate_ref, side_ref, 3, 4)
     below, above = unpack(below), unpack(above)
-    values = {(0, -1): below[0], (0, 8): above[0], (1, -1): below[1], (1, 4): above[1], (1, 5): above[4],
-              (2, -1): below[2], (2, 2): above[2], (2, 3): above[5], (3, -1): below[3], (3, 1): above[3]}
-    for (level, index), v in values.items():
-        if level == 0:
-            got_ref[GOT[level, index]] = spread_level0(v, w0_ref)
-        else:
-            got_ref[GOT[level, index]] = spread_other(level, v, w_ref, ww_ref)
+    wide = spread_level0([below[0], above[0]], w0_ref)
+    wide += spread_other(1, [below[1], above[1], bands_of_sums(above[4])], w_ref, ww_ref)
+    wide += spread_other(2, [below[2], above[2], above[5]], w_ref, ww_ref)
+    wide += spread_other(3, [below[3], above[3]], w_ref, ww_ref)
+    for i, values in enumerate(wide):
+        got_ref[i] = values
 
 
 def spread_coarse(side_ref, passed_ref, w_ref, ww_ref, far_ref):
-    value = jnp.where(is_even(), pltpu.roll(passed_ref[...], 32, 1), unpack_coarse(side_ref[COARSE, :]))
+    value = jnp.where(is_even(), pltpu.roll(part(passed_ref, 2, END_TILE), 32, 1), far_of(part(side_ref, 3)))
     value = jnp.where(lax.axis_index("lat") >= lax.axis_size("lat") - 2, 0.0, value)
-    far_ref[0] = spread_other(3, value, w_ref, ww_ref)
+    far_ref[0] = spread_other(3, [value], w_ref, ww_ref)[0]
 
 
 def middle_kernel(filt_ref, w_ref, ww_ref, own_ref, got_ref, side_ref, passed_ref, hi_ref, lo_ref, far_ref):
@@ -514,17 +566,16 @@
     tail.wait()
 
 
-def prepare_kernel(m_ref, after_ref, plain_ref, turned_ref, wide_ref):
+def prepare_kernel(turned, m_ref, after_ref, out_ref, wide_ref):
     del after_ref
     levels = m_ref.shape[1]
     wide_ref[...] = jnp.zeros_like(wide_ref)
     for band in range(m_ref.shape[0]):
         wide_ref[0:levels, 0:levels] = m_ref[band]
-        values = wide_ref[...]
-        for ref, matrix in ((plain_ref, values), (turned_ref, values.T)):
-            high, low = split(matrix[0:PAD])
-            ref[band, 0:PAD, :] = high
-            ref[band, PAD : 2 * PAD, :] = low
+        matrix = wide_ref[...].T if turned else wide_ref[...]
+        high, low = split(matrix[0:PAD])
+        out_ref[band, 0:PAD, :] = high
+        out_ref[band, PAD : 2 * PAD, :] = low
 
 
 VMEM = pl.BlockSpec(memory_space=pltpu.VMEM)
@@ -532,8 +583,7 @@
 HBM = pl.BlockSpec(memory_space=pltpu.HBM)
 ANY = pl.BlockSpec(memory_space=pl.ANY)
 
-MESSAGE = ((4 * PAD, LANES), F32)
-SIDE = ((4 * PAD + 40, LANES), F32)
+MESSAGE = ((4 * MAIN + 8, LANES), F32)
 FAR = ((40, LANES), F32)
 WEIGHTS = (((80, LANES), F32), ((256, 512), BF16), ((3, 256, 256), BF16), ((3, 256, 256), BF16))
 HALVES = (((SLOTS, PAD, 256), BF16),) * 2
@@ -575,35 +625,41 @@
     flat = increment.reshape(levels * rows, columns)
     filt, w0, w, ww = call(weights_kernel, [SMEM], WEIGHTS, [], 12)(filter_taps)
     hi, lo = call(first_kernel, [VMEM] * 2, HALVES, [], 12)(filt, flat)
-    plain, turned = call(
-        prepare_kernel, [VMEM, ANY], (((5, 2 * PAD, 256), BF16),) * 2, [pltpu.VMEM((256, 256), F32)], 12
-    )(band_roots, hi)
-
-    def half(matrix, hi, lo):
-        side, far = call(side_kernel, [VMEM] * 4, (SIDE, FAR), [], 12)(hi, lo, w0, w)
+
+    def prepare(turned, after):
+        kernel = functools.partial(prepare_kernel, turned)
+        wide = [pltpu.VMEM((256, 256), F32)]
+        (out,) = call(kernel, [VMEM, ANY], (((5, 2 * PAD, 256), BF16),), wide, 12)(band_roots, after)
+        return out
+
+    def half(matrix, hi, lo, first):
+        side, far = call(side_kernel, [VMEM] * 4, (MESSAGE, FAR), [], 12)(hi, lo, w0, w)
         (mate,) = call(mate_kernel, [VMEM] * 4 + [ANY], (MESSAGE,), [], 12)(hi, lo, w0, w, side)
         side, mate, far = swap(side, 1), swap(mate, 0), pass_up(far)
-        *edges, c3, c3up, y0c, y1c = call(
-            own_kernel, [VMEM] * 5, EDGES + (COARSEST, COARSEST) + INNER, [], 12
-        )(hi, lo, w0, w, matrix)
-        side, y1c = lax.optimization_barrier((side, y1c))
-        passed = swap(side[3 * PAD :], 0)
+        *edges, c3, c3up = call(own_kernel, [VMEM] * 4, EDGES + (COARSEST, COARSEST), [], 12)(hi, lo, w0, w)
+        side, c3up = lax.optimization_barrier((side, c3up))
+        passed = swap(side[TAIL:], 0)
         *edges, mate_out, side_out = call(
-            vertical_kernel, [VMEM] * 7, EDGES + (MESSAGE, MESSAGE), [], 12
-        )(matrix, *edges, mate, side)
-        y3, mate, side = call(coarse_kernel, [VMEM] * 9, (COARSEST, MESSAGE, SIDE), [], 12)(
+            vertical_kernel, [VMEM] * 8, EDGES + (MESSAGE, MESSAGE), [], 12
+        )(matrix, filt, *edges, mate, side)
+        y3, mate, side = call(coarse_kernel, [VMEM] * 9, (COARSEST, MESSAGE, MESSAGE), [], 12)(
             matrix, c3, c3up, far, mate, side, passed, mate_out, side_out
         )
         side, mate = swap(side, 1), swap(mate, 0)
+        y0c, y1c = call(inner_kernel, [VMEM] * 5 + [ANY], INNER, [], 12)(hi, lo, w0, w, matrix, y3)
+        turned = prepare(True, y3) if first else None
         (own,) = call(spread_kernel, [VMEM] * 10, (OWN_WIDE,), [], 12)(w0, w, ww, y0c, y1c, *edges, y3)
-        side, own = lax.optimization_barrier((side, own))
-        passed = swap(side[3 * PAD : 4 * PAD], 0)
+        if first:
+            side, own, turned = lax.optimization_barrier((side, own, turned))
+        else:
+            side, own = lax.optimization_barrier((side, own))
+        passed = swap(side[END_TILE:], 0)
         (got,) = call(received_kernel, [VMEM] * 5, (GOT_WIDE,), [], 12)(w0, w, ww, mate, side)
-        return filt, w, ww, own, got, side, passed
-
-    ready = half(plain, hi, lo)
+        return filt, w, ww, own, got, side, passed, turned
+
+    *ready, turned = half(prepare(False, hi), hi, lo, True)
     hi, lo = call(middle_kernel, [VMEM] * 7, HALVES, [FAR_WIDE], 12)(*ready)
-    ready = half(turned, hi, lo)
+    *ready, _ = half(turned, hi, lo, False)
     (out,) = call(
         last_kernel, [VMEM] * 7, (((levels * rows, columns), F32),),
         [FAR_WIDE, pltpu.VMEM((levels * rows, columns), F32), pltpu.SemaphoreType.DMA((9,))], 12, HBM,

time: 78.9 us -> 72.2 us (0.915)
  the two profiles are of different devices: /device:TPU:1057 before, /device:TPU:1577 now
where the time goes in v3:
time: 72.2 us; the launch traced here: 71.9 us
  starting transfers between devices  45.7 us (63%)
  Pallas kernels  20.4 us (28%)
  waiting for transfers between devices  4.53 us (6%)
  local copies, waits for them, and re-layouts  0.83 us (1%)
    ppermute x12, starting transfers between devices, swap(): lax.ppermute(values, 'lat', [(i, partner.get(i, i)) for i in range(count)])  44.1 us
    ppermute x12, waiting for transfers between devices, swap(): lax.ppermute(values, 'lat', [(i, partner.get(i, i)) for i in range(count)])  4.53 us
    pallas_call x2, Pallas kernels, half(): call(inner_kernel, [VMEM] * 5 + [ANY], INNER, [], 12)  3.36 us
    pallas_call x1, Pallas kernels, on_device(): hi, lo = call(middle_kernel, [VMEM] * 7, HALVES, [FAR_WIDE], 12)(*ready)  2.6 us
    pallas_call x1, Pallas kernels, on_device(): call(last_kernel, [VMEM] * 7, (((levels * rows, columns), F32),), [FAR_WI...  2.12 us
    pallas_call x2, Pallas kernels, half(): call(spread_kernel, [VMEM] * 10, (OWN_WIDE,), [], 12)  1.93 us
    ppermute x2, starting transfers between devices, pass_up(): lax.ppermute(values, 'lat', [(i, i + 2) for i in range(0, count - 2, 2)])  1.61 us
    pallas_call x1, Pallas kernels, on_device(): hi, lo = call(first_kernel, [VMEM] * 2, HALVES, [], 12)(filt, flat)  1.58 us
  transfers between devices with their start and end apart: 14, of which 4 were waited for; matrix products, arithmetic and copies ran while one was open for 0% of the time, Pallas kernels for 15%

profile of v3, /device:TPU:1577, one launch (start us, length us, event | category | flops | bytes accessed | tf_op | source)
XLA Modules:
  0.0 71.9 jit_solution(8940862365900634072)
XLA Ops:
  0.0 0.8 %copy-done.2 = s32[4,2,2,5]{3,2,1,0:T(2,128)S(1)} copy-done((s32[4,2,2,5]{3,2,1,0:T(2,128)S(1)}, s32[4,2,2,5]{3,2,1,0:T(2,128)}, u32[]{:S(2)}) %copy-start.2) | copy-done | bytes 344
  0.8 1.4 %shard_map.37 = (f32[80,128]{1,0:T(8,128)S(1)}, bf16[256,512]{1,0:T(8,128)(2,1)S(1)}, bf16[3,256,256]{2,1,0:T(8,128)(2,1)S(1)}, bf16[3,256,256]{2,1,0:T(8,128)(2,1)S(1)}) custom-call(s32[4,2,2,5]{3,2,1,0:T(2,128)S(1)} %copy-done.2), custom_call_target="tpu_custom_call" | custom-call | flops 1000000000 | bytes 8388608 | tf_op jit(solution)/shard_map/pallas_call | solution.py:626
  2.2 1.6 %shard_map.38 = (bf16[26,144,256]{2,1,0:T(8,128)(2,1)S(1)}, bf16[26,144,256]{2,1,0:T(8,128)(2,1)S(1)}) custom-call(f32[80,128]{1,0:T(8,128)S(1)} %get-tuple-element.60.filt_ref, f32[2192,128]{1,0:T(8,128)S(1)} %bitcast.2), custom_call_target="tpu_custom_call" | custom-call | flops 1000000000 | bytes 8388608 | tf_op jit(solution)/shard_map/pallas_call | solution.py:627
  3.8 0.5 shard_map.41
  4.4 3.8 %collective-permute-start = (f32[552,128]{1,0:T(8,128)S(1)}, f32[552,128]{1,0:T(8,128)S(1)}, u32[]{:S(2)}, u32[]{:S(2)}) collective-permute-start(f32[552,128]{1,0:T(8,128)S(1)} %get-tuple-element.67.after_ref), channel_id=1, source_target_pairs={{0,0},{1,2},{2,1},{3,4},{4,3},{5,6},{6,5},{7,8},{8,7},{9,10},{10,9... | collective-permute-start | bytes 847880 | tf_op jit(solution)/shard_map/ppermute | solution.py:615
  8.2 0.5 shard_map.42
  8.7 2.4 %collective-permute-start.2 = (f32[552,128]{1,0:T(8,128)S(1)}, f32[552,128]{1,0:T(8,128)S(1)}, u32[]{:S(2)}, u32[]{:S(2)}) collective-permute-start(f32[552,128]{1,0:T(8,128)S(1)} %shard_map.42), channel_id=1, source_target_pairs={{0,1},{1,0},{2,3},{3,2},{4,5},{5,4},{6,7},{7,6},{8,9},{9,8},{10,11... | collective-permute-start | bytes 847880 | tf_op jit(solution)/shard_map/ppermute | solution.py:615
  11.1 0.8 %collective-permute-start.1 = (f32[40,128]{1,0:T(8,128)S(1)}, f32[40,128]{1,0:T(8,128)S(1)}, u32[]{:S(2)}, u32[]{:S(2)}) collective-permute-start(f32[40,128]{1,0:T(8,128)S(1)} %get-tuple-element.70), channel_id=1, source_target_pairs={{0,2},{2,4},{4,6},{6,8},{8,10},{10,12},{12,14},{14,16},{16,18},{18... | collective-permute-start | bytes 61448 | tf_op jit(solution)/shard_map/ppermute | solution.py:620
  11.8 0.6 shard_map.40
  12.4 0.0 collective-permute-done.side_ref
  12.4 3.9 %collective-permute-start.3 = (f32[280,128]{1,0:T(8,128)S(1)}, f32[280,128]{1,0:T(8,128)S(1)}, u32[]{:S(2)}, u32[]{:S(2)}) collective-permute-start(f32[280,128]{1,0:T(8,128)S(1)} %slice.12), channel_id=1, source_target_pairs={{0,1},{1,0},{2,3},{3,2},{4,5},{5,4},{6,7},{7,6},{8,9},{9,8},{10,11... | collective-permute-start | bytes 430088 | tf_op jit(solution)/shard_map/ppermute | solution.py:615
  16.4 0.2 shard_map.39.m_ref
  16.5 0.0 collective-permute-done.2.mate_ref
  16.6 0.6 shard_map.43
  17.2 0.0 collective-permute-done.1.far_ref
  17.2 0.2 collective-permute-done.3.passed_ref
  17.4 0.5 shard_map.44
  17.9 2.0 %collective-permute-start.4 = (f32[552,128]{1,0:T(8,128)S(1)}, f32[552,128]{1,0:T(8,128)S(1)}, u32[]{:S(2)}, u32[]{:S(2)}) collective-permute-start(f32[552,128]{1,0:T(8,128)S(1)} %get-tuple-element.78), channel_id=1, source_target_pairs={{0,0},{1,2},{2,1},{3,4},{4,3},{5,6},{6,5},{7,8},{8,7},{9,10},{10,9... | collective-permute-start | bytes 847880 | tf_op jit(solution)/shard_map/ppermute | solution.py:615
  19.9 3.9 %collective-permute-start.5 = (f32[552,128]{1,0:T(8,128)S(1)}, f32[552,128]{1,0:T(8,128)S(1)}, u32[]{:S(2)}, u32[]{:S(2)}) collective-permute-start(f32[552,128]{1,0:T(8,128)S(1)} %get-tuple-element.88), channel_id=1, source_target_pairs={{0,1},{1,0},{2,3},{3,2},{4,5},{5,4},{6,7},{7,6},{8,9},{9,8},{10,11... | collective-permute-start | bytes 847880 | tf_op jit(solution)/shard_map/ppermute | solution.py:615
  23.8 1.7 %shard_map.45 = (f32[6,144,256]{2,1,0:T(8,128)S(1)}, f32[144,128]{1,0:T(8,128)S(1)}) custom-call(bf16[26,144,256]{2,1,0:T(8,128)(2,1)S(1)} %get-tuple-element.63.after_ref.hi_ref, bf16[26,144,256]{2,1,0:T(8,128)(2,1)S(1)} %get-tuple-element.64.lo_ref, bf16[256,512]{1,0:T(8,128)(2,1)S(1)} %get-tuple-element.65.w0_ref, ...), custom_call_target="tpu_custom_call" | custom-call | flops 1000000000 | bytes 8388608 | tf_op jit(solution)/shard_map/pallas_call | solution.py:649
  25.5 0.4 shard_map.47.m_ref
  25.9 1.0 %shard_map.46.own_ref = f32[15,144,256]{2,1,0:T(8,128)S(1)} custom-call(bf16[256,512]{1,0:T(8,128)(2,1)S(1)} %get-tuple-element.65.w0_ref, bf16[3,256,256]{2,1,0:T(8,128)(2,1)S(1)} %get-tuple-element.61.w_ref, bf16[3,256,256]{2,1,0:T(8,128)(2,1)S(1)} %get-tuple-element.62.ww_ref, f32[6,144,256]{2,1,0:T(8,128)S(1)} %get-tuple-element.80.y0c_ref, ...), custom_call_target="tpu_custom_call" | custom-call | flops 1000000000 | bytes 8388608 | tf_op jit(solution)/shard_map/pallas_call | solution.py:651
  26.9 5.1 %collective-permute-start.6 = (f32[144,128]{1,0:T(8,128)S(1)}, f32[144,128]{1,0:T(8,128)S(1)}, u32[]{:S(2)}, u32[]{:S(2)}) collective-permute-start(f32[144,128]{1,0:T(8,128)S(1)} %slice.13), channel_id=1, source_target_pairs={{0,1},{1,0},{2,3},{3,2},{4,5},{5,4},{6,7},{7,6},{8,9},{9,8},{10,11... | collective-permute-start | bytes 221192 | tf_op jit(solution)/shard_map/ppermute | solution.py:615
  32.0 0.0 collective-permute-done.5.mate_ref
  32.0 0.6 shard_map.48.got_ref
  32.7 0.3 collective-permute-done.6.passed_ref
  33.0 2.6 %shard_map.49 = (bf16[26,144,256]{2,1,0:T(8,128)(2,1)S(1)}, bf16[26,144,256]{2,1,0:T(8,128)(2,1)S(1)}) custom-call(f32[80,128]{1,0:T(8,128)S(1)} %get-tuple-element.60.filt_ref, bf16[3,256,256]{2,1,0:T(8,128)(2,1)S(1)} %get-tuple-element.61.w_ref, bf16[3,256,256]{2,1,0:T(8,128)(2,1)S(1)} %get-tuple-element.62.ww_ref, f32[15,144,256]{2,1,0:T(8,128)S(1)} %shard_map.46.own_ref, ...), custom_call_target="tpu_custom_call" | custom-call | flops 1000000000 | bytes 8388608 | tf_op jit(solution)/shard_map/pallas_call | solution.py:661
  35.6 0.5 shard_map.51
  36.1 2.0 %collective-permute-start.7 = (f32[552,128]{1,0:T(8,128)S(1)}, f32[552,128]{1,0:T(8,128)S(1)}, u32[]{:S(2)}, u32[]{:S(2)}) collective-permute-start(f32[552,128]{1,0:T(8,128)S(1)} %get-tuple-element.93.after_ref), channel_id=1, source_target_pairs={{0,0},{1,2},{2,1},{3,4},{4,3},{5,6},{6,5},{7,8},{8,7},{9,10},{10,9... | collective-permute-start | bytes 847880 | tf_op jit(solution)/shard_map/ppermute | solution.py:615
  38.1 0.5 shard_map.52
  38.6 1.4 %collective-permute-start.9 = (f32[552,128]{1,0:T(8,128)S(1)}, f32[552,128]{1,0:T(8,128)S(1)}, u32[]{:S(2)}, u32[]{:S(2)}) collective-permute-start(f32[552,128]{1,0:T(8,128)S(1)} %shard_map.52), channel_id=1, source_target_pairs={{0,1},{1,0},{2,3},{3,2},{4,5},{5,4},{6,7},{7,6},{8,9},{9,8},{10,11... | collective-permute-start | bytes 847880 | tf_op jit(solution)/shard_map/ppermute | solution.py:615
  40.0 0.5 shard_map.50
  40.6 3.8 %collective-permute-done.7.side_ref = f32[552,128]{1,0:T(8,128)S(1)} collective-permute-done((f32[552,128]{1,0:T(8,128)S(1)}, f32[552,128]{1,0:T(8,128)S(1)}, u32[]{:S(2)}, u32[]{:S(2)}) %collective-permute-start.7) | collective-permute-done | bytes 282656 | tf_op jit(solution)/shard_map/ppermute | solution.py:615
  44.4 3.5 %collective-permute-start.10 = (f32[280,128]{1,0:T(8,128)S(1)}, f32[280,128]{1,0:T(8,128)S(1)}, u32[]{:S(2)}, u32[]{:S(2)}) collective-permute-start(f32[280,128]{1,0:T(8,128)S(1)} %slice.14), channel_id=1, source_target_pairs={{0,1},{1,0},{2,3},{3,2},{4,5},{5,4},{6,7},{7,6},{8,9},{9,8},{10,11... | collective-permute-start | bytes 430088 | tf_op jit(solution)/shard_map/ppermute | solution.py:615
  47.9 0.8 %collective-permute-start.8 = (f32[40,128]{1,0:T(8,128)S(1)}, f32[40,128]{1,0:T(8,128)S(1)}, u32[]{:S(2)}, u32[]{:S(2)}) collective-permute-start(f32[40,128]{1,0:T(8,128)S(1)} %get-tuple-element.96), channel_id=1, source_target_pairs={{0,2},{2,4},{4,6},{6,8},{8,10},{10,12},{12,14},{14,16},{16,18},{18... | collective-permute-start | bytes 61448 | tf_op jit(solution)/shard_map/ppermute | solution.py:620
  48.7 0.0 collective-permute-done.9.mate_ref
  48.7 0.6 shard_map.53
  49.4 0.0 collective-permute-done.8.far_ref
  49.4 0.5 shard_map.54
  49.9 5.8 %collective-permute-start.11 = (f32[552,128]{1,0:T(8,128)S(1)}, f32[552,128]{1,0:T(8,128)S(1)}, u32[]{:S(2)}, u32[]{:S(2)}) collective-permute-start(f32[552,128]{1,0:T(8,128)S(1)} %get-tuple-element.104), channel_id=1, source_target_pairs={{0,0},{1,2},{2,1},{3,4},{4,3},{5,6},{6,5},{7,8},{8,7},{9,10},{10,9... | collective-permute-start | bytes 847880 | tf_op jit(solution)/shard_map/ppermute | solution.py:615
  55.7 3.8 %collective-permute-start.12 = (f32[552,128]{1,0:T(8,128)S(1)}, f32[552,128]{1,0:T(8,128)S(1)}, u32[]{:S(2)}, u32[]{:S(2)}) collective-permute-start(f32[552,128]{1,0:T(8,128)S(1)} %get-tuple-element.113), channel_id=1, source_target_pairs={{0,1},{1,0},{2,3},{3,2},{4,5},{5,4},{6,7},{7,6},{8,9},{9,8},{10,11... | collective-permute-start | bytes 847880 | tf_op jit(solution)/shard_map/ppermute | solution.py:615
  59.5 1.7 %shard_map.55 = (f32[6,144,256]{2,1,0:T(8,128)S(1)}, f32[144,128]{1,0:T(8,128)S(1)}) custom-call(bf16[26,144,256]{2,1,0:T(8,128)(2,1)S(1)} %get-tuple-element.90.hi_ref, bf16[26,144,256]{2,1,0:T(8,128)(2,1)S(1)} %get-tuple-element.91.lo_ref, bf16[256,512]{1,0:T(8,128)(2,1)S(1)} %get-tuple-element.65.w0_ref, ...), custom_call_target="tpu_custom_call" | custom-call | flops 1000000000 | bytes 8388608 | tf_op jit(solution)/shard_map/pallas_call | solution.py:649
  61.2 1.0 %shard_map.56.own_ref = f32[15,144,256]{2,1,0:T(8,128)S(1)} custom-call(bf16[256,512]{1,0:T(8,128)(2,1)S(1)} %get-tuple-element.65.w0_ref, bf16[3,256,256]{2,1,0:T(8,128)(2,1)S(1)} %get-tuple-element.61.w_ref, bf16[3,256,256]{2,1,0:T(8,128)(2,1)S(1)} %get-tuple-element.62.ww_ref, f32[6,144,256]{2,1,0:T(8,128)S(1)} %get-tuple-element.106.y0c_ref, ...), custom_call_target="tpu_custom_call" | custom-call | flops 1000000000 | bytes 8388608 | tf_op jit(solution)/shard_map/pallas_call | solution.py:651
  62.2 0.0 collective-permute-done.11.side_ref
  62.2 6.5 %collective-permute-start.13 = (f32[144,128]{1,0:T(8,128)S(1)}, f32[144,128]{1,0:T(8,128)S(1)}, u32[]{:S(2)}, u32[]{:S(2)}) collective-permute-start(f32[144,128]{1,0:T(8,128)S(1)} %slice.15), channel_id=1, source_target_pairs={{0,1},{1,0},{2,3},{3,2},{4,5},{5,4},{6,7},{7,6},{8,9},{9,8},{10,11... | collective-permute-start | bytes 221192 | tf_op jit(solution)/shard_map/ppermute | solution.py:615
  68.7 0.6 shard_map.57.got_ref
  69.4 0.3 collective-permute-done.13.passed_ref
  69.6 2.1 %shard_map.58 = f32[2192,128]{1,0:T(8,128)} custom-call(f32[80,128]{1,0:T(8,128)S(1)} %get-tuple-element.60.filt_ref, bf16[3,256,256]{2,1,0:T(8,128)(2,1)S(1)} %get-tuple-element.61.w_ref, bf16[3,256,256]{2,1,0:T(8,128)(2,1)S(1)} %get-tuple-element.62.ww_ref, f32[15,144,256]{2,1,0:T(8,128)S(1)} %shard_map.56.own_ref, f32[10,144,256]{2,1,0:T(8,128)S(1)} %shard_map.57.got_ref, ...), custom_call_target="tpu_custom_call" | custom-call | flops 1000000000 | bytes 8388608 | tf_op jit(solution)/shard_map/pallas_call | solution.py:663
  (12 shorter events, 0.1 us)
Async XLA Ops:
  0.0 2.2 %copy-start = (f32[137,16,128]{2,1,0:T(8,128)S(1)}, f32[137,16,128]{2,1,0:T(8,128)}, u32[]{:S(2)}) copy-start(f32[137,16,128]{2,1,0:T(8,128)} %param.3) | copy-start | bytes 3366916
  0.0 0.8 %copy-start.2 = (s32[4,2,2,5]{3,2,1,0:T(2,128)S(1)}, s32[4,2,2,5]{3,2,1,0:T(2,128)}, u32[]{:S(2)}) copy-start(s32[4,2,2,5]{3,2,1,0:T(2,128)} %taps_ref.1) | copy-start | bytes 964
  4.4 8.1 %collective-permute-start = (f32[552,128]{1,0:T(8,128)S(1)}, f32[552,128]{1,0:T(8,128)S(1)}, u32[]{:S(2)}, u32[]{:S(2)}) collective-permute-start(f32[552,128]{1,0:T(8,128)S(1)} %get-tuple-element.67.after_ref), channel_id=1, source_target_pairs={{0,0},{1,2},{2,1},{3,4},{4,3},{5,6},{6,5},{7,8},{8,7},{9,10},{10,9... | collective-permute-start | bytes 847880 | tf_op jit(solution)/shard_map/ppermute | solution.py:615
  8.7 7.8 %collective-permute-start.2 = (f32[552,128]{1,0:T(8,128)S(1)}, f32[552,128]{1,0:T(8,128)S(1)}, u32[]{:S(2)}, u32[]{:S(2)}) collective-permute-start(f32[552,128]{1,0:T(8,128)S(1)} %shard_map.42), channel_id=1, source_target_pairs={{0,1},{1,0},{2,3},{3,2},{4,5},{5,4},{6,7},{7,6},{8,9},{9,8},{10,11... | collective-permute-start | bytes 847880 | tf_op jit(solution)/shard_map/ppermute | solution.py:615
  11.1 5.3 %copy-start.1 = (f32[5,137,137]{2,1,0:T(8,128)S(1)}, f32[5,137,137]{2,1,0:T(8,128)}, u32[]{:S(2)}) copy-start(f32[5,137,137]{2,1,0:T(8,128)} %m_ref.3) | copy-start | bytes 1126144
  11.1 6.1 %collective-permute-start.1 = (f32[40,128]{1,0:T(8,128)S(1)}, f32[40,128]{1,0:T(8,128)S(1)}, u32[]{:S(2)}, u32[]{:S(2)}) collective-permute-start(f32[40,128]{1,0:T(8,128)S(1)} %get-tuple-element.70), channel_id=1, source_target_pairs={{0,2},{2,4},{4,6},{6,8},{8,10},{10,12},{12,14},{14,16},{16,18},{18... | collective-permute-start | bytes 61448 | tf_op jit(solution)/shard_map/ppermute | solution.py:620
  12.4 4.9 %collective-permute-start.3 = (f32[280,128]{1,0:T(8,128)S(1)}, f32[280,128]{1,0:T(8,128)S(1)}, u32[]{:S(2)}, u32[]{:S(2)}) collective-permute-start(f32[280,128]{1,0:T(8,128)S(1)} %slice.12), channel_id=1, source_target_pairs={{0,1},{1,0},{2,3},{3,2},{4,5},{5,4},{6,7},{7,6},{8,9},{9,8},{10,11... | collective-permute-start | bytes 430088 | tf_op jit(solution)/shard_map/ppermute | solution.py:615
  17.9 9.0 %collective-permute-start.4 = (f32[552,128]{1,0:T(8,128)S(1)}, f32[552,128]{1,0:T(8,128)S(1)}, u32[]{:S(2)}, u32[]{:S(2)}) collective-permute-start(f32[552,128]{1,0:T(8,128)S(1)} %get-tuple-element.78), channel_id=1, source_target_pairs={{0,0},{1,2},{2,1},{3,4},{4,3},{5,6},{6,5},{7,8},{8,7},{9,10},{10,9... | collective-permute-start | bytes 847880 | tf_op jit(solution)/shard_map/ppermute | solution.py:615
  19.9 12.2 %collective-permute-start.5 = (f32[552,128]{1,0:T(8,128)S(1)}, f32[552,128]{1,0:T(8,128)S(1)}, u32[]{:S(2)}, u32[]{:S(2)}) collective-permute-start(f32[552,128]{1,0:T(8,128)S(1)} %get-tuple-element.88), channel_id=1, source_target_pairs={{0,1},{1,0},{2,3},{3,2},{4,5},{5,4},{6,7},{7,6},{8,9},{9,8},{10,11... | collective-permute-start | bytes 847880 | tf_op jit(solution)/shard_map/ppermute | solution.py:615
  26.9 6.0 %collective-permute-start.6 = (f32[144,128]{1,0:T(8,128)S(1)}, f32[144,128]{1,0:T(8,128)S(1)}, u32[]{:S(2)}, u32[]{:S(2)}) collective-permute-start(f32[144,128]{1,0:T(8,128)S(1)} %slice.13), channel_id=1, source_target_pairs={{0,1},{1,0},{2,3},{3,2},{4,5},{5,4},{6,7},{7,6},{8,9},{9,8},{10,11... | collective-permute-start | bytes 221192 | tf_op jit(solution)/shard_map/ppermute | solution.py:615
  36.1 8.2 %collective-permute-start.7 = (f32[552,128]{1,0:T(8,128)S(1)}, f32[552,128]{1,0:T(8,128)S(1)}, u32[]{:S(2)}, u32[]{:S(2)}) collective-permute-start(f32[552,128]{1,0:T(8,128)S(1)} %get-tuple-element.93.after_ref), channel_id=1, source_target_pairs={{0,0},{1,2},{2,1},{3,4},{4,3},{5,6},{6,5},{7,8},{8,7},{9,10},{10,9... | collective-permute-start | bytes 847880 | tf_op jit(solution)/shard_map/ppermute | solution.py:615
  38.6 10.1 %collective-permute-start.9 = (f32[552,128]{1,0:T(8,128)S(1)}, f32[552,128]{1,0:T(8,128)S(1)}, u32[]{:S(2)}, u32[]{:S(2)}) collective-permute-start(f32[552,128]{1,0:T(8,128)S(1)} %shard_map.52), channel_id=1, source_target_pairs={{0,1},{1,0},{2,3},{3,2},{4,5},{5,4},{6,7},{7,6},{8,9},{9,8},{10,11... | collective-permute-start | bytes 847880 | tf_op jit(solution)/shard_map/ppermute | solution.py:615
  44.4 5.0 %collective-permute-start.10 = (f32[280,128]{1,0:T(8,128)S(1)}, f32[280,128]{1,0:T(8,128)S(1)}, u32[]{:S(2)}, u32[]{:S(2)}) collective-permute-start(f32[280,128]{1,0:T(8,128)S(1)} %slice.14), channel_id=1, source_target_pairs={{0,1},{1,0},{2,3},{3,2},{4,5},{5,4},{6,7},{7,6},{8,9},{9,8},{10,11... | collective-permute-start | bytes 430088 | tf_op jit(solution)/shard_map/ppermute | solution.py:615
  47.9 1.5 %collective-permute-start.8 = (f32[40,128]{1,0:T(8,128)S(1)}, f32[40,128]{1,0:T(8,128)S(1)}, u32[]{:S(2)}, u32[]{:S(2)}) collective-permute-start(f32[40,128]{1,0:T(8,128)S(1)} %get-tuple-element.96), channel_id=1, source_target_pairs={{0,2},{2,4},{4,6},{6,8},{8,10},{10,12},{12,14},{14,16},{16,18},{18... | collective-permute-start | bytes 61448 | tf_op jit(solution)/shard_map/ppermute | solution.py:620
  49.9 12.3 %collective-permute-start.11 = (f32[552,128]{1,0:T(8,128)S(1)}, f32[552,128]{1,0:T(8,128)S(1)}, u32[]{:S(2)}, u32[]{:S(2)}) collective-permute-start(f32[552,128]{1,0:T(8,128)S(1)} %get-tuple-element.104), channel_id=1, source_target_pairs={{0,0},{1,2},{2,1},{3,4},{4,3},{5,6},{6,5},{7,8},{8,7},{9,10},{10,9... | collective-permute-start | bytes 847880 | tf_op jit(solution)/shard_map/ppermute | solution.py:615
  55.7 13.0 %collective-permute-start.12 = (f32[552,128]{1,0:T(8,128)S(1)}, f32[552,128]{1,0:T(8,128)S(1)}, u32[]{:S(2)}, u32[]{:S(2)}) collective-permute-start(f32[552,128]{1,0:T(8,128)S(1)} %get-tuple-element.113), channel_id=1, source_target_pairs={{0,1},{1,0},{2,3},{3,2},{4,5},{5,4},{6,7},{7,6},{8,9},{9,8},{10,11... | collective-permute-start | bytes 847880 | tf_op jit(solution)/shard_map/ppermute | solution.py:615
  62.2 7.4 %collective-permute-start.13 = (f32[144,128]{1,0:T(8,128)S(1)}, f32[144,128]{1,0:T(8,128)S(1)}, u32[]{:S(2)}, u32[]{:S(2)}) collective-permute-start(f32[144,128]{1,0:T(8,128)S(1)} %slice.15), channel_id=1, source_target_pairs={{0,1},{1,0},{2,3},{3,2},{4,5},{5,4},{6,7},{7,6},{8,9},{9,8},{10,11... | collective-permute-start | bytes 221192 | tf_op jit(solution)/shard_map/ppermute | solution.py:615

commit v4 on v3

--- a/solution.py
+++ b/solution.py
@@ -160,25 +160,60 @@
     return out
 
 
-def latitude_synthesis(pick, filt_ref, flags):
+SPAN = ((0, ROWS - 1), (FIRST, LAST[0]), (FIRST, LAST[1]), (FIRST, LAST[2]))
+SUM_BASE = (0, 16, 26, 33)
+SUMS = 38
+
+
+def add_term(total, term):
+    return term if total is None else total + term
+
+
+def own_sums(pick, filt_ref):
+    out = {}
+    for level in range(LEVELS):
+        low = coeffs(filt_ref, level, 0, 0)
+        high = coeffs(filt_ref, level, 0, 1)
+        wide = {i: pick(slot(level, i)) for i in range(OWN[level])}
+        first, last = SPAN[level]
+        for r in range(first, last + 1):
+            total = None
+            for index, (a, d) in wide.items():
+                k = r - 2 * index + 2
+                if 0 <= k < TAPS:
+                    total = add_term(total, low[k] * a + high[k] * d)
+            if total is not None:
+                out[SUM_BASE[level] + r - first] = total
+    return out
+
+
+def has_own(level, r):
+    return any(0 <= r - 2 * index + 2 < TAPS for index in range(OWN[level]))
+
+
+def latitude_synthesis(pick, sums, filt_ref, flags):
     rows = None
     for level in reversed(range(LEVELS)):
         low = coeffs(filt_ref, level, 0, 0)
         high = coeffs(filt_ref, level, 0, 1)
-        first, last = (FIRST, LAST[level - 1]) if level else (0, ROWS - 1)
+        first, last = SPAN[level]
         smooth, sharp = {}, {}
         for index in range(FIRST, LAST[level] + 1):
-            a, d = pick(slot(level, index))
-            smooth[index] = a if rows is None else a + rows[index]
-            sharp[index] = d
+            if rows is not None:
+                smooth[index] = rows[index]
+            if not 0 <= index < OWN[level]:
+                a, sharp[index] = pick(slot(level, index))
+                smooth[index] = add_term(smooth.get(index), a)
         out = {}
         for r in range(first, last + 1):
-            total = None
+            total = sums(SUM_BASE[level] + r - first) if has_own(level, r) else None
             for index in range(FIRST, LAST[level] + 1):
                 k = r - 2 * index + 2
                 if 0 <= k < TAPS:
-                    term = low[k] * smooth[index] + high[k] * sharp[index]
-                    total = term if total is None else total + term
+                    if index in smooth:
+                        total = add_term(total, low[k] * smooth[index])
+                    if index in sharp:
+                        total = add_term(total, high[k] * sharp[index])
             out[r] = masked(total, r, OWN[level - 1], flags) if level else total
         rows = out
     return rows
@@ -373,20 +408,22 @@
 GOT = {(0, -1): 0, (0, 8): 1, (1, -1): 2, (1, 4): 3, (1, 5): 4, (2, -1): 5, (2, 2): 6, (2, 3): 7, (3, -1): 8, (3, 1): 9}
 
 
-def pick_at(own_ref, got_ref, far_ref, at):
-    table = {}
-    for level in range(LEVELS):
-        for index in range(FIRST, LAST[level] + 1):
-            if 0 <= index < OWN[level]:
-                table[slot(level, index)] = (own_ref, OWN_BASE[level] + index)
-            elif (level, index) in GOT:
-                table[slot(level, index)] = (got_ref, GOT[level, index])
-            else:
-                table[slot(level, index)] = (far_ref, 0)
+def pick_at(got_ref, far_ref, at):
+    table = {slot(level, index): (got_ref, place) for (level, index), place in GOT.items()}
+    table[slot(3, 2)] = (far_ref, 0)
 
     def pick(place):
         ref, i = table[place]
         return ref[i, at, 0:128], ref[i, at, 128:256]
+
+    return pick
+
+
+def own_at(own_ref, at):
+    def pick(place):
+        level = max(i for i in range(LEVELS) if BASE[i] <= place)
+        i = OWN_BASE[level] + place - slot(level, 0)
+        return own_ref[i, at, 0:128], own_ref[i, at, 128:256]
 
     return pick
 
@@ -495,7 +532,8 @@
     put_one(side_out_ref, 3, with_far(part(side_in_ref, 3), y3_other))
 
 
-def spread_kernel(w0_ref, w_ref, ww_ref, y0c_ref, y1c_ref, y0_ref, y1_ref, y1b_ref, y2_ref, y3_ref, own_ref):
+def spread_kernel(filt_ref, w0_ref, w_ref, ww_ref, y0c_ref, y1c_ref, y0_ref, y1_ref, y1b_ref, y2_ref, y3_ref, sums_ref,
+                  own_ref):
     level0 = [y0_ref[i // 7] if i in (0, 7) else y0c_ref[i - 1] for i in range(8)]
     level1 = [y1_ref[:, 0:128], y1_ref[:, 128:256], y1c_ref[...], y1b_ref[...]]
     level2 = [y2_ref[:, 0:128], y2_ref[:, 128:256]]
@@ -504,6 +542,14 @@
         wide += spread_other(level, values, w_ref, ww_ref)
     for i, values in enumerate(wide):
         own_ref[i] = values
+
+    def chunk(c, carry):
+        at = pl.ds(pl.multiple_of(c * 16, 16), 16)
+        for place, total in own_sums(own_at(own_ref, at), filt_ref).items():
+            sums_ref[place, at, :] = total
+        return carry
+
+    lax.fori_loop(0, 9, chunk, 0)
 
 
 def received_kernel(w0_ref, w_ref, ww_ref, mate_ref, side_ref, got_ref):
@@ -523,20 +569,20 @@
     far_ref[0] = spread_other(3, [value], w_ref, ww_ref)[0]
 
 
-def middle_kernel(filt_ref, w_ref, ww_ref, own_ref, got_ref, side_ref, passed_ref, hi_ref, lo_ref, far_ref):
+def middle_kernel(filt_ref, w_ref, ww_ref, sums_ref, got_ref, side_ref, passed_ref, hi_ref, lo_ref, far_ref):
     flags = edge_flags()
     spread_coarse(side_ref, passed_ref, w_ref, ww_ref, far_ref)
 
     def chunk(c, carry):
         at = pl.ds(pl.multiple_of(c * 16, 16), 16)
-        rows = latitude_synthesis(pick_at(own_ref, got_ref, far_ref, at), filt_ref, flags)
+        rows = latitude_synthesis(pick_at(got_ref, far_ref, at), lambda i: sums_ref[i, at, :], filt_ref, flags)
         store_split(hi_ref, lo_ref, latitude_analysis(rows, filt_ref, flags), at)
         return carry
 
     lax.fori_loop(0, 9, chunk, 0)
 
 
-def last_kernel(filt_ref, w_ref, ww_ref, own_ref, got_ref, side_ref, passed_ref, out_hbm, far_ref, out_ref, sems):
+def last_kernel(filt_ref, w_ref, ww_ref, sums_ref, got_ref, side_ref, passed_ref, out_hbm, far_ref, out_ref, sems):
     flags = edge_flags()
     spread_coarse(side_ref, passed_ref, w_ref, ww_ref, far_ref)
 
@@ -546,7 +592,7 @@
 
     def chunk(c, carry):
         at = pl.ds(pl.multiple_of(c * 16, 16), 16)
-        rows = latitude_synthesis(pick_at(own_ref, got_ref, far_ref, at), filt_ref, flags)
+        rows = latitude_synthesis(pick_at(got_ref, far_ref, at), lambda i: sums_ref[i, at, :], filt_ref, flags)
         start = pl.multiple_of(c * (16 * ROWS), 16 * ROWS)
         for r, values in rows.items():
             out_ref[pl.ds(start + r, 16, stride=ROWS), :] = values
@@ -554,7 +600,8 @@
         return carry
 
     lax.fori_loop(0, 8, chunk, 0)
-    rows = latitude_synthesis(pick_at(own_ref, got_ref, far_ref, slice(128, 144)), filt_ref, flags)
+    end = slice(128, 144)
+    rows = latitude_synthesis(pick_at(got_ref, far_ref, end), lambda i: sums_ref[i, end, :], filt_ref, flags)
     for r, values in rows.items():
         out_ref[pl.ds(128 * ROWS + r, 8, stride=ROWS), :] = values[0:8]
         out_ref[136 * ROWS + r : 136 * ROWS + r + 1, :] = values[8:9]
@@ -590,7 +637,8 @@
 EDGES = (((2, PAD, 256), F32), ((PAD, 256), F32), ((PAD, LANES), F32), ((PAD, 256), F32))
 COARSEST = ((PAD, LANES), F32)
 INNER = (((6, PAD, 256), F32), ((PAD, LANES), F32))
-OWN_WIDE = ((15, PAD, 256), F32)
+OWN_SUMS = ((SUMS, PAD, LANES), F32)
+OWN_WIDE = pltpu.VMEM((15, PAD, 256), F32)
 GOT_WIDE = ((10, PAD, 256), F32)
 FAR_WIDE = pltpu.VMEM((1, PAD, 256), F32)
 
@@ -632,12 +680,13 @@
         (out,) = call(kernel, [VMEM, ANY], (((5, 2 * PAD, 256), BF16),), wide, 12)(band_roots, after)
         return out
 
-    def half(matrix, hi, lo, first):
+    def half(transposed, hi, lo):
         side, far = call(side_kernel, [VMEM] * 4, (MESSAGE, FAR), [], 12)(hi, lo, w0, w)
         (mate,) = call(mate_kernel, [VMEM] * 4 + [ANY], (MESSAGE,), [], 12)(hi, lo, w0, w, side)
         side, mate, far = swap(side, 1), swap(mate, 0), pass_up(far)
         *edges, c3, c3up = call(own_kernel, [VMEM] * 4, EDGES + (COARSEST, COARSEST), [], 12)(hi, lo, w0, w)
-        side, c3up = lax.optimization_barrier((side, c3up))
+        matrix = prepare(transposed, c3up)
+        side, matrix = lax.optimization_barrier((side, matrix))
         passed = swap(side[TAIL:], 0)
         *edges, mate_out, side_out = call(
             vertical_kernel, [VMEM] * 8, EDGES + (MESSAGE, MESSAGE), [], 12
@@ -647,19 +696,15 @@
         )
         side, mate = swap(side, 1), swap(mate, 0)
         y0c, y1c = call(inner_kernel, [VMEM] * 5 + [ANY], INNER, [], 12)(hi, lo, w0, w, matrix, y3)
-        turned = prepare(True, y3) if first else None
-        (own,) = call(spread_kernel, [VMEM] * 10, (OWN_WIDE,), [], 12)(w0, w, ww, y0c, y1c, *edges, y3)
-        if first:
-            side, own, turned = lax.optimization_barrier((side, own, turned))
-        else:
-            side, own = lax.optimization_barrier((side, own))
+        (own,) = call(spread_kernel, [VMEM] * 11, (OWN_SUMS,), [OWN_WIDE], 12)(filt, w0, w, ww, y0c, y1c, *edges, y3)
+        side, own = lax.optimization_barrier((side, own))
         passed = swap(side[END_TILE:], 0)
         (got,) = call(received_kernel, [VMEM] * 5, (GOT_WIDE,), [], 12)(w0, w, ww, mate, side)
-        return filt, w, ww, own, got, side, passed, turned
-
-    *ready, turned = half(prepare(False, hi), hi, lo, True)
+        return filt, w, ww, own, got, side, passed
+
+    ready = half(False, hi, lo)
     hi, lo = call(middle_kernel, [VMEM] * 7, HALVES, [FAR_WIDE], 12)(*ready)
-    *ready, _ = half(turned, hi, lo, False)
+    ready = half(True, hi, lo)
     (out,) = call(
         last_kernel, [VMEM] * 7, (((levels * rows, columns), F32),),
         [FAR_WIDE, pltpu.VMEM((levels * rows, columns), F32), pltpu.SemaphoreType.DMA((9,))], 12, HBM,

time: 72.2 us -> 76.8 us (1.064)
  the two profiles are of different devices: /device:TPU:1577 before, /device:TPU:1065 now
where the time goes in v4:
time: 76.8 us; the launch traced here: 76.5 us
  starting transfers between devices  46.6 us (61%)
  Pallas kernels  21 us (27%)
  waiting for transfers between devices  7.29 us (9%)
  local copies, waits for them, and re-layouts  1.14 us (1%)
    ppermute x12, starting transfers between devices, swap(): lax.ppermute(values, 'lat', [(i, partner.get(i, i)) for i in range(count)])  45.1 us
    ppermute x12, waiting for transfers between devices, swap(): lax.ppermute(values, 'lat', [(i, partner.get(i, i)) for i in range(count)])  7.29 us
    pallas_call x2, Pallas kernels, half(): call(inner_kernel, [VMEM] * 5 + [ANY], INNER, [], 12)  3.36 us
    pallas_call x2, Pallas kernels, half(): call(spread_kernel, [VMEM] * 11, (OWN_SUMS,), [OWN_WIDE], 12)  3.17 us
    pallas_call x1, Pallas kernels, on_device(): hi, lo = call(middle_kernel, [VMEM] * 7, HALVES, [FAR_WIDE], 12)(*ready)  2.34 us
    pallas_call x1, Pallas kernels, on_device(): call(last_kernel, [VMEM] * 7, (((levels * rows, columns), F32),), [FAR_WI...  1.79 us
    pallas_call x1, Pallas kernels, on_device(): hi, lo = call(first_kernel, [VMEM] * 2, HALVES, [], 12)(filt, flat)  1.57 us
  transfers between devices with their start and end apart: 14, of which 4 were waited for; matrix products, arithmetic and copies ran while one was open for 0% of the time, Pallas kernels for 15%

profile of v4, /device:TPU:1065, one launch (start us, length us, event | category | flops | bytes accessed | tf_op | source)
XLA Modules:
  0.0 76.5 jit_solution(15412748556224197150)
XLA Ops:
  0.0 0.8 %copy-done.2 = s32[4,2,2,5]{3,2,1,0:T(2,128)S(1)} copy-done((s32[4,2,2,5]{3,2,1,0:T(2,128)S(1)}, s32[4,2,2,5]{3,2,1,0:T(2,128)}, u32[]{:S(2)}) %copy-start.2) | copy-done | bytes 344
  0.8 1.4 %shard_map.37 = (f32[80,128]{1,0:T(8,128)S(1)}, bf16[256,512]{1,0:T(8,128)(2,1)S(1)}, bf16[3,256,256]{2,1,0:T(8,128)(2,1)S(1)}, bf16[3,256,256]{2,1,0:T(8,128)(2,1)S(1)}) custom-call(s32[4,2,2,5]{3,2,1,0:T(2,128)S(1)} %copy-done.2), custom_call_target="tpu_custom_call" | custom-call | flops 1000000000 | bytes 8388608 | tf_op jit(solution)/shard_map/pallas_call | solution.py:674
  2.2 1.6 %shard_map.38 = (bf16[26,144,256]{2,1,0:T(8,128)(2,1)S(1)}, bf16[26,144,256]{2,1,0:T(8,128)(2,1)S(1)}) custom-call(f32[80,128]{1,0:T(8,128)S(1)} %get-tuple-element.59.filt_ref, f32[2192,128]{1,0:T(8,128)S(1)} %bitcast.2), custom_call_target="tpu_custom_call" | custom-call | flops 1000000000 | bytes 8388608 | tf_op jit(solution)/shard_map/pallas_call | solution.py:675
  3.8 0.5 shard_map.39
  4.4 3.8 %collective-permute-start = (f32[552,128]{1,0:T(8,128)S(1)}, f32[552,128]{1,0:T(8,128)S(1)}, u32[]{:S(2)}, u32[]{:S(2)}) collective-permute-start(f32[552,128]{1,0:T(8,128)S(1)} %get-tuple-element.65.after_ref), channel_id=1, source_target_pairs={{0,0},{1,2},{2,1},{3,4},{4,3},{5,6},{6,5},{7,8},{8,7},{9,10},{10,9... | collective-permute-start | bytes 847880 | tf_op jit(solution)/shard_map/ppermute | solution.py:663
  8.2 0.5 shard_map.42
  8.7 0.0 copy-start.1
  8.7 0.2 collective-permute-start.2
  9.0 0.6 shard_map.40
  9.5 0.3 copy-done.1
  9.8 0.2 shard_map.41.m_ref
  10.0 2.4 %collective-permute-done.side_ref = f32[552,128]{1,0:T(8,128)S(1)} collective-permute-done((f32[552,128]{1,0:T(8,128)S(1)}, f32[552,128]{1,0:T(8,128)S(1)}, u32[]{:S(2)}, u32[]{:S(2)}) %collective-permute-start) | collective-permute-done | bytes 282656 | tf_op jit(solution)/shard_map/ppermute | solution.py:663
  12.4 3.9 %collective-permute-start.3 = (f32[280,128]{1,0:T(8,128)S(1)}, f32[280,128]{1,0:T(8,128)S(1)}, u32[]{:S(2)}, u32[]{:S(2)}) collective-permute-start(f32[280,128]{1,0:T(8,128)S(1)} %slice.12), channel_id=1, source_target_pairs={{0,1},{1,0},{2,3},{3,2},{4,5},{5,4},{6,7},{7,6},{8,9},{9,8},{10,11... | collective-permute-start | bytes 430088 | tf_op jit(solution)/shard_map/ppermute | solution.py:663
  16.4 0.7 collective-permute-start.1
  17.0 0.0 collective-permute-done.2.mate_ref
  17.0 0.6 shard_map.43
  17.7 0.0 collective-permute-done.1.far_ref
  17.7 0.5 shard_map.44
  18.2 6.0 %collective-permute-start.4 = (f32[552,128]{1,0:T(8,128)S(1)}, f32[552,128]{1,0:T(8,128)S(1)}, u32[]{:S(2)}, u32[]{:S(2)}) collective-permute-start(f32[552,128]{1,0:T(8,128)S(1)} %get-tuple-element.77), channel_id=1, source_target_pairs={{0,0},{1,2},{2,1},{3,4},{4,3},{5,6},{6,5},{7,8},{8,7},{9,10},{10,9... | collective-permute-start | bytes 847880 | tf_op jit(solution)/shard_map/ppermute | solution.py:663
  24.2 3.8 %collective-permute-start.5 = (f32[552,128]{1,0:T(8,128)S(1)}, f32[552,128]{1,0:T(8,128)S(1)}, u32[]{:S(2)}, u32[]{:S(2)}) collective-permute-start(f32[552,128]{1,0:T(8,128)S(1)} %get-tuple-element.86), channel_id=1, source_target_pairs={{0,1},{1,0},{2,3},{3,2},{4,5},{5,4},{6,7},{7,6},{8,9},{9,8},{10,11... | collective-permute-start | bytes 847880 | tf_op jit(solution)/shard_map/ppermute | solution.py:663
  28.0 1.7 %shard_map.45 = (f32[6,144,256]{2,1,0:T(8,128)S(1)}, f32[144,128]{1,0:T(8,128)S(1)}) custom-call(bf16[26,144,256]{2,1,0:T(8,128)(2,1)S(1)} %get-tuple-element.62.hi_ref, bf16[26,144,256]{2,1,0:T(8,128)(2,1)S(1)} %get-tuple-element.63.lo_ref, bf16[256,512]{1,0:T(8,128)(2,1)S(1)} %get-tuple-element.64.w0_ref, ...), custom_call_target="tpu_custom_call" | custom-call | flops 1000000000 | bytes 8388608 | tf_op jit(solution)/shard_map/pallas_call | solution.py:698
  29.7 1.6 %shard_map.46.sums_ref = f32[38,144,128]{2,1,0:T(8,128)S(1)} custom-call(f32[80,128]{1,0:T(8,128)S(1)} %get-tuple-element.59.filt_ref, bf16[256,512]{1,0:T(8,128)(2,1)S(1)} %get-tuple-element.64.w0_ref, bf16[3,256,256]{2,1,0:T(8,128)(2,1)S(1)} %get-tuple-element.60.w_ref, bf16[3,256,256]{2,1,0:T(8,128)(2,1)S(1)} %get-tuple-element.61.ww_ref, ...), custom_call_target="tpu_custom_call" | custom-call | flops 1000000000 | bytes 8388608 | tf_op jit(solution)/shard_map/pallas_call | solution.py:699
  31.3 0.0 collective-permute-done.4.side_ref
  31.3 5.9 %collective-permute-start.6 = (f32[144,128]{1,0:T(8,128)S(1)}, f32[144,128]{1,0:T(8,128)S(1)}, u32[]{:S(2)}, u32[]{:S(2)}) collective-permute-start(f32[144,128]{1,0:T(8,128)S(1)} %slice.13), channel_id=1, source_target_pairs={{0,1},{1,0},{2,3},{3,2},{4,5},{5,4},{6,7},{7,6},{8,9},{9,8},{10,11... | collective-permute-start | bytes 221192 | tf_op jit(solution)/shard_map/ppermute | solution.py:663
  37.2 0.0 collective-permute-done.5.mate_ref
  37.2 0.6 shard_map.47.got_ref
  37.9 0.3 collective-permute-done.6.passed_ref
  38.1 2.3 %shard_map.48 = (bf16[26,144,256]{2,1,0:T(8,128)(2,1)S(1)}, bf16[26,144,256]{2,1,0:T(8,128)(2,1)S(1)}) custom-call(f32[80,128]{1,0:T(8,128)S(1)} %get-tuple-element.59.filt_ref, bf16[3,256,256]{2,1,0:T(8,128)(2,1)S(1)} %get-tuple-element.60.w_ref, bf16[3,256,256]{2,1,0:T(8,128)(2,1)S(1)} %get-tuple-element.61.ww_ref, ...), custom_call_target="tpu_custom_call" | custom-call | flops 1000000000 | bytes 8388608 | tf_op jit(solution)/shard_map/pallas_call | solution.py:706
  40.5 0.5 shard_map.49
  41.0 2.0 %collective-permute-start.7 = (f32[552,128]{1,0:T(8,128)S(1)}, f32[552,128]{1,0:T(8,128)S(1)}, u32[]{:S(2)}, u32[]{:S(2)}) collective-permute-start(f32[552,128]{1,0:T(8,128)S(1)} %get-tuple-element.90.after_ref), channel_id=1, source_target_pairs={{0,0},{1,2},{2,1},{3,4},{4,3},{5,6},{6,5},{7,8},{8,7},{9,10},{10,9... | collective-permute-start | bytes 847880 | tf_op jit(solution)/shard_map/ppermute | solution.py:663
  43.0 0.5 shard_map.52
  43.5 0.5 collective-permute-start.9
  44.0 0.6 shard_map.50
  44.6 0.4 shard_map.51.m_ref
  45.0 4.3 %collective-permute-done.7.side_ref = f32[552,128]{1,0:T(8,128)S(1)} collective-permute-done((f32[552,128]{1,0:T(8,128)S(1)}, f32[552,128]{1,0:T(8,128)S(1)}, u32[]{:S(2)}, u32[]{:S(2)}) %collective-permute-start.7) | collective-permute-done | bytes 282656 | tf_op jit(solution)/shard_map/ppermute | solution.py:663
  49.3 3.5 %collective-permute-start.10 = (f32[280,128]{1,0:T(8,128)S(1)}, f32[280,128]{1,0:T(8,128)S(1)}, u32[]{:S(2)}, u32[]{:S(2)}) collective-permute-start(f32[280,128]{1,0:T(8,128)S(1)} %slice.14), channel_id=1, source_target_pairs={{0,1},{1,0},{2,3},{3,2},{4,5},{5,4},{6,7},{7,6},{8,9},{9,8},{10,11... | collective-permute-start | bytes 430088 | tf_op jit(solution)/shard_map/ppermute | solution.py:663
  52.8 0.8 %collective-permute-start.8 = (f32[40,128]{1,0:T(8,128)S(1)}, f32[40,128]{1,0:T(8,128)S(1)}, u32[]{:S(2)}, u32[]{:S(2)}) collective-permute-start(f32[40,128]{1,0:T(8,128)S(1)} %get-tuple-element.94), channel_id=1, source_target_pairs={{0,2},{2,4},{4,6},{6,8},{8,10},{10,12},{12,14},{14,16},{16,18},{18... | collective-permute-start | bytes 61448 | tf_op jit(solution)/shard_map/ppermute | solution.py:668
  53.6 0.6 shard_map.53
  54.3 0.0 collective-permute-done.10.passed_ref
  54.3 0.5 shard_map.54
  54.8 5.8 %collective-permute-start.11 = (f32[552,128]{1,0:T(8,128)S(1)}, f32[552,128]{1,0:T(8,128)S(1)}, u32[]{:S(2)}, u32[]{:S(2)}) collective-permute-start(f32[552,128]{1,0:T(8,128)S(1)} %get-tuple-element.102), channel_id=1, source_target_pairs={{0,0},{1,2},{2,1},{3,4},{4,3},{5,6},{6,5},{7,8},{8,7},{9,10},{10,9... | collective-permute-start | bytes 847880 | tf_op jit(solution)/shard_map/ppermute | solution.py:663
  60.6 3.8 %collective-permute-start.12 = (f32[552,128]{1,0:T(8,128)S(1)}, f32[552,128]{1,0:T(8,128)S(1)}, u32[]{:S(2)}, u32[]{:S(2)}) collective-permute-start(f32[552,128]{1,0:T(8,128)S(1)} %get-tuple-element.111), channel_id=1, source_target_pairs={{0,1},{1,0},{2,3},{3,2},{4,5},{5,4},{6,7},{7,6},{8,9},{9,8},{10,11... | collective-permute-start | bytes 847880 | tf_op jit(solution)/shard_map/ppermute | solution.py:663
  64.4 1.7 %shard_map.55 = (f32[6,144,256]{2,1,0:T(8,128)S(1)}, f32[144,128]{1,0:T(8,128)S(1)}) custom-call(bf16[26,144,256]{2,1,0:T(8,128)(2,1)S(1)} %get-tuple-element.88.hi_ref, bf16[26,144,256]{2,1,0:T(8,128)(2,1)S(1)} %get-tuple-element.89.lo_ref, bf16[256,512]{1,0:T(8,128)(2,1)S(1)} %get-tuple-element.64.w0_ref, ...), custom_call_target="tpu_custom_call" | custom-call | flops 1000000000 | bytes 8388608 | tf_op jit(solution)/shard_map/pallas_call | solution.py:698
  66.1 1.6 %shard_map.56.sums_ref = f32[38,144,128]{2,1,0:T(8,128)S(1)} custom-call(f32[80,128]{1,0:T(8,128)S(1)} %get-tuple-element.59.filt_ref, bf16[256,512]{1,0:T(8,128)(2,1)S(1)} %get-tuple-element.64.w0_ref, bf16[3,256,256]{2,1,0:T(8,128)(2,1)S(1)} %get-tuple-element.60.w_ref, bf16[3,256,256]{2,1,0:T(8,128)(2,1)S(1)} %get-tuple-element.61.ww_ref, ...), custom_call_target="tpu_custom_call" | custom-call | flops 1000000000 | bytes 8388608 | tf_op jit(solution)/shard_map/pallas_call | solution.py:699
  67.7 5.9 %collective-permute-start.13 = (f32[144,128]{1,0:T(8,128)S(1)}, f32[144,128]{1,0:T(8,128)S(1)}, u32[]{:S(2)}, u32[]{:S(2)}) collective-permute-start(f32[144,128]{1,0:T(8,128)S(1)} %slice.15), channel_id=1, source_target_pairs={{0,1},{1,0},{2,3},{3,2},{4,5},{5,4},{6,7},{7,6},{8,9},{9,8},{10,11... | collective-permute-start | bytes 221192 | tf_op jit(solution)/shard_map/ppermute | solution.py:663
  73.6 0.6 shard_map.57.got_ref
  74.3 0.3 collective-permute-done.13.passed_ref
  74.5 1.8 %shard_map.58 = f32[2192,128]{1,0:T(8,128)} custom-call(f32[80,128]{1,0:T(8,128)S(1)} %get-tuple-element.59.filt_ref, bf16[3,256,256]{2,1,0:T(8,128)(2,1)S(1)} %get-tuple-element.60.w_ref, bf16[3,256,256]{2,1,0:T(8,128)(2,1)S(1)} %get-tuple-element.61.ww_ref, f32[38,144,128]{2,1,0:T(8,128)S(1)} %shard_map.56.sums_ref, ...), custom_call_target="tpu_custom_call" | custom-call | flops 1000000000 | bytes 8388608 | tf_op jit(solution)/shard_map/pallas_call | solution.py:708
  (12 shorter events, 0.1 us)
Async XLA Ops:
  0.0 2.2 %copy-start = (f32[137,16,128]{2,1,0:T(8,128)S(1)}, f32[137,16,128]{2,1,0:T(8,128)}, u32[]{:S(2)}) copy-start(f32[137,16,128]{2,1,0:T(8,128)} %param.3) | copy-start | bytes 3366916
  0.0 0.8 %copy-start.2 = (s32[4,2,2,5]{3,2,1,0:T(2,128)S(1)}, s32[4,2,2,5]{3,2,1,0:T(2,128)}, u32[]{:S(2)}) copy-start(s32[4,2,2,5]{3,2,1,0:T(2,128)} %taps_ref.1) | copy-start | bytes 964
  4.4 8.1 %collective-permute-start = (f32[552,128]{1,0:T(8,128)S(1)}, f32[552,128]{1,0:T(8,128)S(1)}, u32[]{:S(2)}, u32[]{:S(2)}) collective-permute-start(f32[552,128]{1,0:T(8,128)S(1)} %get-tuple-element.65.after_ref), channel_id=1, source_target_pairs={{0,0},{1,2},{2,1},{3,4},{4,3},{5,6},{6,5},{7,8},{8,7},{9,10},{10,9... | collective-permute-start | bytes 847880 | tf_op jit(solution)/shard_map/ppermute | solution.py:663
  8.7 1.1 %copy-start.1 = (f32[5,137,137]{2,1,0:T(8,128)S(1)}, f32[5,137,137]{2,1,0:T(8,128)}, u32[]{:S(2)}) copy-start(f32[5,137,137]{2,1,0:T(8,128)} %m_ref.3) | copy-start | bytes 1126144
  8.7 8.3 %collective-permute-start.2 = (f32[552,128]{1,0:T(8,128)S(1)}, f32[552,128]{1,0:T(8,128)S(1)}, u32[]{:S(2)}, u32[]{:S(2)}) collective-permute-start(f32[552,128]{1,0:T(8,128)S(1)} %shard_map.42), channel_id=1, source_target_pairs={{0,1},{1,0},{2,3},{3,2},{4,5},{5,4},{6,7},{7,6},{8,9},{9,8},{10,11... | collective-permute-start | bytes 847880 | tf_op jit(solution)/shard_map/ppermute | solution.py:663
  12.4 5.3 %collective-permute-start.3 = (f32[280,128]{1,0:T(8,128)S(1)}, f32[280,128]{1,0:T(8,128)S(1)}, u32[]{:S(2)}, u32[]{:S(2)}) collective-permute-start(f32[280,128]{1,0:T(8,128)S(1)} %slice.12), channel_id=1, source_target_pairs={{0,1},{1,0},{2,3},{3,2},{4,5},{5,4},{6,7},{7,6},{8,9},{9,8},{10,11... | collective-permute-start | bytes 430088 | tf_op jit(solution)/shard_map/ppermute | solution.py:663
  16.4 1.3 %collective-permute-start.1 = (f32[40,128]{1,0:T(8,128)S(1)}, f32[40,128]{1,0:T(8,128)S(1)}, u32[]{:S(2)}, u32[]{:S(2)}) collective-permute-start(f32[40,128]{1,0:T(8,128)S(1)} %get-tuple-element.69), channel_id=1, source_target_pairs={{0,2},{2,4},{4,6},{6,8},{8,10},{10,12},{12,14},{14,16},{16,18},{18... | collective-permute-start | bytes 61448 | tf_op jit(solution)/shard_map/ppermute | solution.py:668
  18.2 13.1 %collective-permute-start.4 = (f32[552,128]{1,0:T(8,128)S(1)}, f32[552,128]{1,0:T(8,128)S(1)}, u32[]{:S(2)}, u32[]{:S(2)}) collective-permute-start(f32[552,128]{1,0:T(8,128)S(1)} %get-tuple-element.77), channel_id=1, source_target_pairs={{0,0},{1,2},{2,1},{3,4},{4,3},{5,6},{6,5},{7,8},{8,7},{9,10},{10,9... | collective-permute-start | bytes 847880 | tf_op jit(solution)/shard_map/ppermute | solution.py:663
  24.2 13.0 %collective-permute-start.5 = (f32[552,128]{1,0:T(8,128)S(1)}, f32[552,128]{1,0:T(8,128)S(1)}, u32[]{:S(2)}, u32[]{:S(2)}) collective-permute-start(f32[552,128]{1,0:T(8,128)S(1)} %get-tuple-element.86), channel_id=1, source_target_pairs={{0,1},{1,0},{2,3},{3,2},{4,5},{5,4},{6,7},{7,6},{8,9},{9,8},{10,11... | collective-permute-start | bytes 847880 | tf_op jit(solution)/shard_map/ppermute | solution.py:663
  31.3 6.8 %collective-permute-start.6 = (f32[144,128]{1,0:T(8,128)S(1)}, f32[144,128]{1,0:T(8,128)S(1)}, u32[]{:S(2)}, u32[]{:S(2)}) collective-permute-start(f32[144,128]{1,0:T(8,128)S(1)} %slice.13), channel_id=1, source_target_pairs={{0,1},{1,0},{2,3},{3,2},{4,5},{5,4},{6,7},{7,6},{8,9},{9,8},{10,11... | collective-permute-start | bytes 221192 | tf_op jit(solution)/shard_map/ppermute | solution.py:663
  41.0 8.2 %collective-permute-start.7 = (f32[552,128]{1,0:T(8,128)S(1)}, f32[552,128]{1,0:T(8,128)S(1)}, u32[]{:S(2)}, u32[]{:S(2)}) collective-permute-start(f32[552,128]{1,0:T(8,128)S(1)} %get-tuple-element.90.after_ref), channel_id=1, source_target_pairs={{0,0},{1,2},{2,1},{3,4},{4,3},{5,6},{6,5},{7,8},{8,7},{9,10},{10,9... | collective-permute-start | bytes 847880 | tf_op jit(solution)/shard_map/ppermute | solution.py:663
  43.5 10.1 %collective-permute-start.9 = (f32[552,128]{1,0:T(8,128)S(1)}, f32[552,128]{1,0:T(8,128)S(1)}, u32[]{:S(2)}, u32[]{:S(2)}) collective-permute-start(f32[552,128]{1,0:T(8,128)S(1)} %shard_map.52), channel_id=1, source_target_pairs={{0,1},{1,0},{2,3},{3,2},{4,5},{5,4},{6,7},{7,6},{8,9},{9,8},{10,11... | collective-permute-start | bytes 847880 | tf_op jit(solution)/shard_map/ppermute | solution.py:663
  49.3 5.0 %collective-permute-start.10 = (f32[280,128]{1,0:T(8,128)S(1)}, f32[280,128]{1,0:T(8,128)S(1)}, u32[]{:S(2)}, u32[]{:S(2)}) collective-permute-start(f32[280,128]{1,0:T(8,128)S(1)} %slice.14), channel_id=1, source_target_pairs={{0,1},{1,0},{2,3},{3,2},{4,5},{5,4},{6,7},{7,6},{8,9},{9,8},{10,11... | collective-permute-start | bytes 430088 | tf_op jit(solution)/shard_map/ppermute | solution.py:663
  52.8 1.5 %collective-permute-start.8 = (f32[40,128]{1,0:T(8,128)S(1)}, f32[40,128]{1,0:T(8,128)S(1)}, u32[]{:S(2)}, u32[]{:S(2)}) collective-permute-start(f32[40,128]{1,0:T(8,128)S(1)} %get-tuple-element.94), channel_id=1, source_target_pairs={{0,2},{2,4},{4,6},{6,8},{8,10},{10,12},{12,14},{14,16},{16,18},{18... | collective-permute-start | bytes 61448 | tf_op jit(solution)/shard_map/ppermute | solution.py:668
  54.8 12.9 %collective-permute-start.11 = (f32[552,128]{1,0:T(8,128)S(1)}, f32[552,128]{1,0:T(8,128)S(1)}, u32[]{:S(2)}, u32[]{:S(2)}) collective-permute-start(f32[552,128]{1,0:T(8,128)S(1)} %get-tuple-element.102), channel_id=1, source_target_pairs={{0,0},{1,2},{2,1},{3,4},{4,3},{5,6},{6,5},{7,8},{8,7},{9,10},{10,9... | collective-permute-start | bytes 847880 | tf_op jit(solution)/shard_map/ppermute | solution.py:663
  60.6 13.0 %collective-permute-start.12 = (f32[552,128]{1,0:T(8,128)S(1)}, f32[552,128]{1,0:T(8,128)S(1)}, u32[]{:S(2)}, u32[]{:S(2)}) collective-permute-start(f32[552,128]{1,0:T(8,128)S(1)} %get-tuple-element.111), channel_id=1, source_target_pairs={{0,1},{1,0},{2,3},{3,2},{4,5},{5,4},{6,7},{7,6},{8,9},{9,8},{10,11... | collective-permute-start | bytes 847880 | tf_op jit(solution)/shard_map/ppermute | solution.py:663
  67.7 6.8 %collective-permute-start.13 = (f32[144,128]{1,0:T(8,128)S(1)}, f32[144,128]{1,0:T(8,128)S(1)}, u32[]{:S(2)}, u32[]{:S(2)}) collective-permute-start(f32[144,128]{1,0:T(8,128)S(1)} %slice.15), channel_id=1, source_target_pairs={{0,1},{1,0},{2,3},{3,2},{4,5},{5,4},{6,7},{7,6},{8,9},{9,8},{10,11... | collective-permute-start | bytes 221192 | tf_op jit(solution)/shard_map/ppermute | solution.py:663

commit v5 on v4

--- a/solution.py
+++ b/solution.py
@@ -221,13 +221,13 @@
 
 def pack(c0, c1, c2, c3, c1b, c2b, c3b=None):
     lane = lane_ids(PAD)
-    last = jnp.where(lane < 64, c1b, pltpu.roll(c2b, 96, 1))
+    last = jnp.where(lane < 64, c1b, pltpu.roll(c3, 96, 1))
     if c3b is not None:
         last = with_far(last, c3b)
     return [
         c0[:, 0:128],
         jnp.where(lane < 64, c0[:, 128:256], jnp.where(lane < 112, pltpu.roll(c2, 64, 1), pltpu.roll(c2b, 80, 1))),
-        jnp.where(lane < 96, c1, pltpu.roll(c3, 96, 1)),
+        jnp.where(lane < 96, c1, pltpu.roll(c2b, 96, 1)),
         last,
     ]
 
@@ -246,12 +246,10 @@
         jnp.concatenate([tiles[0], tiles[1]], axis=1),
         tiles[2],
         pltpu.roll(tiles[1], 64, 1),
-        pltpu.roll(tiles[2], 32, 1),
+        pltpu.roll(tiles[3], 32, 1),
     ]
-    if len(tiles) > 3:
-        lane = lane_ids(PAD)
-        parts += [tiles[3], jnp.where(lane < 32, pltpu.roll(tiles[3], 32, 1), pltpu.roll(tiles[1], 48, 1))]
-    return parts
+    second = jnp.where(lane_ids(PAD) < 32, pltpu.roll(tiles[2], 32, 1), pltpu.roll(tiles[1], 48, 1))
+    return parts + [tiles[3], second]
 
 
 def three_bands(tile, filt_ref):
@@ -293,10 +291,9 @@
 
 
 MAIN = 136
-ORDERED = (0, 1, 3, 2)
+ORDERED = (0, 1, 2, 3)
 ENDS = 4 * MAIN
-TAIL = 2 * MAIN
-END_TILE = 3 * MAIN
+TAIL = 3 * MAIN
 
 
 def join(main, end):
@@ -483,7 +480,7 @@
 
 def vertical_kernel(m_ref, filt_ref, c0_ref, c1_ref, c1b_ref, c2_ref, mate_ref, side_ref,
                     y0_ref, y1_ref, y1b_ref, y2_ref, mate_out_ref, side_out_ref):
-    below, above = received(mate_ref, side_ref, 4, 3)
+    below, above = received(mate_ref, side_ref, 4, 4)
     below, above = unpack(below), unpack(above)
     c2 = c2_ref[...]
     y2 = apply_vertical(m_ref, 2, jnp.concatenate([c2[:, 0:128] + below[2], c2[:, 128:256] + below[5] + above[2]], axis=1))
@@ -512,12 +509,12 @@
     place = lax.axis_index("lat")
     last = lax.axis_size("lat") - 1
     lane = lane_ids(PAD)
-    from_side = jnp.where((place == 0) | (place == last), 0.0, pltpu.roll(part(side_ref, 2), 32, 1))
+    from_side = jnp.where((place == 0) | (place == last), 0.0, pltpu.roll(part(side_ref, 3), 32, 1))
     passed = far_of(part(passed_ref, 3, TAIL))
     passed = jnp.where(even, unpack_coarse(far_ref[...]), jnp.where(place == 1, 0.0, passed))
-    mine = c3_ref[...] + pltpu.roll(part(mate_ref, 2), 32, 1) + from_side + passed
+    mine = c3_ref[...] + pltpu.roll(part(mate_ref, 3), 32, 1) + from_side + passed
     coarse = jnp.where(place == 0, 0.0, far_of(part(side_ref, 3)))
-    above = jnp.where(place == last - 1, 0.0, pltpu.roll(part(passed_ref, 2, TAIL), 32, 1))
+    above = jnp.where(place == last - 1, 0.0, pltpu.roll(part(passed_ref, 3, TAIL), 32, 1))
     other = far_of(part(mate_ref, 3)) + c3up_ref[...] + coarse + above
     both = jnp.concatenate([mine, other], axis=1)
     detail, smooth = apply_vertical(m_ref, 3, both), apply_vertical(m_ref, 4, both)
@@ -525,11 +522,10 @@
     y3_ref[...] = y3
     moved = pltpu.roll(y3, 96, 1)
     mate_out_ref[...] = mate_in_ref[...]
-    put_one(mate_out_ref, 2, jnp.where(lane < 96, part(mate_in_ref, 2), moved))
+    put_one(mate_out_ref, 3, jnp.where(lane < 96, part(mate_in_ref, 3), moved))
     side_out_ref[...] = side_in_ref[...]
-    put_one(side_out_ref, 2, jnp.where(lane < 96, part(side_in_ref, 2), moved))
     y3_other = jnp.where(lane < 24, detail[:, 128:256], smooth[:, 128:256])
-    put_one(side_out_ref, 3, with_far(part(side_in_ref, 3), y3_other))
+    put_one(side_out_ref, 3, with_far(jnp.where(lane < 96, part(side_in_ref, 3), moved), y3_other))
 
 
 def spread_kernel(filt_ref, w0_ref, w_ref, ww_ref, y0c_ref, y1c_ref, y0_ref, y1_ref, y1b_ref, y2_ref, y3_ref, sums_ref,
@@ -553,7 +549,7 @@
 
 
 def received_kernel(w0_ref, w_ref, ww_ref, mate_ref, side_ref, got_ref):
-    below, above = received(mate_ref, side_ref, 3, 4)
+    below, above = received(mate_ref, side_ref, 4, 4)
     below, above = unpack(below), unpack(above)
     wide = spread_level0([below[0], above[0]], w0_ref)
     wide += spread_other(1, [below[1], above[1], bands_of_sums(above[4])], w_ref, ww_ref)
@@ -564,7 +560,7 @@
 
 
 def spread_coarse(side_ref, passed_ref, w_ref, ww_ref, far_ref):
-    value = jnp.where(is_even(), pltpu.roll(part(passed_ref, 2, END_TILE), 32, 1), far_of(part(side_ref, 3)))
+    value = jnp.where(is_even(), pltpu.roll(part(passed_ref, 3, TAIL), 32, 1), far_of(part(side_ref, 3)))
     value = jnp.where(lax.axis_index("lat") >= lax.axis_size("lat") - 2, 0.0, value)
     far_ref[0] = spread_other(3, [value], w_ref, ww_ref)[0]
 
@@ -698,7 +694,7 @@
         y0c, y1c = call(inner_kernel, [VMEM] * 5 + [ANY], INNER, [], 12)(hi, lo, w0, w, matrix, y3)
         (own,) = call(spread_kernel, [VMEM] * 11, (OWN_SUMS,), [OWN_WIDE], 12)(filt, w0, w, ww, y0c, y1c, *edges, y3)
         side, own = lax.optimization_barrier((side, own))
-        passed = swap(side[END_TILE:], 0)
+        passed = swap(side[TAIL:], 0)
         (got,) = call(received_kernel, [VMEM] * 5, (GOT_WIDE,), [], 12)(w0, w, ww, mate, side)
         return filt, w, ww, own, got, side, passed
 

time: 76.8 us -> 63.7 us (0.83)
  the two profiles are of different devices: /device:TPU:1065 before, /device:TPU:1569 now
where the time goes in v5:
time: 63.7 us; the launch traced here: 63.4 us
  starting transfers between devices  35.3 us (55%)
  Pallas kernels  21 us (33%)
  waiting for transfers between devices  5.89 us (9%)
  local copies, waits for them, and re-layouts  0.82 us (1%)
    ppermute x12, starting transfers between devices, swap(): lax.ppermute(values, 'lat', [(i, partner.get(i, i)) for i in range(count)])  33.9 us
    ppermute x12, waiting for transfers between devices, swap(): lax.ppermute(values, 'lat', [(i, partner.get(i, i)) for i in range(count)])  5.89 us
    pallas_call x2, Pallas kernels, half(): call(inner_kernel, [VMEM] * 5 + [ANY], INNER, [], 12)  3.36 us
    pallas_call x2, Pallas kernels, half(): call(spread_kernel, [VMEM] * 11, (OWN_SUMS,), [OWN_WIDE], 12)  3.17 us
    pallas_call x1, Pallas kernels, on_device(): hi, lo = call(middle_kernel, [VMEM] * 7, HALVES, [FAR_WIDE], 12)(*ready)  2.33 us
    pallas_call x1, Pallas kernels, on_device(): call(last_kernel, [VMEM] * 7, (((levels * rows, columns), F32),), [FAR_WI...  1.79 us
    pallas_call x1, Pallas kernels, on_device(): hi, lo = call(first_kernel, [VMEM] * 2, HALVES, [], 12)(filt, flat)  1.57 us
    ppermute x2, starting transfers between devices, pass_up(): lax.ppermute(values, 'lat', [(i, i + 2) for i in range(0, count - 2, 2)])  1.43 us
  transfers between devices with their start and end apart: 14, of which 6 were waited for; matrix products, arithmetic and copies ran while one was open for 0% of the time, Pallas kernels for 18%

profile of v5, /device:TPU:1569, one launch (start us, length us, event | category | flops | bytes accessed | tf_op | source)
XLA Modules:
  0.0 63.4 jit_solution(347567912756874495)
XLA Ops:
  0.0 0.8 %copy-done.2 = s32[4,2,2,5]{3,2,1,0:T(2,128)S(1)} copy-done((s32[4,2,2,5]{3,2,1,0:T(2,128)S(1)}, s32[4,2,2,5]{3,2,1,0:T(2,128)}, u32[]{:S(2)}) %copy-start.2) | copy-done | bytes 344
  0.8 1.4 %shard_map.37 = (f32[80,128]{1,0:T(8,128)S(1)}, bf16[256,512]{1,0:T(8,128)(2,1)S(1)}, bf16[3,256,256]{2,1,0:T(8,128)(2,1)S(1)}, bf16[3,256,256]{2,1,0:T(8,128)(2,1)S(1)}) custom-call(s32[4,2,2,5]{3,2,1,0:T(2,128)S(1)} %copy-done.2), custom_call_target="tpu_custom_call" | custom-call | flops 1000000000 | bytes 8388608 | tf_op jit(solution)/shard_map/pallas_call | solution.py:670
  2.2 1.6 %shard_map.38 = (bf16[26,144,256]{2,1,0:T(8,128)(2,1)S(1)}, bf16[26,144,256]{2,1,0:T(8,128)(2,1)S(1)}) custom-call(f32[80,128]{1,0:T(8,128)S(1)} %get-tuple-element.59.filt_ref, f32[2192,128]{1,0:T(8,128)S(1)} %bitcast.2), custom_call_target="tpu_custom_call" | custom-call | flops 1000000000 | bytes 8388608 | tf_op jit(solution)/shard_map/pallas_call | solution.py:671
  3.8 0.5 shard_map.39
  4.4 3.8 %collective-permute-start = (f32[552,128]{1,0:T(8,128)S(1)}, f32[552,128]{1,0:T(8,128)S(1)}, u32[]{:S(2)}, u32[]{:S(2)}) collective-permute-start(f32[552,128]{1,0:T(8,128)S(1)} %get-tuple-element.65.after_ref), channel_id=1, source_target_pairs={{0,0},{1,2},{2,1},{3,4},{4,3},{5,6},{6,5},{7,8},{8,7},{9,10},{10,9... | collective-permute-start | bytes 847880 | tf_op jit(solution)/shard_map/ppermute | solution.py:659
  8.2 0.5 shard_map.42
  8.7 2.4 %collective-permute-start.2 = (f32[552,128]{1,0:T(8,128)S(1)}, f32[552,128]{1,0:T(8,128)S(1)}, u32[]{:S(2)}, u32[]{:S(2)}) collective-permute-start(f32[552,128]{1,0:T(8,128)S(1)} %shard_map.42), channel_id=1, source_target_pairs={{0,1},{1,0},{2,3},{3,2},{4,5},{5,4},{6,7},{7,6},{8,9},{9,8},{10,11... | collective-permute-start | bytes 847880 | tf_op jit(solution)/shard_map/ppermute | solution.py:659
  11.1 0.8 %collective-permute-start.1 = (f32[40,128]{1,0:T(8,128)S(1)}, f32[40,128]{1,0:T(8,128)S(1)}, u32[]{:S(2)}, u32[]{:S(2)}) collective-permute-start(f32[40,128]{1,0:T(8,128)S(1)} %get-tuple-element.69), channel_id=1, source_target_pairs={{0,2},{2,4},{4,6},{6,8},{8,10},{10,12},{12,14},{14,16},{16,18},{18... | collective-permute-start | bytes 61448 | tf_op jit(solution)/shard_map/ppermute | solution.py:664
  11.8 0.6 shard_map.40
  12.4 0.2 shard_map.41.m_ref
  12.6 0.0 collective-permute-done.side_ref
  12.6 3.6 %collective-permute-start.3 = (f32[144,128]{1,0:T(8,128)S(1)}, f32[144,128]{1,0:T(8,128)S(1)}, u32[]{:S(2)}, u32[]{:S(2)}) collective-permute-start(f32[144,128]{1,0:T(8,128)S(1)} %slice.12), channel_id=1, source_target_pairs={{0,1},{1,0},{2,3},{3,2},{4,5},{5,4},{6,7},{7,6},{8,9},{9,8},{10,11... | collective-permute-start | bytes 221192 | tf_op jit(solution)/shard_map/ppermute | solution.py:659
  16.2 0.0 collective-permute-done.2.mate_ref
  16.2 0.6 shard_map.43
  16.9 0.0 collective-permute-done.1.far_ref
  16.9 0.3 collective-permute-done.3.passed_ref
  17.2 0.5 shard_map.44
  17.7 2.0 %collective-permute-start.4 = (f32[552,128]{1,0:T(8,128)S(1)}, f32[552,128]{1,0:T(8,128)S(1)}, u32[]{:S(2)}, u32[]{:S(2)}) collective-permute-start(f32[552,128]{1,0:T(8,128)S(1)} %get-tuple-element.77), channel_id=1, source_target_pairs={{0,0},{1,2},{2,1},{3,4},{4,3},{5,6},{6,5},{7,8},{8,7},{9,10},{10,9... | collective-permute-start | bytes 847880 | tf_op jit(solution)/shard_map/ppermute | solution.py:659
  19.6 3.9 %collective-permute-start.5 = (f32[552,128]{1,0:T(8,128)S(1)}, f32[552,128]{1,0:T(8,128)S(1)}, u32[]{:S(2)}, u32[]{:S(2)}) collective-permute-start(f32[552,128]{1,0:T(8,128)S(1)} %get-tuple-element.86), channel_id=1, source_target_pairs={{0,1},{1,0},{2,3},{3,2},{4,5},{5,4},{6,7},{7,6},{8,9},{9,8},{10,11... | collective-permute-start | bytes 847880 | tf_op jit(solution)/shard_map/ppermute | solution.py:659
  23.6 1.7 %shard_map.45 = (f32[6,144,256]{2,1,0:T(8,128)S(1)}, f32[144,128]{1,0:T(8,128)S(1)}) custom-call(bf16[26,144,256]{2,1,0:T(8,128)(2,1)S(1)} %get-tuple-element.62.hi_ref, bf16[26,144,256]{2,1,0:T(8,128)(2,1)S(1)} %get-tuple-element.63.lo_ref, bf16[256,512]{1,0:T(8,128)(2,1)S(1)} %get-tuple-element.64.w0_ref, ...), custom_call_target="tpu_custom_call" | custom-call | flops 1000000000 | bytes 8388608 | tf_op jit(solution)/shard_map/pallas_call | solution.py:694
  25.3 1.6 %shard_map.46.sums_ref = f32[38,144,128]{2,1,0:T(8,128)S(1)} custom-call(f32[80,128]{1,0:T(8,128)S(1)} %get-tuple-element.59.filt_ref, bf16[256,512]{1,0:T(8,128)(2,1)S(1)} %get-tuple-element.64.w0_ref, bf16[3,256,256]{2,1,0:T(8,128)(2,1)S(1)} %get-tuple-element.60.w_ref, bf16[3,256,256]{2,1,0:T(8,128)(2,1)S(1)} %get-tuple-element.61.ww_ref, ...), custom_call_target="tpu_custom_call" | custom-call | flops 1000000000 | bytes 8388608 | tf_op jit(solution)/shard_map/pallas_call | solution.py:695
  26.8 0.0 collective-permute-done.4.side_ref
  26.9 5.2 %collective-permute-start.6 = (f32[144,128]{1,0:T(8,128)S(1)}, f32[144,128]{1,0:T(8,128)S(1)}, u32[]{:S(2)}, u32[]{:S(2)}) collective-permute-start(f32[144,128]{1,0:T(8,128)S(1)} %slice.13), channel_id=1, source_target_pairs={{0,1},{1,0},{2,3},{3,2},{4,5},{5,4},{6,7},{7,6},{8,9},{9,8},{10,11... | collective-permute-start | bytes 221192 | tf_op jit(solution)/shard_map/ppermute | solution.py:659
  32.0 0.6 shard_map.47.got_ref
  32.7 0.3 collective-permute-done.6.passed_ref
  33.0 2.3 %shard_map.48 = (bf16[26,144,256]{2,1,0:T(8,128)(2,1)S(1)}, bf16[26,144,256]{2,1,0:T(8,128)(2,1)S(1)}) custom-call(f32[80,128]{1,0:T(8,128)S(1)} %get-tuple-element.59.filt_ref, bf16[3,256,256]{2,1,0:T(8,128)(2,1)S(1)} %get-tuple-element.60.w_ref, bf16[3,256,256]{2,1,0:T(8,128)(2,1)S(1)} %get-tuple-element.61.ww_ref, ...), custom_call_target="tpu_custom_call" | custom-call | flops 1000000000 | bytes 8388608 | tf_op jit(solution)/shard_map/pallas_call | solution.py:702
  35.3 0.5 shard_map.49
  35.9 2.0 %collective-permute-start.7 = (f32[552,128]{1,0:T(8,128)S(1)}, f32[552,128]{1,0:T(8,128)S(1)}, u32[]{:S(2)}, u32[]{:S(2)}) collective-permute-start(f32[552,128]{1,0:T(8,128)S(1)} %get-tuple-element.90.after_ref), channel_id=1, source_target_pairs={{0,0},{1,2},{2,1},{3,4},{4,3},{5,6},{6,5},{7,8},{8,7},{9,10},{10,9... | collective-permute-start | bytes 847880 | tf_op jit(solution)/shard_map/ppermute | solution.py:659
  37.8 0.5 shard_map.52
  38.4 1.2 %collective-permute-start.9 = (f32[552,128]{1,0:T(8,128)S(1)}, f32[552,128]{1,0:T(8,128)S(1)}, u32[]{:S(2)}, u32[]{:S(2)}) collective-permute-start(f32[552,128]{1,0:T(8,128)S(1)} %shard_map.52), channel_id=1, source_target_pairs={{0,1},{1,0},{2,3},{3,2},{4,5},{5,4},{6,7},{7,6},{8,9},{9,8},{10,11... | collective-permute-start | bytes 847880 | tf_op jit(solution)/shard_map/ppermute | solution.py:659
  39.5 0.7 %collective-permute-start.8 = (f32[40,128]{1,0:T(8,128)S(1)}, f32[40,128]{1,0:T(8,128)S(1)}, u32[]{:S(2)}, u32[]{:S(2)}) collective-permute-start(f32[40,128]{1,0:T(8,128)S(1)} %get-tuple-element.94), channel_id=1, source_target_pairs={{0,2},{2,4},{4,6},{6,8},{8,10},{10,12},{12,14},{14,16},{16,18},{18... | collective-permute-start | bytes 61448 | tf_op jit(solution)/shard_map/ppermute | solution.py:664
  40.2 0.6 shard_map.50
  40.8 0.4 shard_map.51.m_ref
  41.2 2.9 %collective-permute-done.7.side_ref = f32[552,128]{1,0:T(8,128)S(1)} collective-permute-done((f32[552,128]{1,0:T(8,128)S(1)}, f32[552,128]{1,0:T(8,128)S(1)}, u32[]{:S(2)}, u32[]{:S(2)}) %collective-permute-start.7) | collective-permute-done | bytes 282656 | tf_op jit(solution)/shard_map/ppermute | solution.py:659
  44.1 3.4 %collective-permute-start.10 = (f32[144,128]{1,0:T(8,128)S(1)}, f32[144,128]{1,0:T(8,128)S(1)}, u32[]{:S(2)}, u32[]{:S(2)}) collective-permute-start(f32[144,128]{1,0:T(8,128)S(1)} %slice.14), channel_id=1, source_target_pairs={{0,1},{1,0},{2,3},{3,2},{4,5},{5,4},{6,7},{7,6},{8,9},{9,8},{10,11... | collective-permute-start | bytes 221192 | tf_op jit(solution)/shard_map/ppermute | solution.py:659
  47.5 0.6 shard_map.53
  48.1 0.0 collective-permute-done.8.far_ref
  48.1 0.3 collective-permute-done.10.passed_ref
  48.4 0.5 shard_map.54
  48.9 2.0 %collective-permute-start.11 = (f32[552,128]{1,0:T(8,128)S(1)}, f32[552,128]{1,0:T(8,128)S(1)}, u32[]{:S(2)}, u32[]{:S(2)}) collective-permute-start(f32[552,128]{1,0:T(8,128)S(1)} %get-tuple-element.102), channel_id=1, source_target_pairs={{0,0},{1,2},{2,1},{3,4},{4,3},{5,6},{6,5},{7,8},{8,7},{9,10},{10,9... | collective-permute-start | bytes 847880 | tf_op jit(solution)/shard_map/ppermute | solution.py:659
  50.9 1.2 %collective-permute-start.12 = (f32[552,128]{1,0:T(8,128)S(1)}, f32[552,128]{1,0:T(8,128)S(1)}, u32[]{:S(2)}, u32[]{:S(2)}) collective-permute-start(f32[552,128]{1,0:T(8,128)S(1)} %get-tuple-element.111), channel_id=1, source_target_pairs={{0,1},{1,0},{2,3},{3,2},{4,5},{5,4},{6,7},{7,6},{8,9},{9,8},{10,11... | collective-permute-start | bytes 847880 | tf_op jit(solution)/shard_map/ppermute | solution.py:659
  52.1 1.7 %shard_map.55 = (f32[6,144,256]{2,1,0:T(8,128)S(1)}, f32[144,128]{1,0:T(8,128)S(1)}) custom-call(bf16[26,144,256]{2,1,0:T(8,128)(2,1)S(1)} %get-tuple-element.88.hi_ref, bf16[26,144,256]{2,1,0:T(8,128)(2,1)S(1)} %get-tuple-element.89.lo_ref, bf16[256,512]{1,0:T(8,128)(2,1)S(1)} %get-tuple-element.64.w0_ref, ...), custom_call_target="tpu_custom_call" | custom-call | flops 1000000000 | bytes 8388608 | tf_op jit(solution)/shard_map/pallas_call | solution.py:694
  53.7 1.6 %shard_map.56.sums_ref = f32[38,144,128]{2,1,0:T(8,128)S(1)} custom-call(f32[80,128]{1,0:T(8,128)S(1)} %get-tuple-element.59.filt_ref, bf16[256,512]{1,0:T(8,128)(2,1)S(1)} %get-tuple-element.64.w0_ref, bf16[3,256,256]{2,1,0:T(8,128)(2,1)S(1)} %get-tuple-element.60.w_ref, bf16[3,256,256]{2,1,0:T(8,128)(2,1)S(1)} %get-tuple-element.61.ww_ref, ...), custom_call_target="tpu_custom_call" | custom-call | flops 1000000000 | bytes 8388608 | tf_op jit(solution)/shard_map/pallas_call | solution.py:695
  55.3 1.8 %collective-permute-done.11.side_ref = f32[552,128]{1,0:T(8,128)S(1)} collective-permute-done((f32[552,128]{1,0:T(8,128)S(1)}, f32[552,128]{1,0:T(8,128)S(1)}, u32[]{:S(2)}, u32[]{:S(2)}) %collective-permute-start.11) | collective-permute-done | bytes 282656 | tf_op jit(solution)/shard_map/ppermute | solution.py:659
  57.2 3.4 %collective-permute-start.13 = (f32[144,128]{1,0:T(8,128)S(1)}, f32[144,128]{1,0:T(8,128)S(1)}, u32[]{:S(2)}, u32[]{:S(2)}) collective-permute-start(f32[144,128]{1,0:T(8,128)S(1)} %slice.15), channel_id=1, source_target_pairs={{0,1},{1,0},{2,3},{3,2},{4,5},{5,4},{6,7},{7,6},{8,9},{9,8},{10,11... | collective-permute-start | bytes 221192 | tf_op jit(solution)/shard_map/ppermute | solution.py:659
  60.5 0.6 shard_map.57.got_ref
  61.2 0.3 collective-permute-done.13.passed_ref
  61.4 1.8 %shard_map.58 = f32[2192,128]{1,0:T(8,128)} custom-call(f32[80,128]{1,0:T(8,128)S(1)} %get-tuple-element.59.filt_ref, bf16[3,256,256]{2,1,0:T(8,128)(2,1)S(1)} %get-tuple-element.60.w_ref, bf16[3,256,256]{2,1,0:T(8,128)(2,1)S(1)} %get-tuple-element.61.ww_ref, f32[38,144,128]{2,1,0:T(8,128)S(1)} %shard_map.56.sums_ref, ...), custom_call_target="tpu_custom_call" | custom-call | flops 1000000000 | bytes 8388608 | tf_op jit(solution)/shard_map/pallas_call | solution.py:704
  (12 shorter events, 0.0 us)
Async XLA Ops:
  0.0 2.2 %copy-start = (f32[137,16,128]{2,1,0:T(8,128)S(1)}, f32[137,16,128]{2,1,0:T(8,128)}, u32[]{:S(2)}) copy-start(f32[137,16,128]{2,1,0:T(8,128)} %param.3) | copy-start | bytes 3366916
  0.0 0.8 %copy-start.2 = (s32[4,2,2,5]{3,2,1,0:T(2,128)S(1)}, s32[4,2,2,5]{3,2,1,0:T(2,128)}, u32[]{:S(2)}) copy-start(s32[4,2,2,5]{3,2,1,0:T(2,128)} %taps_ref.1) | copy-start | bytes 964
  4.4 8.2 %collective-permute-start = (f32[552,128]{1,0:T(8,128)S(1)}, f32[552,128]{1,0:T(8,128)S(1)}, u32[]{:S(2)}, u32[]{:S(2)}) collective-permute-start(f32[552,128]{1,0:T(8,128)S(1)} %get-tuple-element.65.after_ref), channel_id=1, source_target_pairs={{0,0},{1,2},{2,1},{3,4},{4,3},{5,6},{6,5},{7,8},{8,7},{9,10},{10,9... | collective-permute-start | bytes 847880 | tf_op jit(solution)/shard_map/ppermute | solution.py:659
  8.7 7.5 %collective-permute-start.2 = (f32[552,128]{1,0:T(8,128)S(1)}, f32[552,128]{1,0:T(8,128)S(1)}, u32[]{:S(2)}, u32[]{:S(2)}) collective-permute-start(f32[552,128]{1,0:T(8,128)S(1)} %shard_map.42), channel_id=1, source_target_pairs={{0,1},{1,0},{2,3},{3,2},{4,5},{5,4},{6,7},{7,6},{8,9},{9,8},{10,11... | collective-permute-start | bytes 847880 | tf_op jit(solution)/shard_map/ppermute | solution.py:659
  11.1 1.4 %copy-start.1 = (f32[5,137,137]{2,1,0:T(8,128)S(1)}, f32[5,137,137]{2,1,0:T(8,128)}, u32[]{:S(2)}) copy-start(f32[5,137,137]{2,1,0:T(8,128)} %m_ref.3) | copy-start | bytes 1126144
  11.1 5.8 %collective-permute-start.1 = (f32[40,128]{1,0:T(8,128)S(1)}, f32[40,128]{1,0:T(8,128)S(1)}, u32[]{:S(2)}, u32[]{:S(2)}) collective-permute-start(f32[40,128]{1,0:T(8,128)S(1)} %get-tuple-element.69), channel_id=1, source_target_pairs={{0,2},{2,4},{4,6},{6,8},{8,10},{10,12},{12,14},{14,16},{16,18},{18... | collective-permute-start | bytes 61448 | tf_op jit(solution)/shard_map/ppermute | solution.py:664
  12.6 4.6 %collective-permute-start.3 = (f32[144,128]{1,0:T(8,128)S(1)}, f32[144,128]{1,0:T(8,128)S(1)}, u32[]{:S(2)}, u32[]{:S(2)}) collective-permute-start(f32[144,128]{1,0:T(8,128)S(1)} %slice.12), channel_id=1, source_target_pairs={{0,1},{1,0},{2,3},{3,2},{4,5},{5,4},{6,7},{7,6},{8,9},{9,8},{10,11... | collective-permute-start | bytes 221192 | tf_op jit(solution)/shard_map/ppermute | solution.py:659
  17.7 9.2 %collective-permute-start.4 = (f32[552,128]{1,0:T(8,128)S(1)}, f32[552,128]{1,0:T(8,128)S(1)}, u32[]{:S(2)}, u32[]{:S(2)}) collective-permute-start(f32[552,128]{1,0:T(8,128)S(1)} %get-tuple-element.77), channel_id=1, source_target_pairs={{0,0},{1,2},{2,1},{3,4},{4,3},{5,6},{6,5},{7,8},{8,7},{9,10},{10,9... | collective-permute-start | bytes 847880 | tf_op jit(solution)/shard_map/ppermute | solution.py:659
  19.6 12.4 %collective-permute-start.5 = (f32[552,128]{1,0:T(8,128)S(1)}, f32[552,128]{1,0:T(8,128)S(1)}, u32[]{:S(2)}, u32[]{:S(2)}) collective-permute-start(f32[552,128]{1,0:T(8,128)S(1)} %get-tuple-element.86), channel_id=1, source_target_pairs={{0,1},{1,0},{2,3},{3,2},{4,5},{5,4},{6,7},{7,6},{8,9},{9,8},{10,11... | collective-permute-start | bytes 847880 | tf_op jit(solution)/shard_map/ppermute | solution.py:659
  26.9 6.1 %collective-permute-start.6 = (f32[144,128]{1,0:T(8,128)S(1)}, f32[144,128]{1,0:T(8,128)S(1)}, u32[]{:S(2)}, u32[]{:S(2)}) collective-permute-start(f32[144,128]{1,0:T(8,128)S(1)} %slice.13), channel_id=1, source_target_pairs={{0,1},{1,0},{2,3},{3,2},{4,5},{5,4},{6,7},{7,6},{8,9},{9,8},{10,11... | collective-permute-start | bytes 221192 | tf_op jit(solution)/shard_map/ppermute | solution.py:659
  35.9 8.2 %collective-permute-start.7 = (f32[552,128]{1,0:T(8,128)S(1)}, f32[552,128]{1,0:T(8,128)S(1)}, u32[]{:S(2)}, u32[]{:S(2)}) collective-permute-start(f32[552,128]{1,0:T(8,128)S(1)} %get-tuple-element.90.after_ref), channel_id=1, source_target_pairs={{0,0},{1,2},{2,1},{3,4},{4,3},{5,6},{6,5},{7,8},{8,7},{9,10},{10,9... | collective-permute-start | bytes 847880 | tf_op jit(solution)/shard_map/ppermute | solution.py:659
  38.4 9.1 %collective-permute-start.9 = (f32[552,128]{1,0:T(8,128)S(1)}, f32[552,128]{1,0:T(8,128)S(1)}, u32[]{:S(2)}, u32[]{:S(2)}) collective-permute-start(f32[552,128]{1,0:T(8,128)S(1)} %shard_map.52), channel_id=1, source_target_pairs={{0,1},{1,0},{2,3},{3,2},{4,5},{5,4},{6,7},{7,6},{8,9},{9,8},{10,11... | collective-permute-start | bytes 847880 | tf_op jit(solution)/shard_map/ppermute | solution.py:659
  39.5 8.5 %collective-permute-start.8 = (f32[40,128]{1,0:T(8,128)S(1)}, f32[40,128]{1,0:T(8,128)S(1)}, u32[]{:S(2)}, u32[]{:S(2)}) collective-permute-start(f32[40,128]{1,0:T(8,128)S(1)} %get-tuple-element.94), channel_id=1, source_target_pairs={{0,2},{2,4},{4,6},{6,8},{8,10},{10,12},{12,14},{14,16},{16,18},{18... | collective-permute-start | bytes 61448 | tf_op jit(solution)/shard_map/ppermute | solution.py:664
  44.1 4.3 %collective-permute-start.10 = (f32[144,128]{1,0:T(8,128)S(1)}, f32[144,128]{1,0:T(8,128)S(1)}, u32[]{:S(2)}, u32[]{:S(2)}) collective-permute-start(f32[144,128]{1,0:T(8,128)S(1)} %slice.14), channel_id=1, source_target_pairs={{0,1},{1,0},{2,3},{3,2},{4,5},{5,4},{6,7},{7,6},{8,9},{9,8},{10,11... | collective-permute-start | bytes 221192 | tf_op jit(solution)/shard_map/ppermute | solution.py:659
  48.9 8.2 %collective-permute-start.11 = (f32[552,128]{1,0:T(8,128)S(1)}, f32[552,128]{1,0:T(8,128)S(1)}, u32[]{:S(2)}, u32[]{:S(2)}) collective-permute-start(f32[552,128]{1,0:T(8,128)S(1)} %get-tuple-element.102), channel_id=1, source_target_pairs={{0,0},{1,2},{2,1},{3,4},{4,3},{5,6},{6,5},{7,8},{8,7},{9,10},{10,9... | collective-permute-start | bytes 847880 | tf_op jit(solution)/shard_map/ppermute | solution.py:659
  50.9 9.7 %collective-permute-start.12 = (f32[552,128]{1,0:T(8,128)S(1)}, f32[552,128]{1,0:T(8,128)S(1)}, u32[]{:S(2)}, u32[]{:S(2)}) collective-permute-start(f32[552,128]{1,0:T(8,128)S(1)} %get-tuple-element.111), channel_id=1, source_target_pairs={{0,1},{1,0},{2,3},{3,2},{4,5},{5,4},{6,7},{7,6},{8,9},{9,8},{10,11... | collective-permute-start | bytes 847880 | tf_op jit(solution)/shard_map/ppermute | solution.py:659
  57.2 4.3 %collective-permute-start.13 = (f32[144,128]{1,0:T(8,128)S(1)}, f32[144,128]{1,0:T(8,128)S(1)}, u32[]{:S(2)}, u32[]{:S(2)}) collective-permute-start(f32[144,128]{1,0:T(8,128)S(1)} %slice.15), channel_id=1, source_target_pairs={{0,1},{1,0},{2,3},{3,2},{4,5},{5,4},{6,7},{7,6},{8,9},{9,8},{10,11... | collective-permute-start | bytes 221192 | tf_op jit(solution)/shard_map/ppermute | solution.py:659
